TPU v7x, 8 devices: a whole 2x2x1 slice. The times are simulated.
8 devices in a mesh: pairs: 2 (over z, y), rows: 4 (over x, core).
Axes of the slice: x: 2, y: 2, z: 1, core: 2. Of those that a mesh axis runs over, the one named last changes fastest.
Arguments:
- cost_src: float32 [8192, 4096], P(('pairs', 'rows')), parts along dimension 0
- cost_tgt: float32 [8192, 4096], P(('pairs', 'rows')), parts along dimension 0
- plan_init: float32 [8192, 4096], P(('pairs', 'rows')), parts along dimension 0
- mass_src: float32 [8192], P(('pairs', 'rows')), parts along dimension 0
- mass_tgt: float32 [8192], P('pairs'), parts along dimension 0
- feat_src: float32 [8192, 256], P(('pairs', 'rows')), parts along dimension 0
- feat_tgt: float32 [8192, 256], P(('pairs', 'rows')), parts along dimension 0
- epsilon: float32 [], replicated
Outputs:
- output: float32 [8192, 4096], P(('pairs', 'rows')), parts along dimension 0
There are 2 independent parts. A program takes and returns all parts, laid end to end along the dimension named above; an argument that names none is the same for every part.
All inputs are finite; a program needn't handle non-finite values.
Results may differ from a plain program's by a relative error of at most 0.001.
Values are sent between devices in bfloat16 or wider.
A program may use at most 1 GiB of HBM per device.

v0:
```python
import jax
import jax.numpy as jnp
from jax import lax
from jax.sharding import PartitionSpec as P

ALPHA = 0.5
OUTER_STEPS = 2
SWEEPS = 10


def gibbs_kernel(cost_rows, epsilon):
    return jnp.exp(-(cost_rows - jnp.min(cost_rows, axis=1, keepdims=True)) / epsilon)


def scaled_plan(kernel, mass_rows, mass_tgt):
    def value_a14(sweep_index, scales):
        row_scale = mass_rows / jnp.sum(kernel * scales[1][None, :], axis=1)
        col_sum = lax.psum(jnp.sum(kernel * row_scale[:, None], axis=0), 'rows')
        return row_scale, mass_tgt / col_sum
    start_scales = (jnp.ones_like(mass_rows), jnp.ones_like(mass_tgt))
    row_scale, col_scale = lax.fori_loop(0, SWEEPS, value_a14, start_scales)
    return row_scale[:, None] * kernel * col_scale[None, :]


def solution(mesh):
    def local_fgw(cost_src, cost_tgt, plan_init, mass_src, mass_tgt, feat_src, feat_tgt, epsilon):
        src_half = cost_src.astype(jnp.bfloat16)
        tgt_half = cost_tgt.astype(jnp.bfloat16)
        feat_all = lax.all_gather(feat_tgt.astype(jnp.bfloat16), 'rows', tiled=True)
        cross_term = jnp.einsum('id,jd->ij', feat_src.astype(jnp.bfloat16), feat_all, preferred_element_type=jnp.float32)
        feat_cost = (-2.0 * ALPHA) * cross_term
        transport = plan_init
        for step_index in range(OUTER_STEPS):
            transport_all = lax.all_gather(transport.astype(jnp.bfloat16), 'rows', tiled=True)
            tgt_all = lax.all_gather(tgt_half, 'rows', tiled=True)
            prod_a = jnp.dot(src_half, transport_all, preferred_element_type=jnp.float32)
            prod_b = jnp.dot(prod_a.astype(jnp.bfloat16), tgt_all, preferred_element_type=jnp.float32)
            step_cost = feat_cost - (2.0 * (1.0 - ALPHA)) * prod_b
            transport = scaled_plan(gibbs_kernel(step_cost, epsilon), mass_src, mass_tgt)
        return transport

    row_spec = P(('pairs', 'rows'), None)
    vec_spec = P(('pairs', 'rows'))
    in_specs = (row_spec, row_spec, row_spec, vec_spec, P('pairs'), row_spec, row_spec, P())
    return jax.shard_map(local_fgw, mesh=mesh, in_specs=in_specs, out_specs=row_spec, check_vma=False)
```

profile of v0, /device:TPU:0, one launch (start us, length us, event | category | flops | bytes accessed | tf_op | source)
XLA Modules:
  0.0 1304.5 jit_solution(3059750444784048319)
XLA Ops:
  8.7 9.0 convert_element_type.28
  17.7 9.0 convert_element_type.30
  31.3 10.1 fusion.12
  41.4 190.8 %all-gather.7.cloned.1.call-done = bf16[4096,4096]{1,0:T(8,128)(2,1)} async-done(((bf16[1024,4096]{1,0:T(8,128)(2,1)}), bf16[4096,4096]{1,0:T(8,128)(2,1)}) %all-gather.7.cloned.1.call-update) | async-done | bytes 33554448 | tf_op jit(solution)/shard_map/all_gather | solution.py:34
  232.2 44.8 %fusion.10 = bf16[1024,4096]{1,0:T(8,128)(2,1)} fusion(bf16[4096,4096]{1,0:T(8,128)(2,1)} %all-gather.7.cloned.1.call-done, f32[1024,4096]{1,0:T(8,128)} %param.12), kind=kOutput, calls=%fused_computation.18 | convolution fusion | flops 34363932672 | bytes 58720256 | tf_op jit(solution)/shard_map/dot_general | solution.py:36
  277.0 156.1 %all-gather.9.cloned.1.call-done = bf16[4096,4096]{1,0:T(8,128)(2,1)} async-done(((bf16[1024,4096]{1,0:T(8,128)(2,1)}), bf16[4096,4096]{1,0:T(8,128)(2,1)}) %all-gather.9.cloned.1.call-update) | async-done | bytes 33554448 | tf_op jit(solution)/shard_map/all_gather | solution.py:35
  433.1 41.9 %fusion.14 = (f32[1024]{0:T(1024)S(1)}, f32[1024,4096]{1,0:T(8,128)S(1)}) fusion(bf16[1024,4096]{1,0:T(8,128)(2,1)} %fusion.10, bf16[4096,4096]{1,0:T(8,128)(2,1)} %all-gather.9.cloned.1.call-done, f32[1024,4096]{1,0:T(8,128)} %fusion.12), kind=kOutput, calls=%fused_computation.22 | convolution fusion | flops 34372321280 | bytes 75501568 | tf_op jit(solution)/shard_map/dot_general | solution.py:37
  475.0 8.1 divide_exponential_fusion.1
  486.3 244.3 %while.26 = (s32[]{:T(128)}, f32[1024]{0:T(1024)}, f32[4096]{0:T(1024)S(1)}, f32[1024,4096]{1,0:T(8,128)}, f32[1024]{0:T(1024)S(1)}, /*index=5*/f32[4096]{0:T(1024)S(1)}, s32[]{:T(128)}, s32[]{:T(128)}) while((s32[]{:T(128)}, f32[1024]{0:T(1024)}, f32[4096]{0:T(1024)S(1)}, f32[1024,4096]{1,0:T(8,128)}, f32[1024]{0:T(1024)S(1)}, ...), condition=%wide.region_5.0_spmd.clone, body=%wide.region_1.0_spmd.clone.sunk | while | flops 16785412 | bytes 33738872 | solution.py:21
  493.6 7.2 multiply_reduce_fusion.9
  500.7 10.2 psum.18
  525.3 10.1 psum.18
  542.5 7.2 multiply_reduce_fusion.9
  549.7 10.1 psum.18
  566.9 7.2 multiply_reduce_fusion.9
  574.1 10.1 psum.18
  591.3 7.2 multiply_reduce_fusion.9
  598.5 10.1 psum.18
  615.7 7.2 multiply_reduce_fusion.9
  622.9 10.1 psum.18
  640.1 7.2 multiply_reduce_fusion.9
  647.3 10.1 psum.18
  664.5 7.2 multiply_reduce_fusion.9
  671.7 10.1 psum.18
  688.9 7.2 multiply_reduce_fusion.9
  696.1 10.1 psum.18
  713.3 7.2 multiply_reduce_fusion.9
  720.5 10.1 psum.18
  730.6 11.0 multiply_convert_fusion
  741.7 200.7 %all-gather.11.cloned.1.call-done = bf16[4096,4096]{1,0:T(8,128)(2,1)} async-done(((bf16[1024,4096]{1,0:T(8,128)(2,1)}), bf16[4096,4096]{1,0:T(8,128)(2,1)}) %all-gather.11.cloned.1.call-update) | async-done | bytes 33554448 | tf_op jit(solution)/shard_map/all_gather | solution.py:34
  942.4 44.9 %fusion.8 = bf16[4096,1024]{1,0:T(8,128)(2,1)} fusion(bf16[4096,4096]{1,0:T(8,128)(2,1)} %all-gather.11.cloned.1.call-done, f32[1024,4096]{1,0:T(8,128)} %param.12), kind=kOutput, calls=%fused_computation.16 | convolution fusion | flops 34363932672 | bytes 58720256 | tf_op jit(solution)/shard_map/dot_general | solution.py:36
  987.3 42.3 %fusion.15 = (f32[1024]{0:T(1024)S(1)}, f32[1024,4096]{1,0:T(8,128)S(1)}) fusion(bf16[4096,1024]{1,0:T(8,128)(2,1)} %fusion.8, bf16[4096,4096]{1,0:T(8,128)(2,1)} %all-gather.9.cloned.1.call-done, f32[1024,4096]{1,0:T(8,128)} %fusion.12), kind=kOutput, calls=%fused_computation.23 | convolution fusion | flops 34372321280 | bytes 75501568 | tf_op jit(solution)/shard_map/dot_general | solution.py:37
  1029.6 8.0 divide_exponential_fusion
  1040.9 244.1 %while.27 = (s32[]{:T(128)}, f32[1024]{0:T(1024)}, f32[4096]{0:T(1024)S(1)}, f32[1024,4096]{1,0:T(8,128)}, f32[1024]{0:T(1024)S(1)}, /*index=5*/f32[4096]{0:T(1024)S(1)}, s32[]{:T(128)}, s32[]{:T(128)}) while((s32[]{:T(128)}, f32[1024]{0:T(1024)}, f32[4096]{0:T(1024)S(1)}, f32[1024,4096]{1,0:T(8,128)}, f32[1024]{0:T(1024)S(1)}, ...), condition=%wide.region_11.0_spmd.clone, body=%wide.region_7.0_spmd.clone.sunk | while | flops 16785412 | bytes 33738872 | solution.py:21
  1048.0 7.2 multiply_reduce_fusion.11
  1055.1 10.2 psum.19
  1072.5 7.2 multiply_reduce_fusion.11
  1079.6 10.1 psum.19
  1096.9 7.2 multiply_reduce_fusion.11
  1104.0 10.1 psum.19
  1128.4 10.1 psum.19
  1152.8 10.1 psum.19
  1177.2 10.1 psum.19
  1201.6 10.1 psum.19
  1226.0 10.1 psum.19
  1250.4 10.1 psum.19
  1274.8 10.1 psum.19
  1285.0 13.0 multiply_multiply_fusion
  (154 shorter events, 211.4 us)
Async XLA Ops:
  6.5 24.7 %all-gather.5.cloned.1.call-start = ((), (), s32[]{:S(2)}) async-start(), calls=%async_computation | async-start | bytes 2621440 | tf_op jit(solution)/shard_map/all_gather | solution.py:29
  8.6 223.5 %all-gather.7.cloned.1.call-start = ((), (), s32[]{:S(2)}) async-start(), calls=%async_computation.1 | async-start | bytes 41943040 | tf_op jit(solution)/shard_map/all_gather | solution.py:34
  17.7 13.6 %copy-start.3 = (f32[1024,256]{1,0:T(8,128)S(1)}, f32[1024,256]{1,0:T(8,128)}, u32[]{:S(2)}) copy-start(f32[1024,256]{1,0:T(8,128)} %param.17) | copy-start | bytes 3145732
  17.7 415.4 %all-gather.9.cloned.1.call-start = ((), (), s32[]{:S(2)}) async-start(), calls=%async_computation.2 | async-start | bytes 41943040 | tf_op jit(solution)/shard_map/all_gather | solution.py:35
  26.8 915.6 %all-gather.11.cloned.1.call-start = ((), (), s32[]{:S(2)}) async-start(), calls=%async_computation.3 | async-start | bytes 41943040 | tf_op jit(solution)/shard_map/all_gather | solution.py:34
  475.0 10.7 copy-start.1
  475.0 11.3 copy-start.2
  475.0 11.3 copy-start.4
  475.0 11.3 copy-start.5
  493.6 17.4 %copy-start.7 = (f32[1024]{0:T(1024)}, f32[1024]{0:T(1024)S(1)}, u32[]{:S(2)}) copy-start(f32[1024]{0:T(1024)S(1)} %div.53) | copy-start | bytes 12292 | tf_op jit(solution)/shard_map/while
  518.1 17.3 %copy-start.7 = (f32[1024]{0:T(1024)}, f32[1024]{0:T(1024)S(1)}, u32[]{:S(2)}) copy-start(f32[1024]{0:T(1024)S(1)} %div.53) | copy-start | bytes 12292 | tf_op jit(solution)/shard_map/while
  542.5 17.3 %copy-start.7 = (f32[1024]{0:T(1024)}, f32[1024]{0:T(1024)S(1)}, u32[]{:S(2)}) copy-start(f32[1024]{0:T(1024)S(1)} %div.53) | copy-start | bytes 12292 | tf_op jit(solution)/shard_map/while
  566.9 17.3 %copy-start.7 = (f32[1024]{0:T(1024)}, f32[1024]{0:T(1024)S(1)}, u32[]{:S(2)}) copy-start(f32[1024]{0:T(1024)S(1)} %div.53) | copy-start | bytes 12292 | tf_op jit(solution)/shard_map/while
  591.3 17.3 %copy-start.7 = (f32[1024]{0:T(1024)}, f32[1024]{0:T(1024)S(1)}, u32[]{:S(2)}) copy-start(f32[1024]{0:T(1024)S(1)} %div.53) | copy-start | bytes 12292 | tf_op jit(solution)/shard_map/while
  615.7 17.3 %copy-start.7 = (f32[1024]{0:T(1024)}, f32[1024]{0:T(1024)S(1)}, u32[]{:S(2)}) copy-start(f32[1024]{0:T(1024)S(1)} %div.53) | copy-start | bytes 12292 | tf_op jit(solution)/shard_map/while
  640.1 17.3 %copy-start.7 = (f32[1024]{0:T(1024)}, f32[1024]{0:T(1024)S(1)}, u32[]{:S(2)}) copy-start(f32[1024]{0:T(1024)S(1)} %div.53) | copy-start | bytes 12292 | tf_op jit(solution)/shard_map/while
  664.5 17.3 %copy-start.7 = (f32[1024]{0:T(1024)}, f32[1024]{0:T(1024)S(1)}, u32[]{:S(2)}) copy-start(f32[1024]{0:T(1024)S(1)} %div.53) | copy-start | bytes 12292 | tf_op jit(solution)/shard_map/while
  688.9 17.3 %copy-start.7 = (f32[1024]{0:T(1024)}, f32[1024]{0:T(1024)S(1)}, u32[]{:S(2)}) copy-start(f32[1024]{0:T(1024)S(1)} %div.53) | copy-start | bytes 12292 | tf_op jit(solution)/shard_map/while
  713.3 17.3 %copy-start.7 = (f32[1024]{0:T(1024)}, f32[1024]{0:T(1024)S(1)}, u32[]{:S(2)}) copy-start(f32[1024]{0:T(1024)S(1)} %div.53) | copy-start | bytes 12292 | tf_op jit(solution)/shard_map/while
  1029.6 10.7 copy-start
  1048.0 17.4 %copy-start.6 = (f32[1024]{0:T(1024)}, f32[1024]{0:T(1024)S(1)}, u32[]{:S(2)}) copy-start(f32[1024]{0:T(1024)S(1)} %div.55) | copy-start | bytes 12292 | tf_op jit(solution)/shard_map/while
  1072.5 17.3 %copy-start.6 = (f32[1024]{0:T(1024)}, f32[1024]{0:T(1024)S(1)}, u32[]{:S(2)}) copy-start(f32[1024]{0:T(1024)S(1)} %div.55) | copy-start | bytes 12292 | tf_op jit(solution)/shard_map/while
  1096.9 17.3 %copy-start.6 = (f32[1024]{0:T(1024)}, f32[1024]{0:T(1024)S(1)}, u32[]{:S(2)}) copy-start(f32[1024]{0:T(1024)S(1)} %div.55) | copy-start | bytes 12292 | tf_op jit(solution)/shard_map/while
  1121.3 17.3 %copy-start.6 = (f32[1024]{0:T(1024)}, f32[1024]{0:T(1024)S(1)}, u32[]{:S(2)}) copy-start(f32[1024]{0:T(1024)S(1)} %div.55) | copy-start | bytes 12292 | tf_op jit(solution)/shard_map/while
  1145.7 17.3 %copy-start.6 = (f32[1024]{0:T(1024)}, f32[1024]{0:T(1024)S(1)}, u32[]{:S(2)}) copy-start(f32[1024]{0:T(1024)S(1)} %div.55) | copy-start | bytes 12292 | tf_op jit(solution)/shard_map/while
  1170.1 17.3 %copy-start.6 = (f32[1024]{0:T(1024)}, f32[1024]{0:T(1024)S(1)}, u32[]{:S(2)}) copy-start(f32[1024]{0:T(1024)S(1)} %div.55) | copy-start | bytes 12292 | tf_op jit(solution)/shard_map/while
  1194.5 17.3 %copy-start.6 = (f32[1024]{0:T(1024)}, f32[1024]{0:T(1024)S(1)}, u32[]{:S(2)}) copy-start(f32[1024]{0:T(1024)S(1)} %div.55) | copy-start | bytes 12292 | tf_op jit(solution)/shard_map/while
  1218.9 17.3 %copy-start.6 = (f32[1024]{0:T(1024)}, f32[1024]{0:T(1024)S(1)}, u32[]{:S(2)}) copy-start(f32[1024]{0:T(1024)S(1)} %div.55) | copy-start | bytes 12292 | tf_op jit(solution)/shard_map/while
  1243.3 17.3 %copy-start.6 = (f32[1024]{0:T(1024)}, f32[1024]{0:T(1024)S(1)}, u32[]{:S(2)}) copy-start(f32[1024]{0:T(1024)S(1)} %div.55) | copy-start | bytes 12292 | tf_op jit(solution)/shard_map/while
  1267.7 17.3 %copy-start.6 = (f32[1024]{0:T(1024)}, f32[1024]{0:T(1024)S(1)}, u32[]{:S(2)}) copy-start(f32[1024]{0:T(1024)S(1)} %div.55) | copy-start | bytes 12292 | tf_op jit(solution)/shard_map/while
Sparse Core Ops, SparseCore 0:
  8.9 22.3 all-gather.4
  32.8 199.3 all-gather.6
  233.7 199.3 all-gather.8
  741.8 200.5 all-gather.10
where the time goes:
time: 1310 us; the launch traced here: 1300 us
  waiting for transfers between devices  551 us (42%)
  other arithmetic  345 us (26%)
  blocking collectives  203 us (15%)
  matrix products  184 us (14%)
  between operations  13.9 us (1%)
    all_gather x2, waiting for transfers between devices, local_fgw(): lax.all_gather(transport.astype(jnp.bfloat16), 'rows', tiled=True)  391 us
    psum x20, blocking collectives, value_a14(): col_sum = lax.psum(jnp.sum(kernel * row_scale[:, None], axis=0), 'rows')  203 us
    all_gather x1, waiting for transfers between devices, local_fgw(): tgt_all = lax.all_gather(tgt_half, 'rows', tiled=True)  156 us
    reduce_sum x20, other arithmetic, value_a14(): col_sum = lax.psum(jnp.sum(kernel * row_scale[:, None], axis=0), 'rows')  143 us
    reduce_sum x20, other arithmetic, value_a14(): row_scale = mass_rows / jnp.sum(kernel * scales[1][None, :], axis=1)  141 us
    dot_general x2, matrix products, local_fgw(): jnp.dot(src_half, transport_all, preferred_element_type=jnp.float32)  89.8 us
    dot_general x2, matrix products, local_fgw(): jnp.dot(prod_a.astype(jnp.bfloat16), tgt_all, preferred_element_type=jnp....  84.1 us
  transfers between devices with their start and end apart: 4, of which 4 were waited for; matrix products, arithmetic and copies ran while one was open for 6% of the time, Pallas kernels for 0%

commit v1 on v0

v1 whole, which is shorter than its diff:
```python
import functools

import jax
import jax.numpy as jnp
from jax import lax
from jax.experimental import pallas as pl
from jax.experimental.pallas import tpu as pltpu
from jax.sharding import PartitionSpec as P

ALPHA = 0.5
OUTER_STEPS = 2
SWEEPS = 10
LANES = 128
CHUNKS = 4
BLOCK = 64
LOAD_ROWS = 128
MESH = pl.DeviceIdType.MESH


def sinkhorn_kernel(group, gain_hbm, mass_row, mass_col, epsilon, plan_hbm, kern, plan, row_scale, acc, col_scale,
                    part_sum, peer_sum, load_sem, store_sem, send_sem, recv_sem):
    rows, cols = kern.shape
    tiles = cols // LANES // CHUNKS
    width = cols // CHUNKS
    me = lax.axis_index('rows')
    peers = [lax.rem(me + k, group) for k in range(1, group)]

    loads = [pltpu.make_async_copy(gain_hbm.at[pl.ds(b * LOAD_ROWS, LOAD_ROWS)], kern.at[pl.ds(b * LOAD_ROWS, LOAD_ROWS)],
                                   load_sem.at[b]) for b in range(rows // LOAD_ROWS)]
    for load in loads:
        load.start()

    barrier = pltpu.get_barrier_semaphore()
    for peer in peers:
        pl.semaphore_signal(barrier, inc=1, device_id={'rows': peer}, device_id_type=MESH)
    pl.semaphore_wait(barrier, group - 1)

    def tile(j, t):
        start = j * width + t * LANES
        return slice(start, start + LANES)

    def sends(slot, j):
        return [pltpu.make_async_remote_copy(
            src_ref=part_sum.at[slot, j], dst_ref=peer_sum.at[slot, k, j], send_sem=send_sem.at[slot, k, j],
            recv_sem=recv_sem.at[slot, k, j], device_id={'rows': peers[k]}, device_id_type=MESH) for k in range(group - 1)]

    inv_eps = 1.0 / epsilon[0]
    for b, load in enumerate(loads):
        load.wait()

        def exp_block(i, carry, b=b):
            span = pl.ds(b * LOAD_ROWS + i * BLOCK, BLOCK)
            top = kern[span, 0:LANES]
            for t in range(1, cols // LANES):
                top = jnp.maximum(top, kern[span, t * LANES:(t + 1) * LANES])
            top = jnp.max(top, axis=1, keepdims=True)
            total = jnp.zeros((BLOCK, LANES), jnp.float32)
            for t in range(cols // LANES):
                val = jnp.exp((kern[span, t * LANES:(t + 1) * LANES] - top) * inv_eps)
                kern[span, t * LANES:(t + 1) * LANES] = val
                total = total + val
            acc[span, :] = total
            return carry
        lax.fori_loop(0, LOAD_ROWS // BLOCK, exp_block, 0)

    def row_update():
        for h in range(0, rows, 256):
            span = slice(h, h + 256)
            row_scale[span, :] = mass_row[span, :] / jnp.sum(acc[span, :], axis=1, keepdims=True)

    def col_pass(slot, j):
        def body(i, sums):
            span = pl.ds(i * BLOCK, BLOCK)
            scale = row_scale[span, :].reshape(BLOCK // 8, 8, LANES)
            return tuple(sums[t] + jnp.sum(kern[span, tile(j, t)].reshape(BLOCK // 8, 8, LANES) * scale, axis=0)
                         for t in range(tiles))
        sums = lax.fori_loop(0, rows // BLOCK, body, tuple(jnp.zeros((8, LANES), jnp.float32) for _ in range(tiles)))
        part_sum[slot, j] = jnp.concatenate([jnp.sum(s, axis=0, keepdims=True) for s in sums], axis=0)
        for send in sends(slot, j):
            send.start()

    def col_update(slot, j):
        for send in sends(slot, j):
            send.wait()
        total = part_sum[slot, j]
        for k in range(group - 1):
            total = total + peer_sum[slot, k, j]
        col_scale[j] = mass_col[j] / total

    def scale_rows(j):
        return [jnp.broadcast_to(col_scale[j, t:t + 1, :], (8, LANES)) for t in range(tiles)]

    def row_pass(j):
        scale = scale_rows(j)

        def body(i, carry):
            span = pl.ds(i * BLOCK, BLOCK)
            total = None if j == 0 else acc[span, :].reshape(BLOCK // 8, 8, LANES)
            for t in range(tiles):
                term = kern[span, tile(j, t)].reshape(BLOCK // 8, 8, LANES) * scale[t][None]
                total = term if total is None else total + term
            acc[span, :] = total.reshape(BLOCK, LANES)
            return carry
        lax.fori_loop(0, rows // BLOCK, body, 0)

    row_update()

    def sweep(n, carry):
        slot = lax.rem(n, 2)
        for j in range(CHUNKS):
            col_pass(slot, j)
        for j in range(CHUNKS):
            col_update(slot, j)
            row_pass(j)
        row_update()
        return carry
    lax.fori_loop(0, SWEEPS - 1, sweep, 0)

    last = (SWEEPS - 1) % 2
    for j in range(CHUNKS):
        col_pass(last, j)
    stores = []
    for j in range(CHUNKS):
        col_update(last, j)
        scale = scale_rows(j)

        def plan_block(i, carry, j=j, scale=scale):
            span = pl.ds(i * BLOCK, BLOCK)
            left = row_scale[span, :].reshape(BLOCK // 8, 8, LANES)
            for t in range(tiles):
                val = left * kern[span, tile(j, t)].reshape(BLOCK // 8, 8, LANES) * scale[t][None]
                plan[span, tile(j, t)] = val.reshape(BLOCK, LANES).astype(plan.dtype)
            return carry
        lax.fori_loop(0, rows // BLOCK, plan_block, 0)
        span = pl.ds(j * width, width)
        stores.append(pltpu.make_async_copy(plan.at[:, span], plan_hbm.at[:, span], store_sem.at[j]))
        stores[-1].start()
    for store in stores:
        store.wait()


def sinkhorn(group, gain, mass_rows, mass_tgt, epsilon, dtype, collective_id):
    rows, cols = gain.shape
    tiles = cols // LANES // CHUNKS
    row_rep = jnp.broadcast_to(mass_rows[:, None], (rows, LANES))
    col_tiles = mass_tgt.reshape(CHUNKS, tiles, LANES)
    n_load = rows // LOAD_ROWS
    return pl.pallas_call(
        functools.partial(sinkhorn_kernel, group),
        out_shape=jax.ShapeDtypeStruct((rows, cols), dtype),
        in_specs=[pl.BlockSpec(memory_space=pl.ANY), pl.BlockSpec(memory_space=pltpu.VMEM),
                  pl.BlockSpec(memory_space=pltpu.VMEM), pl.BlockSpec(memory_space=pltpu.SMEM)],
        out_specs=pl.BlockSpec(memory_space=pl.ANY),
        scratch_shapes=[
            pltpu.VMEM((rows, cols), jnp.float32),
            pltpu.VMEM((rows, cols), dtype),
            pltpu.VMEM((rows, LANES), jnp.float32),
            pltpu.VMEM((rows, LANES), jnp.float32),
            pltpu.VMEM((CHUNKS, tiles, LANES), jnp.float32),
            pltpu.VMEM((2, CHUNKS, tiles, LANES), jnp.float32),
            pltpu.VMEM((2, group - 1, CHUNKS, tiles, LANES), jnp.float32),
            pltpu.SemaphoreType.DMA((n_load,)),
            pltpu.SemaphoreType.DMA((CHUNKS,)),
            pltpu.SemaphoreType.DMA((2, group - 1, CHUNKS)),
            pltpu.SemaphoreType.DMA((2, group - 1, CHUNKS)),
        ],
        compiler_params=pltpu.CompilerParams(collective_id=collective_id, has_side_effects=True,
                                             vmem_limit_bytes=48 * 1024 * 1024),
        cost_estimate=pl.CostEstimate(flops=4 * SWEEPS * rows * cols, bytes_accessed=8 * rows * cols,
                                      transcendentals=rows * cols),
        name='sinkhorn',
    )(gain, row_rep, col_tiles, epsilon.reshape(1))


def solution(mesh):
    group = mesh.shape['rows']

    def local_fgw(cost_src, cost_tgt, plan_init, mass_src, mass_tgt, feat_src, feat_tgt, epsilon):
        src_half = cost_src.astype(jnp.bfloat16)
        tgt_half = cost_tgt.astype(jnp.bfloat16)
        feat_all = lax.all_gather(feat_tgt.astype(jnp.bfloat16), 'rows', tiled=True)
        cross_term = jnp.einsum('id,jd->ij', feat_src.astype(jnp.bfloat16), feat_all, preferred_element_type=jnp.float32)
        tgt_all = lax.all_gather(tgt_half, 'rows', tiled=True)
        transport = plan_init.astype(jnp.bfloat16)
        for step_index in range(OUTER_STEPS):
            transport_all = lax.all_gather(transport, 'rows', tiled=True)
            prod_a = jnp.dot(src_half, transport_all, preferred_element_type=jnp.float32)
            prod_b = jnp.dot(prod_a.astype(jnp.bfloat16), tgt_all, preferred_element_type=jnp.float32)
            gain = (2.0 * ALPHA) * cross_term + (2.0 * (1.0 - ALPHA)) * prod_b
            last = step_index == OUTER_STEPS - 1
            transport = sinkhorn(group, gain, mass_src, mass_tgt, epsilon,
                                 jnp.float32 if last else jnp.bfloat16, step_index)
        return transport

    row_spec = P(('pairs', 'rows'), None)
    vec_spec = P(('pairs', 'rows'))
    in_specs = (row_spec, row_spec, row_spec, vec_spec, P('pairs'), row_spec, row_spec, P())
    return jax.shard_map(local_fgw, mesh=mesh, in_specs=in_specs, out_specs=row_spec, check_vma=False)
```

time: 1310 us -> 902 us (0.69)
  other arithmetic: 345 us -> 20.1 us
  blocking collectives: 203 us -> 0 us
  Pallas kernels: 0 us -> 120 us
    reduce_sum x40 -> x0, other arithmetic: 284 us -> none  [the longest x20 143 us: value_a14(): col_sum = lax.psum(jnp.sum(kernel * row_scale[:, None], axis=0), 'rows')]
    psum x20 -> x0, blocking collectives: 203 us -> none  [value_a14(): col_sum = lax.psum(jnp.sum(kernel * row_scale[:, None], axis=0), 'rows')]
    pallas_call x0 -> x2, Pallas kernels: none -> 120 us  [sinkhorn(): pl.pallas_call(functools.partial(sinkhorn_kernel, group), out_shape=jax.S...]
    exp x2 -> x0, other arithmetic: 16.1 us -> none  [gibbs_kernel(): jnp.exp(-(cost_rows - jnp.min(cost_rows, axis=1, keepdims=True)) / epsilon)]
  transfers between devices with their start and end apart: 4 -> 4, of which waited for: 4 -> 4; matrix products, arithmetic and copies ran while one was open for 6% -> 8% of each run, Pallas kernels for 0% -> 0%
where the time goes in v1:
time: 902 us
  waiting for transfers between devices  550 us (61%)
  matrix products  186 us (21%)
  Pallas kernels  120 us (13%)
  other arithmetic  20.1 us (2%)
  between operations  13.8 us (2%)
  local copies, waits for them, and re-layouts  11.9 us (1%)
    all_gather x2, waiting for transfers between devices, local_fgw(): transport_all = lax.all_gather(transport, 'rows', tiled=True)  390 us
    all_gather x1, waiting for transfers between devices, local_fgw(): tgt_all = lax.all_gather(tgt_half, 'rows', tiled=True)  156 us
    pallas_call x2, Pallas kernels, sinkhorn(): pl.pallas_call(functools.partial(sinkhorn_kernel, group), out_shape=jax.S...  120 us
    dot_general x2, matrix products, local_fgw(): jnp.dot(src_half, transport_all, preferred_element_type=jnp.float32)  89.8 us
    dot_general x2, matrix products, local_fgw(): jnp.dot(prod_a.astype(jnp.bfloat16), tgt_all, preferred_element_type=jnp....  85.6 us
  transfers between devices with their start and end apart: 4, of which 4 were waited for; matrix products, arithmetic and copies ran while one was open for 8% of the time, Pallas kernels for 0%

profile of v1, /device:TPU:0, one launch (start us, length us, event | category | flops | bytes accessed | tf_op | source)
XLA Modules:
  0.0 901.6 jit_solution(1616755100086013939)
XLA Ops:
  6.5 0.0 all-gather.5.cloned.1.call-start
  6.5 2.1 convert_element_type.23
  8.6 0.0 all-gather.5.cloned.1.call-update
  8.6 0.0 all-gather.7.cloned.1.call-start
  8.7 9.0 convert_element_type.25
  17.6 0.0 all-gather.7.cloned.1.call-update
  17.7 0.0 copy-start.1
  17.7 0.0 all-gather.9.cloned.1.call-start
  17.7 9.1 %convert_element_type.27 = bf16[1024,4096]{1,0:T(8,128)(2,1)} convert(f32[1024,4096]{1,0:T(8,128)} %param.9) | non-fusion elementwise | flops 4194304 | bytes 25165824 | tf_op jit(solution)/shard_map/convert_element_type | solution.py:180
  26.8 0.0 all-gather.9.cloned.1.call-update
  26.8 0.0 all-gather.11.cloned.1.call-start
  27.5 3.7 all-gather.5.cloned.1.call-done
  31.3 0.0 copy-done.1
  31.3 10.1 %fusion.14 = f32[1024,4096]{1,0:T(8,128)} fusion(bf16[4096,256]{1,0:T(8,128)(2,1)} %all-gather.5.cloned.1.call-done, f32[1024,256]{1,0:T(8,128)S(1)} %copy-done.1), kind=kOutput, calls=%fused_computation.10 | convolution fusion | flops 2147745792 | bytes 19922944 | tf_op jit(solution)/shard_map/id,jd->ij/dot_general | solution.py:182
  41.4 190.8 %all-gather.7.cloned.1.call-done = bf16[4096,4096]{1,0:T(8,128)(2,1)} async-done(((bf16[1024,4096]{1,0:T(8,128)(2,1)}), bf16[4096,4096]{1,0:T(8,128)(2,1)}) %all-gather.7.cloned.1.call-update) | async-done | bytes 33554448 | tf_op jit(solution)/shard_map/all_gather | solution.py:186
  232.2 44.8 %fusion.12 = bf16[1024,4096]{1,0:T(8,128)(2,1)} fusion(bf16[4096,4096]{1,0:T(8,128)(2,1)} %all-gather.7.cloned.1.call-done, f32[1024,4096]{1,0:T(8,128)} %param.8), kind=kOutput, calls=%fused_computation.8 | convolution fusion | flops 34363932672 | bytes 58720256 | tf_op jit(solution)/shard_map/dot_general | solution.py:187
  277.0 0.0 copy-start.2
  277.0 0.0 copy-start
  277.0 156.1 %all-gather.9.cloned.1.call-done = bf16[4096,4096]{1,0:T(8,128)(2,1)} async-done(((bf16[1024,4096]{1,0:T(8,128)(2,1)}), bf16[4096,4096]{1,0:T(8,128)(2,1)}) %all-gather.9.cloned.1.call-update) | async-done | bytes 33554448 | tf_op jit(solution)/shard_map/all_gather | solution.py:183
  433.1 42.6 %fusion.4.gain_hbm = f32[1024,4096]{1,0:T(8,128)} fusion(f32[1024,4096]{1,0:T(8,128)} %fusion.14, bf16[4096,4096]{1,0:T(8,128)(2,1)} %all-gather.9.cloned.1.call-done, bf16[1024,4096]{1,0:T(8,128)(2,1)} %fusion.12), kind=kOutput, calls=%fused_computation.4 | convolution fusion | flops 34363932672 | bytes 75497472 | tf_op jit(solution)/shard_map/dot_general | solution.py:188
  475.7 0.0 copy-done.2
  475.7 0.2 broadcast_in_dim.2.mass_row
  475.9 0.0 copy-done
  475.9 58.7 %sinkhorn.2 = bf16[1024,4096]{1,0:T(8,128)(2,1)} custom-call(f32[1024,4096]{1,0:T(8,128)} %fusion.4.gain_hbm, f32[1024,128]{1,0:T(8,128)S(1)} %broadcast_in_dim.2.mass_row, f32[4,8,128]{2,1,0:T(8,128)S(1)} %bitcast.11, f32[1]{0:T(128)} %bitcast.9.epsilon), custom_call_target="tpu_custom_call" | custom-call | flops 167772160 | bytes 33554432 | tf_op jit(solution)/shard_map/sinkhorn/pallas_call | solution.py:148
  534.6 0.0 all-gather.11.cloned.1.call-update
  534.7 199.6 %all-gather.11.cloned.1.call-done = bf16[4096,4096]{1,0:T(8,128)(2,1)} async-done(((bf16[1024,4096]{1,0:T(8,128)(2,1)}), bf16[4096,4096]{1,0:T(8,128)(2,1)}) %all-gather.11.cloned.1.call-update) | async-done | bytes 33554448 | tf_op jit(solution)/shard_map/all_gather | solution.py:186
  734.2 45.0 %fusion.10 = bf16[4096,1024]{1,0:T(8,128)(2,1)} fusion(bf16[4096,4096]{1,0:T(8,128)(2,1)} %all-gather.11.cloned.1.call-done, f32[1024,4096]{1,0:T(8,128)} %param.8), kind=kOutput, calls=%fused_computation.6 | convolution fusion | flops 34363932672 | bytes 58720256 | tf_op jit(solution)/shard_map/dot_general | solution.py:187
  779.2 43.0 %fusion.7.gain_hbm = f32[1024,4096]{1,0:T(8,128)} fusion(f32[1024,4096]{1,0:T(8,128)} %fusion.14, bf16[4096,4096]{1,0:T(8,128)(2,1)} %all-gather.9.cloned.1.call-done, bf16[4096,1024]{1,0:T(8,128)(2,1)} %fusion.10), kind=kOutput, calls=%fused_computation.5 | convolution fusion | flops 34363932672 | bytes 75497472 | tf_op jit(solution)/shard_map/dot_general | solution.py:188
  822.2 61.1 %sinkhorn.3 = f32[1024,4096]{1,0:T(8,128)} custom-call(f32[1024,4096]{1,0:T(8,128)} %fusion.7.gain_hbm, f32[1024,128]{1,0:T(8,128)S(1)} %broadcast_in_dim.2.mass_row, f32[4,8,128]{2,1,0:T(8,128)S(1)} %bitcast.12, f32[1]{0:T(128)} %bitcast.10.epsilon), custom_call_target="tpu_custom_call" | custom-call | flops 167772160 | bytes 33554432 | tf_op jit(solution)/shard_map/sinkhorn/pallas_call | solution.py:148
  883.3 11.7 %copy.11 = f32[1024,4096]{1,0:T(8,128)} copy(f32[1024,4096]{1,0:T(8,128)} %sinkhorn.3) | data formatting | bytes 33554432
Async XLA Ops:
  6.5 24.7 %all-gather.5.cloned.1.call-start = ((), (), s32[]{:S(2)}) async-start(), calls=%async_computation | async-start | bytes 2621440 | tf_op jit(solution)/shard_map/all_gather | solution.py:181
  8.6 223.5 %all-gather.7.cloned.1.call-start = ((), (), s32[]{:S(2)}) async-start(), calls=%async_computation.1 | async-start | bytes 41943040 | tf_op jit(solution)/shard_map/all_gather | solution.py:186
  17.7 13.6 %copy-start.1 = (f32[1024,256]{1,0:T(8,128)S(1)}, f32[1024,256]{1,0:T(8,128)}, u32[]{:S(2)}) copy-start(f32[1024,256]{1,0:T(8,128)} %param.13) | copy-start | bytes 3145732
  17.7 415.4 %all-gather.9.cloned.1.call-start = ((), (), s32[]{:S(2)}) async-start(), calls=%async_computation.2 | async-start | bytes 41943040 | tf_op jit(solution)/shard_map/all_gather | solution.py:183
  26.8 707.4 %all-gather.11.cloned.1.call-start = ((), (), s32[]{:S(2)}) async-start(), calls=%async_computation.3 | async-start | bytes 41943040 | tf_op jit(solution)/shard_map/all_gather | solution.py:186
  277.0 198.8 %copy-start.2 = (f32[1024]{0:T(1024)S(1)}, f32[1024]{0:T(1024)}, u32[]{:S(2)}) copy-start(f32[1024]{0:T(1024)} %param.11) | copy-start | bytes 12292
  277.0 199.0 %copy-start = (f32[4096]{0:T(1024)S(1)}, f32[4096]{0:T(1024)}, u32[]{:S(2)}) copy-start(f32[4096]{0:T(1024)} %param.12) | copy-start | bytes 49156
Sparse Core Ops, SparseCore 0:
  8.9 22.3 all-gather.4
  32.8 199.3 all-gather.6
  233.7 199.3 all-gather.8
  534.8 199.3 all-gather.10

commit v2 on v1

v2 whole, which is shorter than its diff:
```python
import functools

import jax
import jax.numpy as jnp
from jax import lax
from jax.experimental import pallas as pl
from jax.experimental.pallas import tpu as pltpu
from jax.sharding import PartitionSpec as P

ALPHA = 0.5
SWEEPS = 10
LANES = 128
CHUNKS = 4
BLOCK = 64
LOAD_ROWS = 128
STEP_WIDTHS = (512, 512, 512, 256, 256)
ROW_PARTS = 4
MESH = pl.DeviceIdType.MESH


def sinkhorn_kernel(group, n_gain, transposed, *refs):
    gains, refs = refs[:n_gain], refs[n_gain:]
    (mass_row, mass_col, epsilon, plan_hbm, kern, plan, row_scale, acc, col_scale, shift_fix,
     part_sum, peer_sum, part_top, peer_top, load_sem, store_sem, send_sem, recv_sem, top_send, top_recv) = refs
    rows, cols = kern.shape
    tiles = cols // LANES // CHUNKS
    width = cols // CHUNKS
    gain_rows = rows // n_gain
    me = lax.axis_index('rows')
    chip, core = me // 2, me % 2
    peers = [chip * 2 + (1 - core), (1 - chip) * 2 + core, (1 - chip) * 2 + (1 - core)]

    if transposed:
        loads = [pltpu.make_async_copy(gains[0].at[:, pl.ds(j * width, width)], kern.at[:, pl.ds(j * width, width)],
                                       load_sem.at[j]) for j in range(CHUNKS)]
    else:
        loads = []
        for b in range(rows // LOAD_ROWS):
            start = b * LOAD_ROWS
            source = gains[start // gain_rows].at[pl.ds(start % gain_rows, LOAD_ROWS)]
            loads.append(pltpu.make_async_copy(source, kern.at[pl.ds(start, LOAD_ROWS)], load_sem.at[b]))
    for load in loads:
        load.start()

    barrier = pltpu.get_barrier_semaphore()
    for peer in peers:
        pl.semaphore_signal(barrier, inc=1, device_id={'rows': peer}, device_id_type=MESH)
    pl.semaphore_wait(barrier, group - 1)

    def tile(j, t):
        start = j * width + t * LANES
        return slice(start, start + LANES)

    def sends(slot, j):
        return [pltpu.make_async_remote_copy(
            src_ref=part_sum.at[slot, j], dst_ref=peer_sum.at[slot, k, j], send_sem=send_sem.at[slot, k, j],
            recv_sem=recv_sem.at[slot, k, j], device_id={'rows': peers[k]}, device_id_type=MESH) for k in range(group - 1)]

    def top_sends(j):
        return [pltpu.make_async_remote_copy(
            src_ref=part_top.at[j], dst_ref=peer_top.at[k, j], send_sem=top_send.at[k, j],
            recv_sem=top_recv.at[k, j], device_id={'rows': peers[k]}, device_id_type=MESH) for k in range(group - 1)]

    inv_eps = 1.0 / epsilon[0]

    def split(val):
        return val.reshape(val.shape[0] // 8, 8, LANES)

    def row_update():
        for h in range(0, rows, 256):
            span = slice(h, h + 256)
            row_scale[span, :] = mass_row[span, :] / jnp.sum(acc[span, :], axis=1, keepdims=True)

    def col_pass(slot, j):
        def body(i, sums):
            span = pl.ds(i * BLOCK, BLOCK)
            scale = split(row_scale[span, :])
            return tuple(sums[t] + jnp.sum(split(kern[span, tile(j, t)]) * scale, axis=0) for t in range(tiles))
        sums = lax.fori_loop(0, rows // BLOCK, body, tuple(jnp.zeros((8, LANES), jnp.float32) for _ in range(tiles)))
        total = jnp.concatenate([jnp.sum(s, axis=0, keepdims=True) for s in sums], axis=0)
        if transposed:
            total = total * shift_fix[j]
        part_sum[slot, j] = total
        for send in sends(slot, j):
            send.start()

    def col_update(slot, j):
        for send in sends(slot, j):
            send.wait()
        total = part_sum[slot, j]
        for k in range(group - 1):
            total = total + peer_sum[slot, k, j]
        scale = mass_col[j] / total
        if transposed:
            scale = scale * shift_fix[j]
        col_scale[j] = scale

    def scale_rows(j):
        return [jnp.broadcast_to(col_scale[j, t:t + 1, :], (8, LANES)) for t in range(tiles)]

    def row_pass(j):
        scale = scale_rows(j)

        def body(i, carry):
            span = pl.ds(i * BLOCK, BLOCK)
            total = None if j == 0 else split(acc[span, :])
            for t in range(tiles):
                term = split(kern[span, tile(j, t)]) * scale[t][None]
                total = term if total is None else total + term
            acc[span, :] = total.reshape(BLOCK, LANES)
            return carry
        lax.fori_loop(0, rows // BLOCK, body, 0)

    def plan_chunk(j):
        scale = scale_rows(j)

        def plan_block(i, carry):
            span = pl.ds(i * BLOCK, BLOCK)
            left = split(row_scale[span, :])
            for t in range(tiles):
                val = left * split(kern[span, tile(j, t)]) * scale[t][None]
                plan[span, tile(j, t)] = val.reshape(BLOCK, LANES).astype(plan.dtype)
            return carry
        lax.fori_loop(0, rows // BLOCK, plan_block, 0)
        span = pl.ds(j * width, width)
        store = pltpu.make_async_copy(plan.at[:, span], plan_hbm.at[:, span], store_sem.at[j])
        store.start()
        return store

    if transposed:
        for j in range(CHUNKS):
            loads[j].wait()

            def top_block(i, tops, j=j):
                span = pl.ds(i * BLOCK, BLOCK)
                return tuple(jnp.maximum(tops[t], jnp.max(split(kern[span, tile(j, t)]), axis=0)) for t in range(tiles))
            tops = lax.fori_loop(0, rows // BLOCK, top_block,
                                 tuple(kern[0:8, tile(j, t)] for t in range(tiles)))
            tops = [jnp.max(top, axis=0, keepdims=True) for top in tops]
            wide = [jnp.broadcast_to(top, (8, LANES)) for top in tops]

            def exp_block(i, sums, j=j, wide=wide):
                span = pl.ds(i * BLOCK, BLOCK)
                out = []
                for t in range(tiles):
                    val = jnp.exp((split(kern[span, tile(j, t)]) - wide[t][None]) * inv_eps)
                    kern[span, tile(j, t)] = val.reshape(BLOCK, LANES)
                    out.append(sums[t] + jnp.sum(val, axis=0))
                return tuple(out)
            sums = lax.fori_loop(0, rows // BLOCK, exp_block,
                                 tuple(jnp.zeros((8, LANES), jnp.float32) for _ in range(tiles)))
            part_top[j, 0] = jnp.concatenate(tops, axis=0)
            part_top[j, 1] = jnp.concatenate([jnp.sum(s, axis=0, keepdims=True) for s in sums], axis=0)
            for send in top_sends(j):
                send.start()
        for j in range(CHUNKS):
            for send in top_sends(j):
                send.wait()
            top = part_top[j, 0]
            for k in range(group - 1):
                top = jnp.maximum(top, peer_top[k, j, 0])
            fix = jnp.exp((part_top[j, 0] - top) * inv_eps)
            total = part_top[j, 1] * fix
            for k in range(group - 1):
                total = total + peer_top[k, j, 1] * jnp.exp((peer_top[k, j, 0] - top) * inv_eps)
            shift_fix[j] = fix
            col_scale[j] = mass_col[j] / total * fix
            row_pass(j)
        row_update()
    else:
        for b, load in enumerate(loads):
            load.wait()

            def exp_rows(i, carry, b=b):
                span = pl.ds(b * LOAD_ROWS + i * BLOCK, BLOCK)
                top = kern[span, 0:LANES]
                for t in range(1, cols // LANES):
                    top = jnp.maximum(top, kern[span, t * LANES:(t + 1) * LANES])
                top = jnp.max(top, axis=1, keepdims=True)
                total = jnp.zeros((BLOCK, LANES), jnp.float32)
                for t in range(cols // LANES):
                    val = jnp.exp((kern[span, t * LANES:(t + 1) * LANES] - top) * inv_eps)
                    kern[span, t * LANES:(t + 1) * LANES] = val
                    total = total + val
                acc[span, :] = total
                return carry
            lax.fori_loop(0, LOAD_ROWS // BLOCK, exp_rows, 0)
        row_update()

    def sweep(n, carry):
        slot = lax.rem(n, 2)
        for j in range(CHUNKS):
            col_pass(slot, j)
        for j in range(CHUNKS):
            col_update(slot, j)
            row_pass(j)
        row_update()
        return carry
    lax.fori_loop(0, SWEEPS - 1, sweep, 0)

    stores = []
    if transposed:
        for j in range(CHUNKS):
            stores.append(plan_chunk(j))
    else:
        last = (SWEEPS - 1) % 2
        for j in range(CHUNKS):
            col_pass(last, j)
        for j in range(CHUNKS):
            col_update(last, j)
            stores.append(plan_chunk(j))
    for store in stores:
        store.wait()


def sinkhorn(group, gains, mass_row, mass_col, epsilon, dtype, transposed, collective_id):
    cols = gains[0].shape[1]
    rows = sum(g.shape[0] for g in gains)
    tiles = cols // LANES // CHUNKS
    row_rep = jnp.broadcast_to(mass_row[:, None], (rows, LANES))
    col_tiles = mass_col.reshape(CHUNKS, tiles, LANES)
    n_load = CHUNKS if transposed else rows // LOAD_ROWS
    vec = (CHUNKS, tiles, LANES)
    pair = (CHUNKS, 2, tiles, LANES)
    return pl.pallas_call(
        functools.partial(sinkhorn_kernel, group, len(gains), transposed),
        out_shape=jax.ShapeDtypeStruct((rows, cols), dtype),
        in_specs=[pl.BlockSpec(memory_space=pl.ANY)] * len(gains) + [
            pl.BlockSpec(memory_space=pltpu.VMEM), pl.BlockSpec(memory_space=pltpu.VMEM),
            pl.BlockSpec(memory_space=pltpu.SMEM)],
        out_specs=pl.BlockSpec(memory_space=pl.ANY),
        scratch_shapes=[
            pltpu.VMEM((rows, cols), jnp.float32),
            pltpu.VMEM((rows, cols), dtype),
            pltpu.VMEM((rows, LANES), jnp.float32),
            pltpu.VMEM((rows, LANES), jnp.float32),
            pltpu.VMEM(vec, jnp.float32),
            pltpu.VMEM(vec, jnp.float32),
            pltpu.VMEM((2,) + vec, jnp.float32),
            pltpu.VMEM((2, group - 1) + vec, jnp.float32),
            pltpu.VMEM(pair, jnp.float32),
            pltpu.VMEM((group - 1,) + pair, jnp.float32),
            pltpu.SemaphoreType.DMA((n_load,)),
            pltpu.SemaphoreType.DMA((CHUNKS,)),
            pltpu.SemaphoreType.DMA((2, group - 1, CHUNKS)),
            pltpu.SemaphoreType.DMA((2, group - 1, CHUNKS)),
            pltpu.SemaphoreType.DMA((group - 1, CHUNKS)),
            pltpu.SemaphoreType.DMA((group - 1, CHUNKS)),
        ],
        compiler_params=pltpu.CompilerParams(collective_id=collective_id, has_side_effects=True,
                                             vmem_limit_bytes=48 * 1024 * 1024),
        cost_estimate=pl.CostEstimate(flops=4 * SWEEPS * rows * cols, bytes_accessed=8 * rows * cols,
                                      transcendentals=rows * cols),
        name='sinkhorn_cols' if transposed else 'sinkhorn_rows',
    )(*gains, row_rep, col_tiles, epsilon.reshape(1))


def swap(value, distance):
    return lax.ppermute(value, 'rows', [(i, i ^ distance) for i in range(4)])


class Wire:
    def __init__(self):
        self.landed = []

    def send(self, value, distance):
        if len(self.landed) >= 2:
            value, self.landed[-2] = lax.optimization_barrier((value, self.landed[-2]))
        self.landed.append(swap(value, distance))
        return len(self.landed) - 1

    def get(self, index):
        return self.landed[index]


def solution(mesh):
    group = mesh.shape['rows']

    def local_fgw(cost_src, cost_tgt, plan_init, mass_src, mass_tgt, feat_src, feat_tgt, epsilon):
        rows, cols = cost_src.shape
        half = cols // 2
        quad = rows // 2
        me = lax.axis_index('rows')
        chip, core = me // 2, me % 2
        even = core == 0
        dot = functools.partial(jnp.einsum, preferred_element_type=jnp.float32)
        wire = Wire()

        def ordered(mine, other, axis=0):
            return jnp.where(even, jnp.concatenate([mine, other], axis), jnp.concatenate([other, mine], axis))

        def chip_order(mine, other, axis):
            return jnp.where(chip == 0, jnp.concatenate([mine, other], axis), jnp.concatenate([other, mine], axis))

        def pack(cost):
            diag = lax.dynamic_slice(cost, (0, rows * me), (rows, rows))
            off = lax.dynamic_slice(cost, (0, rows * (me + 1 - 2 * core)), (rows, rows))
            edge = jnp.where(even, off[:quad, :], off[:, quad:].T)
            return jnp.concatenate([diag[:quad, :quad], diag[:quad, quad:], diag[quad:, quad:],
                                    edge[:, :quad], edge[:, quad:]], axis=0)

        def assemble(cost, packed):
            near = ordered(cost, swap(cost, 1))
            packed_pair = swap(packed, 1)
            packs = [jnp.where(even, packed, packed_pair), jnp.where(even, packed_pair, packed)]
            diags, edges = [], []
            for item in packs:
                p = [item[k * quad:(k + 1) * quad] for k in range(5)]
                diags.append(jnp.block([[p[0], p[1]], [p[1].T, p[2]]]))
                edges.append(jnp.concatenate([p[3], p[4]], axis=1))
            edge = jnp.concatenate(edges, axis=0)
            far = jnp.block([[diags[0], edge], [edge.T, diags[1]]])
            turned = lax.dynamic_slice(near, (0, half * (1 - chip)), (half, half)).T
            return jnp.concatenate([near, chip_order(turned, far, 1)], axis=0)

        src_half = cost_src.astype(jnp.bfloat16)
        tgt_half = cost_tgt.astype(jnp.bfloat16)
        feats = jnp.concatenate([feat_src, feat_tgt], axis=1).astype(jnp.bfloat16)
        start = plan_init.astype(jnp.bfloat16)
        depth = feat_src.shape[1]

        src_wire = wire.send(pack(src_half), 2)
        feat_wire = wire.send(feats, 2)
        start_mine = lax.dynamic_slice(start, (0, half * core), (rows, half))
        start_other = lax.dynamic_slice(start, (0, half * (1 - core)), (rows, half))
        spans, at = [], 0
        for w in STEP_WIDTHS:
            spans.append((at, at + w))
            at += w
        plan_wires = []
        for lo, hi in spans:
            plan_wires.append((wire.send(start_mine[:, lo:hi], 2), wire.send(start_other[:, lo:hi], 3)))
        tgt_wire = wire.send(pack(tgt_half), 2)

        src_all = assemble(src_half, wire.get(src_wire))
        feat_near = ordered(feats, swap(feats, 1))
        feat_far = ordered(wire.get(feat_wire), swap(wire.get(feat_wire), 1))
        feat_all = chip_order(feat_near, feat_far, 0)
        start_pair = swap(start_other, 1)
        tgt_mine = lax.dynamic_slice(tgt_half, (0, half * core), (rows, half))
        tgt_other = lax.dynamic_slice(tgt_half, (0, half * (1 - core)), (rows, half))
        mass_all = lax.all_gather(mass_src, 'rows', tiled=True)
        mass_cols = lax.dynamic_slice(mass_tgt, (rows * me,), (rows,))

        gain = (2.0 * ALPHA) * dot('jd,id->ji', feats[:, depth:], feat_all[:, :depth])
        for (lo, hi), (same, cross) in zip(spans, plan_wires):
            near = ordered(start_mine[:, lo:hi], start_pair[:, lo:hi])
            far = ordered(wire.get(same), wire.get(cross))
            prod_a = dot('kj,ki->ji', jnp.concatenate([near, far], axis=0), src_all).astype(jnp.bfloat16)
            both_a = jnp.concatenate([prod_a, swap(prod_a, 1)], axis=0)
            both_c = jnp.concatenate([tgt_mine[:, lo:hi], tgt_other[:, lo:hi]], axis=1)
            gain = gain + (2.0 * (1.0 - ALPHA)) * dot('rj,ji->ri', both_c, both_a)
        plan_t = sinkhorn(group, [gain], mass_cols, mass_all, epsilon, jnp.bfloat16, True, 0)

        tgt_all = assemble(tgt_half, wire.get(tgt_wire))
        part = rows // ROW_PARTS
        src_parts = src_all.reshape(4, ROW_PARTS, part, cols)
        arrived = []
        for h in range(ROW_PARTS):
            blocks = [dot('ik,jk->ij', src_parts[2 + k, h], plan_t).astype(jnp.bfloat16) for k in range(2)]
            arrived.append((wire.send(jnp.where(even, blocks[0], blocks[1]), 2),
                            wire.send(jnp.where(even, blocks[1], blocks[0]), 3)))
        near_blocks = [dot('ik,jk->ij', src_all[k * rows:(k + 1) * rows], plan_t).astype(jnp.bfloat16) for k in range(2)]
        near_mine = jnp.where(even, near_blocks[0], near_blocks[1])
        near_pair = swap(jnp.where(even, near_blocks[1], near_blocks[0]), 1)
        near = ordered(near_mine, near_pair, 1)
        gains = []
        for h in range(ROW_PARTS):
            span = slice(h * part, (h + 1) * part)
            far = ordered(wire.get(arrived[h][0]), wire.get(arrived[h][1]), 1)
            prod_b = dot('ij,jl->il', jnp.concatenate([near[span], far], axis=1), tgt_all)
            cross = dot('id,jd->ij', feats[span, :depth], feat_all[:, depth:])
            gains.append((2.0 * ALPHA) * cross + (2.0 * (1.0 - ALPHA)) * prod_b)
        return sinkhorn(group, gains, mass_src, mass_tgt, epsilon, jnp.float32, False, 1)

    row_spec = P(('pairs', 'rows'), None)
    vec_spec = P(('pairs', 'rows'))
    in_specs = (row_spec, row_spec, row_spec, vec_spec, P('pairs'), row_spec, row_spec, P())
    return jax.shard_map(local_fgw, mesh=mesh, in_specs=in_specs, out_specs=row_spec, check_vma=False)
```

time: 902 us -> 1230 us (1.36)
  waiting for transfers between devices: 550 us -> 122 us
  other arithmetic: 20.1 us -> 362 us
  local copies, waits for them, and re-layouts: 11.9 us -> 202 us
  matrix products: 186 us -> 347 us
  blocking collectives: 0 us -> 39.6 us
  starting transfers between devices: 0.13 us -> 23 us
    all_gather x4 -> x0, waiting for transfers between devices: 550 us -> none  [the longest x2 390 us: local_fgw(): transport_all = lax.all_gather(transport, 'rows', tiled=True)]
    select_n x0 -> x26, other arithmetic: none -> 255 us  [the longest x3 166 us: chip_order(): jnp.where(chip == 0, jnp.concatenate([mine, other], axis), jnp.concatenat...]
    dot_general x5 -> x29, matrix products: 186 us -> 347 us  [the longest x5 103 us: local_fgw(): dot('kj,ki->ji', jnp.concatenate([near, far], axis=0), src_all)]
    ppermute x0 -> x34, waiting for transfers between devices: none -> 122 us  [swap(): return lax.ppermute(value, 'rows', [(i, i ^ distance) for i in range(4)])]
    concatenate x0 -> x6, other arithmetic: none -> 82.7 us  [the longest x1 36.4 us: assemble(): far = jnp.block([[diags[0], edge], [edge.T, diags[1]]])]
    concatenate x0 -> x3, local copies, waits for them, and re-layouts: none -> 75.2 us  [the longest x1 40.4 us: assemble(): return jnp.concatenate([near, chip_order(turned, far, 1)], axis=0)]
    all_gather x0 -> x1, blocking collectives: none -> 39.6 us  [local_fgw(): mass_all = lax.all_gather(mass_src, 'rows', tiled=True)]
    slice x0 -> x18, local copies, waits for them, and re-layouts: none -> 34.9 us  [the longest x3 8.67 us: local_fgw(): near = ordered(start_mine[:, lo:hi], start_pair[:, lo:hi])]
  transfers between devices with their start and end apart: 4 -> 34, of which waited for: 4 -> 11; matrix products, arithmetic and copies ran while one was open for 8% -> 66% of each run, Pallas kernels for 0% -> 0%
where the time goes in v2:
time: 1230 us; the launch traced here: 1220 us
  other arithmetic  362 us (29%)
  matrix products  347 us (28%)
  local copies, waits for them, and re-layouts  202 us (16%)
  waiting for transfers between devices  122 us (10%)
  Pallas kernels  121 us (10%)
  blocking collectives  39.6 us (3%)
  starting transfers between devices  23 us (2%)
    select_n x3, other arithmetic, chip_order(): jnp.where(chip == 0, jnp.concatenate([mine, other], axis), jnp.concatenat...  166 us
    ppermute x34, waiting for transfers between devices, swap(): return lax.ppermute(value, 'rows', [(i, i ^ distance) for i in range(4)])  122 us
    pallas_call x2, Pallas kernels, sinkhorn(): pl.pallas_call(functools.partial(sinkhorn_kernel, group, len(gains), tran...  121 us
    dot_general x5, matrix products, local_fgw(): dot('kj,ki->ji', jnp.concatenate([near, far], axis=0), src_all)  103 us
    dot_general x5, matrix products, local_fgw(): gain = gain + 2.0 * (1.0 - ALPHA) * dot('rj,ji->ri', both_c, both_a)  90.7 us
    select_n x19, other arithmetic, ordered(): jnp.where(even, jnp.concatenate([mine, other], axis), jnp.concatenate([ot...  81.9 us
    dot_general x4, matrix products, local_fgw(): dot('ij,jl->il', jnp.concatenate([near[span], far], axis=1), tgt_all)  73.5 us
    unnamed x88, local copies, waits for them, and re-layouts  43.5 us
  transfers between devices with their start and end apart: 34, of which 11 were waited for; matrix products, arithmetic and copies ran while one was open for 66% of the time, Pallas kernels for 0%

profile of v2, /device:TPU:0, one launch (start us, length us, event | category | flops | bytes accessed | tf_op | source)
XLA Modules:
  0.0 1219.0 jit_solution(52545726758680362)
XLA Ops:
  7.0 13.8 %copy.77 = bf16[1024,4096]{0,1:T(8,128)(2,1)} copy(f32[1024,4096]{1,0:T(8,128)} %param.8) | data formatting | bytes 25165824 | tf_op args[0]
  30.4 9.0 convert_element_type.55
  44.7 9.0 convert_element_type.57
  53.7 6.3 constant_dynamic-slice_fusion.22
  74.8 39.6 %all_gather.3 = f32[4096]{0:T(1024)S(1)} all-gather(f32[1024]{0:T(1024)S(1)} %copy-done.33), channel_id=1, replica_groups=mesh['pairs'=2,'rows'=4] {'rows'}, dimensions={0}, use_global_device_ids=true | all-gather | bytes 20480 | tf_op jit(solution)/shard_map/all_gather | solution.py:342
  124.4 8.2 maximum_select_fusion.6
  141.8 8.3 fusion.47
  165.6 15.7 %collective-permute-done.6 = bf16[1024,512]{1,0:T(8,128)(2,1)S(1)} collective-permute-done((bf16[1024,512]{1,0:T(8,128)(2,1)S(1)}, bf16[1024,512]{1,0:T(8,128)(2,1)S(1)}, u32[]{:S(2)}, u32[]{:S(2)}) %collective-permute-start.6) | collective-permute-done | bytes 1048608 | tf_op jit(solution)/shard_map/ppermute | solution.py:259
  184.8 17.7 %collective-permute-done.14 = bf16[1024,512]{1,0:T(8,128)(2,1)S(1)} collective-permute-done((bf16[1024,512]{1,0:T(8,128)(2,1)S(1)}, bf16[1024,512]{1,0:T(8,128)(2,1)S(1)}, u32[]{:S(2)}, u32[]{:S(2)}) %collective-permute-start.14) | collective-permute-done | bytes 1048608 | tf_op jit(solution)/shard_map/ppermute | solution.py:259
  217.7 21.0 %collective-permute-done.17 = bf16[1024,256]{1,0:T(8,128)(2,1)S(1)} collective-permute-done((bf16[1024,256]{1,0:T(8,128)(2,1)S(1)}, bf16[1024,256]{1,0:T(8,128)(2,1)S(1)}, u32[]{:S(2)}, u32[]{:S(2)}) %collective-permute-start.17) | collective-permute-done | bytes 524320 | tf_op jit(solution)/shard_map/ppermute | solution.py:259
  256.9 18.5 %collective-permute-done.13 = bf16[1024,512]{1,0:T(8,128)(2,1)} collective-permute-done((bf16[1024,512]{1,0:T(8,128)(2,1)}, bf16[1024,512]{1,0:T(8,128)(2,1)}, u32[]{:S(2)}, u32[]{:S(2)}) %collective-permute-start.13) | collective-permute-done | bytes 1048608 | tf_op jit(solution)/shard_map/ppermute | solution.py:259
  277.1 36.4 %maximum_maximum_fusion = bf16[2048,2048]{0,1:T(8,128)(2,1)} fusion(bf16[512,512]{0,1:T(8,128)(2,1)} %get-tuple-element.153, bf16[512,512]{0,1:T(8,128)(2,1)} %copy.83, bf16[512,512]{0,1:T(8,128)(2,1)} %get-tuple-element.152, bf16[512,512]{0,1:T(8,128)(2,1)} %get-tuple-element.151, bf16[1024,1024]{0,1:T(8,128)(2,1)S(1)} %copy.84, ...), kind=kLoop, calls=%fused_computation.16 | loop fusion | flops 109051904 | bytes 16777216 | tf_op jit(solution)/shard_map/jit(block)/concatenate | solution.py:312
  313.5 12.3 %copy.85 = bf16[2048,2048]{1,0:T(8,128)(2,1)} copy(bf16[2048,2048]{0,1:T(8,128)(2,1)} %maximum_maximum_fusion) | data formatting | bytes 16777216 | tf_op jit(solution)/shard_map/jit(block)/concatenate | solution.py:312
  341.9 20.9 %maximum_select_fusion = bf16[2048,4096]{0,1:T(8,128)(2,1)} fusion(bf16[1024,4096]{0,1:T(8,128)(2,1)} %collective-permute-done.3, bf16[1024,4096]{0,1:T(8,128)(2,1)} %copy.77, pred[]{:T(512)S(6)} %eq.11), kind=kLoop, calls=%fused_computation.2 | loop fusion | flops 75497472 | bytes 33554432 | tf_op jit(solution)/shard_map/jit(_where)/select_n | solution.py:290
  362.9 8.4 dynamic-slice_bitcast_fusion
  371.3 12.3 %copy.86 = bf16[2048,2048]{0,1:T(8,128)(2,1)} copy(bf16[2048,2048]{1,0:T(8,128)(2,1)} %dynamic-slice_bitcast_fusion) | data formatting | bytes 16777216 | tf_op jit(solution)/shard_map/transpose | solution.py:313
  383.6 13.8 %pad_maximum_fusion.2 = bf16[2048,4096]{1,0:T(8,128)(2,1)} fusion(bf16[2048,2048]{1,0:T(8,128)(2,1)} %copy.85, bf16[2048,2048]{1,0:T(8,128)(2,1)} %dynamic-slice_bitcast_fusion), kind=kLoop, calls=%fused_computation.3 | loop fusion | flops 33554432 | bytes 33554432 | tf_op jit(solution)/shard_map/concatenate | solution.py:293
  397.4 22.5 %copy.87 = bf16[2048,4096]{0,1:T(8,128)(2,1)} copy(bf16[2048,4096]{1,0:T(8,128)(2,1)} %pad_maximum_fusion.2) | data formatting | bytes 33554432 | tf_op jit(solution)/shard_map/concatenate | solution.py:293
  419.9 21.8 %maximum_select_fusion.1 = bf16[2048,4096]{0,1:T(8,128)(2,1)} fusion(bf16[2048,4096]{0,1:T(8,128)(2,1)} %copy.87, bf16[2048,2048]{0,1:T(8,128)(2,1)} %copy.86, bf16[512,512]{0,1:T(8,128)(2,1)} %get-tuple-element.153, bf16[512,512]{0,1:T(8,128)(2,1)} %copy.83, bf16[512,512]{0,1:T(8,128)(2,1)} %get-tuple-element.152, bf16[512,512]{0,1:T(8,128)(2,1)} %get-tuple-element.151, ...), kind=kLoop, calls=%fused_computation.4 | loop fusion | flops 243269632 | bytes 50331648 | tf_op jit(solution)/shard_map/jit(_where)/select_n | solution.py:293
  441.8 16.0 %convolution_convert_fusion.3 = bf16[256,4096]{1,0:T(8,128)(2,1)} fusion(bf16[2048,256]{1,0:T(8,128)(2,1)S(1)} %copy-done.25, bf16[2048,256]{1,0:T(8,128)(2,1)S(1)} %copy-done.23, bf16[2048,4096]{0,1:T(8,128)(2,1)} %maximum_select_fusion.1, bf16[2048,4096]{0,1:T(8,128)(2,1)} %maximum_select_fusion), kind=kOutput, calls=%fused_computation.41 | convolution fusion | flops 8662286336 | bytes 37748736 | tf_op jit(solution)/shard_map/kj,ki->ji/dot_general | solution.py:349
  457.8 23.4 %convolution_convert_fusion.2 = bf16[512,4096]{1,0:T(8,128)(2,1)} fusion(bf16[2048,512]{1,0:T(8,128)(2,1)S(1)} %copy-done.11, bf16[2048,512]{1,0:T(8,128)(2,1)} %maximum_select_fusion.8, bf16[2048,4096]{0,1:T(8,128)(2,1)} %maximum_select_fusion.1, bf16[2048,4096]{0,1:T(8,128)(2,1)} %maximum_select_fusion), kind=kOutput, calls=%fused_computation.32 | convolution fusion | flops 17257463808 | bytes 41943040 | tf_op jit(solution)/shard_map/kj,ki->ji/dot_general | solution.py:349
  481.7 24.2 %convolution_convert_fusion.1 = bf16[512,4096]{1,0:T(8,128)(2,1)} fusion(bf16[2048,512]{1,0:T(8,128)(2,1)} %maximum_select_fusion.11, bf16[2048,512]{1,0:T(8,128)(2,1)} %maximum_select_fusion.10, bf16[2048,4096]{0,1:T(8,128)(2,1)} %maximum_select_fusion.1, bf16[2048,4096]{0,1:T(8,128)(2,1)} %maximum_select_fusion), kind=kOutput, calls=%fused_computation.31 | convolution fusion | flops 17257463808 | bytes 41943040 | tf_op jit(solution)/shard_map/kj,ki->ji/dot_general | solution.py:349
  506.0 15.5 %convolution_convert_fusion.4 = bf16[256,4096]{1,0:T(8,128)(2,1)} fusion(bf16[2048,256]{1,0:T(8,128)(2,1)S(1)} %copy-done.24, bf16[2048,256]{1,0:T(8,128)(2,1)S(1)} %copy-done.22, bf16[2048,4096]{0,1:T(8,128)(2,1)} %maximum_select_fusion.1, bf16[2048,4096]{0,1:T(8,128)(2,1)} %maximum_select_fusion), kind=kOutput, calls=%fused_computation.42 | convolution fusion | flops 8662286336 | bytes 37748736 | tf_op jit(solution)/shard_map/kj,ki->ji/dot_general | solution.py:349
  521.5 22.8 %pad_maximum_fusion = bf16[4096,4096]{0,1:T(8,128)(2,1)} fusion(bf16[2048,4096]{0,1:T(8,128)(2,1)} %maximum_select_fusion.1, bf16[2048,4096]{0,1:T(8,128)(2,1)} %maximum_select_fusion), kind=kLoop, calls=%fused_computation | loop fusion | flops 67108864 | bytes 67108864 | tf_op jit(solution)/shard_map/concatenate | solution.py:314
  544.4 40.4 %copy.90 = bf16[4096,4096]{1,0:T(8,128)(2,1)} copy(bf16[4096,4096]{0,1:T(8,128)(2,1)} %pad_maximum_fusion) | data formatting | bytes 67108864 | tf_op jit(solution)/shard_map/concatenate | solution.py:314
  585.1 18.7 %maximum_select_fusion.2 = bf16[2048,4096]{1,0:T(8,128)(2,1)} fusion(bf16[1024,4096]{1,0:T(8,128)(2,1)} %collective-permute-done.26, bf16[1024,4096]{1,0:T(8,128)(2,1)} %convert_element_type.57, pred[]{:T(512)S(6)} %eq.11), kind=kLoop, calls=%fused_computation.5 | loop fusion | flops 75497472 | bytes 33554432 | tf_op jit(solution)/shard_map/jit(_where)/select_n | solution.py:290
  603.8 8.4 constant_dynamic-slice_fusion.20
  612.2 12.3 %copy.126 = bf16[2048,2048]{0,1:T(8,128)(2,1)} copy(bf16[2048,2048]{1,0:T(8,128)(2,1)} %constant_dynamic-slice_fusion.20) | data formatting | bytes 16777216
  624.7 24.3 %convolution_convert_fusion = bf16[512,4096]{1,0:T(8,128)(2,1)} fusion(bf16[2048,512]{1,0:T(8,128)(2,1)} %maximum_select_fusion.13, bf16[2048,512]{1,0:T(8,128)(2,1)} %maximum_select_fusion.12, bf16[2048,4096]{0,1:T(8,128)(2,1)} %maximum_select_fusion.1, bf16[2048,4096]{0,1:T(8,128)(2,1)} %maximum_select_fusion), kind=kOutput, calls=%fused_computation.30 | convolution fusion | flops 17257463808 | bytes 41943040 | tf_op jit(solution)/shard_map/kj,ki->ji/dot_general | solution.py:349
  649.4 12.8 %fusion.29 = f32[1024,4096]{1,0:T(8,128)} fusion(bf16[256,4096]{1,0:T(8,128)(2,1)} %collective-permute-done.18, bf16[256,4096]{1,0:T(8,128)(2,1)} %convolution_convert_fusion.4, bf16[1024,256]{1,0:T(8,128)(2,1)S(1)} %copy-done.31, bf16[1024,256]{1,0:T(8,128)(2,1)} %get-tuple-element.79), kind=kOutput, calls=%fused_computation.53 | convolution fusion | flops 4305453056 | bytes 22020096 | tf_op jit(solution)/shard_map/rj,ji->ri/dot_general | solution.py:352
  676.0 142.3 %maximum_select_fusion.3 = bf16[2048,4096]{1,0:T(8,128)(2,1)} fusion(bf16[512,512]{1,0:T(8,128)(2,1)} %get-tuple-element.159, bf16[512,512]{1,0:T(8,128)(2,1)} %copy.100, bf16[512,512]{1,0:T(8,128)(2,1)} %get-tuple-element.158, bf16[512,512]{1,0:T(8,128)(2,1)} %get-tuple-element.157, bf16[1024,1024]{1,0:T(8,128)(2,1)S(1)} %copy.101, ...), kind=kLoop, calls=%fused_computation.6 | loop fusion | flops 478150656 | bytes 33554432 | tf_op jit(solution)/shard_map/jit(_where)/select_n | solution.py:293
  818.3 14.8 %fusion.8 = f32[1024,4096]{1,0:T(8,128)} fusion(bf16[512,4096]{1,0:T(8,128)(2,1)} %collective-permute-done.9, bf16[512,4096]{1,0:T(8,128)(2,1)} %convolution_convert_fusion.2, bf16[1024,512]{1,0:T(8,128)(2,1)S(1)} %copy-done.19, bf16[1024,512]{1,0:T(8,128)(2,1)S(1)} %copy-done.20), kind=kOutput, calls=%fused_computation.17 | convolution fusion | flops 8610906112 | bytes 27262976 | tf_op jit(solution)/shard_map/rj,ji->ri/dot_general | solution.py:352
  833.2 14.0 %fusion.12 = f32[1024,4096]{1,0:T(8,128)} fusion(bf16[512,4096]{1,0:T(8,128)(2,1)} %collective-permute-done.12, bf16[512,4096]{1,0:T(8,128)(2,1)S(1)} %copy-done.35, bf16[1024,512]{1,0:T(8,128)(2,1)S(1)} %copy-done.17, bf16[1024,512]{1,0:T(8,128)(2,1)S(1)} %copy-done.18), kind=kOutput, calls=%fused_computation.21 | convolution fusion | flops 8610906112 | bytes 27262976 | tf_op jit(solution)/shard_map/rj,ji->ri/dot_general | solution.py:352
  847.2 14.6 %fusion.16 = f32[1024,4096]{1,0:T(8,128)} fusion(bf16[512,4096]{1,0:T(8,128)(2,1)} %collective-permute-done.15, bf16[512,4096]{1,0:T(8,128)(2,1)} %convolution_convert_fusion, bf16[1024,512]{1,0:T(8,128)(2,1)S(1)} %copy-done.15, bf16[1024,512]{1,0:T(8,128)(2,1)S(1)} %copy-done.16), kind=kOutput, calls=%fused_computation.25 | convolution fusion | flops 8610906112 | bytes 27262976 | tf_op jit(solution)/shard_map/rj,ji->ri/dot_general | solution.py:352
  861.8 34.6 %fusion.3.refs_0_ = f32[1024,4096]{1,0:T(8,128)} fusion(f32[1024,4096]{1,0:T(8,128)} %fusion.29, f32[1024,4096]{1,0:T(8,128)} %fusion.16, f32[1024,4096]{1,0:T(8,128)} %fusion.12, f32[1024,4096]{1,0:T(8,128)} %fusion.8, f32[4096,1024]{0,1:T(8,128)} %fusion.47, bf16[256,4096]{1,0:T(8,128)(2,1)} %collective-permute-done.21, ...), kind=kOutput, calls=%fused_computation.11 | convolution fusion | flops 4326424576 | bytes 105906176 | tf_op jit(solution)/shard_map/rj,ji->ri/dot_general | solution.py:352
  896.6 59.9 %sinkhorn_cols.1 = bf16[1024,4096]{1,0:T(8,128)(2,1)} custom-call(f32[1024,4096]{1,0:T(8,128)} %fusion.3.refs_0_, f32[1024,128]{1,0:T(8,128)S(1)} %broadcast_in_dim.4.refs_1_, f32[4,8,128]{2,1,0:T(8,128)S(1)} %bitcast.104, f32[1]{0:T(128)} %bitcast.102.refs_3_), custom_call_target="tpu_custom_call" | custom-call | flops 167772160 | bytes 33554432 | tf_op jit(solution)/shard_map/sinkhorn_cols/pallas_call | solution.py:225
  956.5 6.5 fusion.91
  972.1 10.1 fusion.79
  993.6 11.8 broadcast_select_fusion.5
  1021.6 7.8 collective-permute-done.28
  1029.4 9.5 collective-permute-done.29
  1051.9 9.5 collective-permute-done.31
  1067.4 18.4 %convolution_add_fusion.1.refs_2_ = f32[256,4096]{1,0:T(8,128)} fusion(f32[256,4096]{1,0:T(8,128)} %convolution_bitcast_fusion.1, bf16[256,2048]{0,1:T(8,128)(2,1)S(1)} %maximum_select_fusion.20, bf16[256,2048]{0,1:T(8,128)(2,1)} %get-tuple-element.104, bf16[2048,4096]{1,0:T(8,128)(2,1)} %maximum_select_fusion.3, bf16[2048,4096]{1,0:T(8,128)(2,1)} %maximum_select_fusion.2), kind=kOutput, calls=%fused_computation.38 | convolution fusion | flops 8662286336 | bytes 44040192 | tf_op jit(solution)/shard_map/ij,jl->il/dot_general | solution.py:371
  1085.7 18.7 %convolution_add_fusion.2.refs_1_ = f32[256,4096]{1,0:T(8,128)} fusion(f32[256,4096]{1,0:T(8,128)} %convolution_bitcast_fusion.2, bf16[256,2048]{0,1:T(8,128)(2,1)S(1)} %maximum_select_fusion.19, bf16[256,2048]{0,1:T(8,128)(2,1)} %get-tuple-element.105, bf16[2048,4096]{1,0:T(8,128)(2,1)} %maximum_select_fusion.3, bf16[2048,4096]{1,0:T(8,128)(2,1)} %maximum_select_fusion.2), kind=kOutput, calls=%fused_computation.39 | convolution fusion | flops 8662286336 | bytes 44040192 | tf_op jit(solution)/shard_map/ij,jl->il/dot_general | solution.py:371
  1104.5 18.2 %convolution_add_fusion.3.refs_0_ = f32[256,4096]{1,0:T(8,128)} fusion(f32[256,4096]{1,0:T(8,128)} %convolution_bitcast_fusion.3, bf16[256,2048]{0,1:T(8,128)(2,1)S(1)} %maximum_select_fusion.18, bf16[256,2048]{0,1:T(8,128)(2,1)S(1)} %copy-done.29, bf16[2048,4096]{1,0:T(8,128)(2,1)} %maximum_select_fusion.3, bf16[2048,4096]{1,0:T(8,128)(2,1)} %maximum_select_fusion.2), kind=kOutput, calls=%fused_computation.40 | convolution fusion | flops 8662286336 | bytes 44040192 | tf_op jit(solution)/shard_map/ij,jl->il/dot_general | solution.py:371
  1124.6 18.2 %convolution_add_fusion.refs_3_ = f32[256,4096]{1,0:T(8,128)} fusion(f32[256,4096]{1,0:T(8,128)} %convolution_bitcast_fusion, bf16[256,2048]{0,1:T(8,128)(2,1)S(1)} %maximum_select_fusion.21, bf16[256,2048]{0,1:T(8,128)(2,1)S(1)} %copy-done.28, bf16[2048,4096]{1,0:T(8,128)(2,1)} %maximum_select_fusion.3, bf16[2048,4096]{1,0:T(8,128)(2,1)} %maximum_select_fusion.2), kind=kOutput, calls=%fused_computation.37 | convolution fusion | flops 8662286336 | bytes 44040192 | tf_op jit(solution)/shard_map/ij,jl->il/dot_general | solution.py:371
  1145.2 61.6 %sinkhorn_rows.1 = f32[1024,4096]{1,0:T(8,128)} custom-call(f32[256,4096]{1,0:T(8,128)S(1)} %copy-done, f32[256,4096]{1,0:T(8,128)} %convolution_add_fusion.2.refs_1_, f32[256,4096]{1,0:T(8,128)} %convolution_add_fusion.1.refs_2_, f32[256,4096]{1,0:T(8,128)} %convolution_add_fusion.refs_3_, f32[1024,128]{1,0:T(8,128)S(1)} %broadcast_in_dim.5.refs_4_, ...), custom_call_target="tpu_custom_call" | custom-call | flops 167772160 | bytes 33554432 | tf_op jit(solution)/shard_map/sinkhorn_rows/pallas_call | solution.py:225
  1206.8 11.7 copy.129
  (214 shorter events, 200.5 us)
Async XLA Ops:
  3.6 65.7 %collective-permute-start.1 = (bf16[1024,512]{1,0:T(8,128)(2,1)}, bf16[1024,512]{1,0:T(8,128)(2,1)}, u32[]{:S(2)}, u32[]{:S(2)}) collective-permute-start(bf16[1024,512]{1,0:T(8,128)(2,1)} %pad_maximum_fusion.5), channel_id=1, source_target_pairs={{0,2},{1,3},{2,0},{3,1},{4,6},{5,7},{6,4},{7,5}} | collective-permute-start | bytes 3145736 | tf_op jit(solution)/shard_map/ppermute | solution.py:259
  7.0 117.4 %collective-permute-start = (bf16[1024,512]{1,0:T(8,128)(2,1)}, bf16[1024,512]{1,0:T(8,128)(2,1)}, u32[]{:S(2)}, u32[]{:S(2)}) collective-permute-start(bf16[1024,512]{1,0:T(8,128)(2,1)} %pad_maximum_fusion.5), channel_id=1, source_target_pairs={{0,1},{1,0},{2,3},{3,2},{4,5},{5,4},{6,7},{7,6}} | collective-permute-start | bytes 3145736 | tf_op jit(solution)/shard_map/ppermute | solution.py:259
  30.4 119.6 %collective-permute-start.5 = (bf16[2560,512]{0,1:T(8,128)(2,1)}, bf16[2560,512]{0,1:T(8,128)(2,1)}, u32[]{:S(2)}, u32[]{:S(2)}) collective-permute-start(bf16[2560,512]{0,1:T(8,128)(2,1)} %pad_maximum_fusion.3), channel_id=1, source_target_pairs={{0,2},{1,3},{2,0},{3,1},{4,6},{5,7},{6,4},{7,5}} | collective-permute-start | bytes 7864328 | tf_op jit(solution)/shard_map/ppermute | solution.py:259
  44.2 160.0 %collective-permute-start.4 = (bf16[1024,2048]{1,0:T(8,128)(2,1)}, bf16[1024,2048]{1,0:T(8,128)(2,1)}, u32[]{:S(2)}, u32[]{:S(2)}) collective-permute-start(bf16[1024,2048]{1,0:T(8,128)(2,1)} %constant_dynamic-slice_fusion.27), channel_id=1, source_target_pairs={{0,1},{1,0},{2,3},{3,2},{4,5},{5,4},{6,7},{7,6}} | collective-permute-start | bytes 12582920 | tf_op jit(solution)/shard_map/ppermute | solution.py:259
  69.3 63.3 %collective-permute-start.7 = (bf16[1024,512]{1,0:T(8,128)(2,1)}, bf16[1024,512]{1,0:T(8,128)(2,1)}, u32[]{:S(2)}, u32[]{:S(2)}) collective-permute-start(bf16[1024,512]{1,0:T(8,128)(2,1)} %get-tuple-element.44), channel_id=1, source_target_pairs={{0,3},{1,2},{2,1},{3,0},{4,7},{5,6},{6,5},{7,4}} | collective-permute-start | bytes 3145736 | tf_op jit(solution)/shard_map/ppermute | solution.py:259
  70.9 63.5 %collective-permute-start.2 = (bf16[1024,512]{1,0:T(8,128)(2,1)}, bf16[1024,512]{1,0:T(8,128)(2,1)}, u32[]{:S(2)}, u32[]{:S(2)}) collective-permute-start(bf16[1024,512]{1,0:T(8,128)(2,1)} %collective-permute-done.1), channel_id=1, source_target_pairs={{0,1},{1,0},{2,3},{3,2},{4,5},{5,4},{6,7},{7,6}} | collective-permute-start | bytes 3145736 | tf_op jit(solution)/shard_map/ppermute | solution.py:259
  74.7 57.9 %copy-start.27 = (bf16[1024,512]{1,0:T(8,128)(2,1)S(1)}, bf16[1024,512]{1,0:T(8,128)(2,1)}, u32[]{:S(2)}) copy-start(bf16[1024,512]{1,0:T(8,128)(2,1)} %get-tuple-element.49) | copy-start | bytes 3145732
  124.4 217.5 %collective-permute-start.3 = (bf16[1024,4096]{0,1:T(8,128)(2,1)}, bf16[1024,4096]{0,1:T(8,128)(2,1)}, u32[]{:S(2)}, u32[]{:S(2)}) collective-permute-start(bf16[1024,4096]{0,1:T(8,128)(2,1)} %copy.77), channel_id=1, source_target_pairs={{0,1},{1,0},{2,3},{3,2},{4,5},{5,4},{6,7},{7,6}} | collective-permute-start | bytes 25165832 | tf_op jit(solution)/shard_map/ppermute | solution.py:259
  132.6 25.4 %collective-permute-start.11 = (bf16[1024,512]{1,0:T(8,128)(2,1)S(1)}, bf16[1024,512]{1,0:T(8,128)(2,1)S(1)}, u32[]{:S(2)}, u32[]{:S(2)}) collective-permute-start(bf16[1024,512]{1,0:T(8,128)(2,1)S(1)} %copy-done.27), channel_id=1, source_target_pairs={{0,3},{1,2},{2,1},{3,0},{4,7},{5,6},{6,5},{7,4}} | collective-permute-start | bytes 3145736 | tf_op jit(solution)/shard_map/ppermute | solution.py:259
  150.0 31.2 %collective-permute-start.6 = (bf16[1024,512]{1,0:T(8,128)(2,1)S(1)}, bf16[1024,512]{1,0:T(8,128)(2,1)S(1)}, u32[]{:S(2)}, u32[]{:S(2)}) collective-permute-start(bf16[1024,512]{1,0:T(8,128)(2,1)S(1)} %copy-done.8), channel_id=1, source_target_pairs={{0,2},{1,3},{2,0},{3,1},{4,6},{5,7},{6,4},{7,5}} | collective-permute-start | bytes 3145736 | tf_op jit(solution)/shard_map/ppermute | solution.py:259
  158.0 44.6 %collective-permute-start.14 = (bf16[1024,512]{1,0:T(8,128)(2,1)S(1)}, bf16[1024,512]{1,0:T(8,128)(2,1)S(1)}, u32[]{:S(2)}, u32[]{:S(2)}) collective-permute-start(bf16[1024,512]{1,0:T(8,128)(2,1)S(1)} %copy-done.26), channel_id=1, source_target_pairs={{0,3},{1,2},{2,1},{3,0},{4,7},{5,6},{6,5},{7,4}} | collective-permute-start | bytes 3145736 | tf_op jit(solution)/shard_map/ppermute | solution.py:259
  162.8 41.4 %copy-start.32 = (bf16[1024,256]{1,0:T(8,128)(2,1)S(1)}, bf16[1024,256]{1,0:T(8,128)(2,1)}, u32[]{:S(2)}) copy-start(bf16[1024,256]{1,0:T(8,128)(2,1)} %get-tuple-element.57) | copy-start | bytes 1572868
  162.8 79.9 %collective-permute-start.8 = (bf16[2560,512]{0,1:T(8,128)(2,1)}, bf16[2560,512]{0,1:T(8,128)(2,1)S(1)}, u32[]{:S(2)}, u32[]{:S(2)}) collective-permute-start(bf16[2560,512]{0,1:T(8,128)(2,1)} %collective-permute-done.5), channel_id=1, source_target_pairs={{0,1},{1,0},{2,3},{3,2},{4,5},{5,4},{6,7},{7,6}} | collective-permute-start | bytes 7864328 | tf_op jit(solution)/shard_map/ppermute | solution.py:259
  181.2 403.5 %collective-permute-start.26 = (bf16[1024,4096]{1,0:T(8,128)(2,1)}, bf16[1024,4096]{1,0:T(8,128)(2,1)}, u32[]{:S(2)}, u32[]{:S(2)}) collective-permute-start(bf16[1024,4096]{1,0:T(8,128)(2,1)} %convert_element_type.57), channel_id=1, source_target_pairs={{0,1},{1,0},{2,3},{3,2},{4,5},{5,4},{6,7},{7,6}} | collective-permute-start | bytes 25165832 | tf_op jit(solution)/shard_map/ppermute | solution.py:259
  181.2 28.4 %copy-start.13 = (bf16[1024,256]{1,0:T(8,128)(2,1)S(1)}, bf16[1024,256]{1,0:T(8,128)(2,1)}, u32[]{:S(2)}) copy-start(bf16[1024,256]{1,0:T(8,128)(2,1)} %get-tuple-element.59) | copy-start | bytes 1572868
  202.6 37.8 %collective-permute-start.10 = (bf16[1024,512]{1,0:T(8,128)(2,1)S(1)}, bf16[1024,512]{1,0:T(8,128)(2,1)S(1)}, u32[]{:S(2)}, u32[]{:S(2)}) collective-permute-start(bf16[1024,512]{1,0:T(8,128)(2,1)S(1)} %get-tuple-element.47), channel_id=1, source_target_pairs={{0,2},{1,3},{2,0},{3,1},{4,6},{5,7},{6,4},{7,5}} | collective-permute-start | bytes 3145736 | tf_op jit(solution)/shard_map/ppermute | solution.py:259
  204.2 34.5 %collective-permute-start.17 = (bf16[1024,256]{1,0:T(8,128)(2,1)S(1)}, bf16[1024,256]{1,0:T(8,128)(2,1)S(1)}, u32[]{:S(2)}, u32[]{:S(2)}) collective-permute-start(bf16[1024,256]{1,0:T(8,128)(2,1)S(1)} %copy-done.32), channel_id=1, source_target_pairs={{0,3},{1,2},{2,1},{3,0},{4,7},{5,6},{6,5},{7,4}} | collective-permute-start | bytes 1572872 | tf_op jit(solution)/shard_map/ppermute | solution.py:259
  238.7 100.7 %collective-permute-start.20 = (bf16[1024,256]{1,0:T(8,128)(2,1)}, bf16[1024,256]{1,0:T(8,128)(2,1)}, u32[]{:S(2)}, u32[]{:S(2)}) collective-permute-start(bf16[1024,256]{1,0:T(8,128)(2,1)} %get-tuple-element.61), channel_id=1, source_target_pairs={{0,3},{1,2},{2,1},{3,0},{4,7},{5,6},{6,5},{7,4}} | collective-permute-start | bytes 1572872 | tf_op jit(solution)/shard_map/ppermute | solution.py:259
  240.4 35.0 %collective-permute-start.13 = (bf16[1024,512]{1,0:T(8,128)(2,1)}, bf16[1024,512]{1,0:T(8,128)(2,1)}, u32[]{:S(2)}, u32[]{:S(2)}) collective-permute-start(bf16[1024,512]{1,0:T(8,128)(2,1)} %get-tuple-element.51), channel_id=1, source_target_pairs={{0,2},{1,3},{2,0},{3,1},{4,6},{5,7},{6,4},{7,5}} | collective-permute-start | bytes 3145736 | tf_op jit(solution)/shard_map/ppermute | solution.py:259
  275.4 50.5 %collective-permute-start.16 = (bf16[1024,256]{1,0:T(8,128)(2,1)}, bf16[1024,256]{1,0:T(8,128)(2,1)}, u32[]{:S(2)}, u32[]{:S(2)}) collective-permute-start(bf16[1024,256]{1,0:T(8,128)(2,1)} %get-tuple-element.55), channel_id=1, source_target_pairs={{0,2},{1,3},{2,0},{3,1},{4,6},{5,7},{6,4},{7,5}} | collective-permute-start | bytes 1572872 | tf_op jit(solution)/shard_map/ppermute | solution.py:259
  325.9 13.3 %collective-permute-start.19 = (bf16[1024,256]{1,0:T(8,128)(2,1)}, bf16[1024,256]{1,0:T(8,128)(2,1)S(1)}, u32[]{:S(2)}, u32[]{:S(2)}) collective-permute-start(bf16[1024,256]{1,0:T(8,128)(2,1)} %get-tuple-element.59), channel_id=1, source_target_pairs={{0,2},{1,3},{2,0},{3,1},{4,6},{5,7},{6,4},{7,5}} | collective-permute-start | bytes 1572872 | tf_op jit(solution)/shard_map/ppermute | solution.py:259
  339.1 285.4 %collective-permute-start.24 = (bf16[2560,512]{1,0:T(8,128)(2,1)}, bf16[2560,512]{1,0:T(8,128)(2,1)}, u32[]{:S(2)}, u32[]{:S(2)}) collective-permute-start(bf16[2560,512]{1,0:T(8,128)(2,1)} %pad_maximum_fusion.4), channel_id=1, source_target_pairs={{0,2},{1,3},{2,0},{3,1},{4,6},{5,7},{6,4},{7,5}} | collective-permute-start | bytes 7864328 | tf_op jit(solution)/shard_map/ppermute | solution.py:259
  419.9 21.8 %copy-start.23 = (bf16[2048,256]{1,0:T(8,128)(2,1)S(1)}, bf16[2048,256]{1,0:T(8,128)(2,1)}, u32[]{:S(2)}) copy-start(bf16[2048,256]{1,0:T(8,128)(2,1)} %maximum_select_fusion.16) | copy-start | bytes 3145732
  419.9 21.8 %copy-start.25 = (bf16[2048,256]{1,0:T(8,128)(2,1)S(1)}, bf16[2048,256]{1,0:T(8,128)(2,1)}, u32[]{:S(2)}) copy-start(bf16[2048,256]{1,0:T(8,128)(2,1)} %maximum_select_fusion.17) | copy-start | bytes 3145732
  457.8 404.0 %collective-permute-start.21 = (bf16[256,4096]{1,0:T(8,128)(2,1)}, bf16[256,4096]{1,0:T(8,128)(2,1)}, u32[]{:S(2)}, u32[]{:S(2)}) collective-permute-start(bf16[256,4096]{1,0:T(8,128)(2,1)} %convolution_convert_fusion.3), channel_id=1, source_target_pairs={{0,1},{1,0},{2,3},{3,2},{4,5},{5,4},{6,7},{7,6}} | collective-permute-start | bytes 6291464 | tf_op jit(solution)/shard_map/ppermute | solution.py:259
  481.2 24.8 %copy-start.22 = (bf16[2048,256]{1,0:T(8,128)(2,1)S(1)}, bf16[2048,256]{1,0:T(8,128)(2,1)}, u32[]{:S(2)}) copy-start(bf16[2048,256]{1,0:T(8,128)(2,1)} %maximum_select_fusion.14) | copy-start | bytes 3145732
  481.2 24.8 %copy-start.24 = (bf16[2048,256]{1,0:T(8,128)(2,1)S(1)}, bf16[2048,256]{1,0:T(8,128)(2,1)}, u32[]{:S(2)}) copy-start(bf16[2048,256]{1,0:T(8,128)(2,1)} %maximum_select_fusion.15) | copy-start | bytes 3145732
  481.2 337.1 %collective-permute-start.9 = (bf16[512,4096]{1,0:T(8,128)(2,1)}, bf16[512,4096]{1,0:T(8,128)(2,1)}, u32[]{:S(2)}, u32[]{:S(2)}) collective-permute-start(bf16[512,4096]{1,0:T(8,128)(2,1)} %convolution_convert_fusion.2), channel_id=1, source_target_pairs={{0,1},{1,0},{2,3},{3,2},{4,5},{5,4},{6,7},{7,6}} | collective-permute-start | bytes 12582920 | tf_op jit(solution)/shard_map/ppermute | solution.py:259
  505.9 327.3 %collective-permute-start.12 = (bf16[512,4096]{1,0:T(8,128)(2,1)}, bf16[512,4096]{1,0:T(8,128)(2,1)}, u32[]{:S(2)}, u32[]{:S(2)}) collective-permute-start(bf16[512,4096]{1,0:T(8,128)(2,1)} %convolution_convert_fusion.1), channel_id=1, source_target_pairs={{0,1},{1,0},{2,3},{3,2},{4,5},{5,4},{6,7},{7,6}} | collective-permute-start | bytes 12582920 | tf_op jit(solution)/shard_map/ppermute | solution.py:259
  584.7 64.3 %collective-permute-start.18 = (bf16[256,4096]{1,0:T(8,128)(2,1)}, bf16[256,4096]{1,0:T(8,128)(2,1)}, u32[]{:S(2)}, u32[]{:S(2)}) collective-permute-start(bf16[256,4096]{1,0:T(8,128)(2,1)} %convolution_convert_fusion.4), channel_id=1, source_target_pairs={{0,1},{1,0},{2,3},{3,2},{4,5},{5,4},{6,7},{7,6}} | collective-permute-start | bytes 6291464 | tf_op jit(solution)/shard_map/ppermute | solution.py:259
  624.5 24.9 %copy-start.31 = (bf16[1024,256]{1,0:T(8,128)(2,1)S(1)}, bf16[1024,256]{1,0:T(8,128)(2,1)}, u32[]{:S(2)}) copy-start(bf16[1024,256]{1,0:T(8,128)(2,1)} %get-tuple-element.78) | copy-start | bytes 1572868
  624.5 37.6 %collective-permute-start.27 = (bf16[2560,512]{1,0:T(8,128)(2,1)}, bf16[2560,512]{1,0:T(8,128)(2,1)S(1)}, u32[]{:S(2)}, u32[]{:S(2)}) collective-permute-start(bf16[2560,512]{1,0:T(8,128)(2,1)} %collective-permute-done.24), channel_id=1, source_target_pairs={{0,1},{1,0},{2,3},{3,2},{4,5},{5,4},{6,7},{7,6}} | collective-permute-start | bytes 7864328 | tf_op jit(solution)/shard_map/ppermute | solution.py:259
  649.0 198.2 %collective-permute-start.15 = (bf16[512,4096]{1,0:T(8,128)(2,1)}, bf16[512,4096]{1,0:T(8,128)(2,1)}, u32[]{:S(2)}, u32[]{:S(2)}) collective-permute-start(bf16[512,4096]{1,0:T(8,128)(2,1)} %convolution_convert_fusion), channel_id=1, source_target_pairs={{0,1},{1,0},{2,3},{3,2},{4,5},{5,4},{6,7},{7,6}} | collective-permute-start | bytes 12582920 | tf_op jit(solution)/shard_map/ppermute | solution.py:259
  676.0 142.3 %copy-start.19 = (bf16[1024,512]{1,0:T(8,128)(2,1)S(1)}, bf16[1024,512]{1,0:T(8,128)(2,1)}, u32[]{:S(2)}) copy-start(bf16[1024,512]{1,0:T(8,128)(2,1)} %get-tuple-element.86) | copy-start | bytes 3145732
  676.0 142.3 %copy-start.20 = (bf16[1024,512]{1,0:T(8,128)(2,1)S(1)}, bf16[1024,512]{1,0:T(8,128)(2,1)}, u32[]{:S(2)}) copy-start(bf16[1024,512]{1,0:T(8,128)(2,1)} %get-tuple-element.87) | copy-start | bytes 3145732
  861.8 34.6 %dynamic-slice-start = ((f32[4096]{0:T(1024)}, s32[]{:T(128)}), f32[1024]{0:T(1024)S(1)}, s32[]{:S(2)}) async-start(f32[4096]{0:T(1024)} %param.12, s32[]{:T(128)} %select_n.240), calls=%async_computation | async-start | bytes 8704 | tf_op jit(solution)/shard_map/dynamic_slice | solution.py:343
  992.2 18.0 %collective-permute-start.23 = (bf16[256,1024]{0,1:T(8,128)(2,1)}, bf16[256,1024]{0,1:T(8,128)(2,1)S(1)}, u32[]{:S(2)}, u32[]{:S(2)}) collective-permute-start(bf16[256,1024]{0,1:T(8,128)(2,1)} %get-tuple-element.62), channel_id=1, source_target_pairs={{0,2},{1,3},{2,0},{3,1},{4,6},{5,7},{6,4},{7,5}} | collective-permute-start | bytes 1572872 | tf_op jit(solution)/shard_map/ppermute | solution.py:259
  992.2 24.3 %collective-permute-start.25 = (bf16[256,1024]{0,1:T(8,128)(2,1)}, bf16[256,1024]{0,1:T(8,128)(2,1)}, u32[]{:S(2)}, u32[]{:S(2)}) collective-permute-start(bf16[256,1024]{0,1:T(8,128)(2,1)} %get-tuple-element.65), channel_id=1, source_target_pairs={{0,3},{1,2},{2,1},{3,0},{4,7},{5,6},{6,5},{7,4}} | collective-permute-start | bytes 1572872 | tf_op jit(solution)/shard_map/ppermute | solution.py:259
  1005.4 57.4 %collective-permute-start.22 = (bf16[1024,1024]{0,1:T(8,128)(2,1)}, bf16[1024,1024]{0,1:T(8,128)(2,1)S(1)}, u32[]{:S(2)}, u32[]{:S(2)}) collective-permute-start(bf16[1024,1024]{0,1:T(8,128)(2,1)} %get-tuple-element.108), channel_id=1, source_target_pairs={{0,1},{1,0},{2,3},{3,2},{4,5},{5,4},{6,7},{7,6}} | collective-permute-start | bytes 6291464 | tf_op jit(solution)/shard_map/ppermute | solution.py:259
  1010.2 19.2 %collective-permute-start.28 = (bf16[256,1024]{0,1:T(8,128)(2,1)S(1)}, bf16[256,1024]{0,1:T(8,128)(2,1)S(1)}, u32[]{:S(2)}, u32[]{:S(2)}) collective-permute-start(bf16[256,1024]{0,1:T(8,128)(2,1)S(1)} %get-tuple-element.67), channel_id=1, source_target_pairs={{0,2},{1,3},{2,0},{3,1},{4,6},{5,7},{6,4},{7,5}} | collective-permute-start | bytes 1572872 | tf_op jit(solution)/shard_map/ppermute | solution.py:259
  1016.5 22.5 %copy-start.36 = (bf16[256,1024]{0,1:T(8,128)(2,1)S(1)}, bf16[256,1024]{0,1:T(8,128)(2,1)}, u32[]{:S(2)}) copy-start(bf16[256,1024]{0,1:T(8,128)(2,1)} %get-tuple-element.73) | copy-start | bytes 1572868
  1016.5 22.5 %collective-permute-start.29 = (bf16[256,1024]{0,1:T(8,128)(2,1)S(1)}, bf16[256,1024]{0,1:T(8,128)(2,1)S(1)}, u32[]{:S(2)}, u32[]{:S(2)}) collective-permute-start(bf16[256,1024]{0,1:T(8,128)(2,1)S(1)} %get-tuple-element.69), channel_id=1, source_target_pairs={{0,3},{1,2},{2,1},{3,0},{4,7},{5,6},{6,5},{7,4}} | collective-permute-start | bytes 1572872 | tf_op jit(solution)/shard_map/ppermute | solution.py:259
  1029.4 22.5 %collective-permute-start.30 = (bf16[256,1024]{0,1:T(8,128)(2,1)S(1)}, bf16[256,1024]{0,1:T(8,128)(2,1)S(1)}, u32[]{:S(2)}, u32[]{:S(2)}) collective-permute-start(bf16[256,1024]{0,1:T(8,128)(2,1)S(1)} %copy-done.37), channel_id=1, source_target_pairs={{0,2},{1,3},{2,0},{3,1},{4,6},{5,7},{6,4},{7,5}} | collective-permute-start | bytes 1572872 | tf_op jit(solution)/shard_map/ppermute | solution.py:259
  1039.0 23.9 %copy-start.12 = (bf16[1024,1024]{0,1:T(8,128)(2,1)S(1)}, bf16[1024,1024]{0,1:T(8,128)(2,1)}, u32[]{:S(2)}) copy-start(bf16[1024,1024]{0,1:T(8,128)(2,1)} %get-tuple-element.107) | copy-start | bytes 6291460
  1039.0 22.5 %collective-permute-start.31 = (bf16[256,1024]{0,1:T(8,128)(2,1)S(1)}, bf16[256,1024]{0,1:T(8,128)(2,1)S(1)}, u32[]{:S(2)}, u32[]{:S(2)}) collective-permute-start(bf16[256,1024]{0,1:T(8,128)(2,1)S(1)} %copy-done.36), channel_id=1, source_target_pairs={{0,3},{1,2},{2,1},{3,0},{4,7},{5,6},{6,5},{7,4}} | collective-permute-start | bytes 1572872 | tf_op jit(solution)/shard_map/ppermute | solution.py:259
  1051.9 70.8 %collective-permute-start.32 = (bf16[256,1024]{0,1:T(8,128)(2,1)}, bf16[256,1024]{0,1:T(8,128)(2,1)}, u32[]{:S(2)}, u32[]{:S(2)}) collective-permute-start(bf16[256,1024]{0,1:T(8,128)(2,1)} %get-tuple-element.75), channel_id=1, source_target_pairs={{0,2},{1,3},{2,0},{3,1},{4,6},{5,7},{6,4},{7,5}} | collective-permute-start | bytes 1572872 | tf_op jit(solution)/shard_map/ppermute | solution.py:259
  1061.4 61.3 %collective-permute-start.33 = (bf16[256,1024]{0,1:T(8,128)(2,1)}, bf16[256,1024]{0,1:T(8,128)(2,1)}, u32[]{:S(2)}, u32[]{:S(2)}) collective-permute-start(bf16[256,1024]{0,1:T(8,128)(2,1)} %get-tuple-element.76), channel_id=1, source_target_pairs={{0,3},{1,2},{2,1},{3,0},{4,7},{5,6},{6,5},{7,4}} | collective-permute-start | bytes 1572872 | tf_op jit(solution)/shard_map/ppermute | solution.py:259
  1104.5 20.1 %copy-start.28 = (bf16[256,2048]{0,1:T(8,128)(2,1)S(1)}, bf16[256,2048]{0,1:T(8,128)(2,1)}, u32[]{:S(2)}) copy-start(bf16[256,2048]{0,1:T(8,128)(2,1)} %get-tuple-element.103) | copy-start | bytes 3145732
  (29 other events, 282.9 us)

commit v3 on v2

--- a/solution.py
+++ b/solution.py
@@ -13,8 +13,6 @@
 CHUNKS = 4
 BLOCK = 64
 LOAD_ROWS = 128
-STEP_WIDTHS = (512, 512, 512, 256, 256)
-ROW_PARTS = 4
 MESH = pl.DeviceIdType.MESH
 
 
@@ -255,123 +253,448 @@
     )(*gains, row_rep, col_tiles, epsilon.reshape(1))
 
 
-def swap(value, distance):
-    return lax.ppermute(value, 'rows', [(i, i ^ distance) for i in range(4)])
-
-
-class Wire:
-    def __init__(self):
-        self.landed = []
-
-    def send(self, value, distance):
-        if len(self.landed) >= 2:
-            value, self.landed[-2] = lax.optimization_barrier((value, self.landed[-2]))
-        self.landed.append(swap(value, distance))
-        return len(self.landed) - 1
-
-    def get(self, index):
-        return self.landed[index]
+STEP = 256
+SLAB = 512
+NT = (((1,), (1,)), ((), ()))
+NN = (((1,), (0,)), ((), ()))
+
+
+def weighted(value, factor):
+    return value if factor == 1.0 else value * factor
+
+
+def mm(left, right, dims):
+    return lax.dot_general(left, right, dims, preferred_element_type=jnp.float32)
+
+
+class Links:
+    def __init__(self, send_sem, recv_sem):
+        self.send_sem, self.recv_sem = send_sem, recv_sem
+
+    def copy(self, source, target, peer, index):
+        return pltpu.make_async_remote_copy(src_ref=source, dst_ref=target, send_sem=self.send_sem.at[index],
+                                            recv_sem=self.recv_sem.at[index], device_id={'rows': peer}, device_id_type=MESH)
+
+
+def places():
+    me = lax.axis_index('rows')
+    chip, core = me // 2, me % 2
+    return me, chip, core, chip * 2 + (1 - core), (1 - chip) * 2 + core, (1 - chip) * 2 + (1 - core)
+
+
+def entry_barrier(peers):
+    barrier = pltpu.get_barrier_semaphore()
+    for peer in peers:
+        pl.semaphore_signal(barrier, inc=1, device_id={'rows': peer}, device_id_type=MESH)
+    pl.semaphore_wait(barrier, len(peers))
+
+
+def block_sources(cost, me, core, rows):
+    quad = rows // 2
+    diag = me * rows
+    off = (me + 1 - 2 * core) * rows
+
+    def at(row, col):
+        return cost.at[pl.ds(pl.multiple_of(row, quad), quad), pl.ds(pl.multiple_of(col, quad), quad)]
+    return [at(0, diag), at(0, diag + quad), at(quad, diag + quad), at(0, off + quad * core), at(quad * core, off + quad)]
+
+
+def assemble(cost, cost_near, blocks, far, slab, turned, sems, chip, core, rows):
+    quad = rows // 2
+    half = 2 * rows
+    away = half * (1 - chip)
+    for source, owner in ((cost, core), (cost_near, 1 - core)):
+        for a in range(rows // SLAB):
+            load = pltpu.make_async_copy(source.at[pl.ds(a * SLAB, SLAB), pl.ds(pl.multiple_of(away, half), half)], slab, sems.at[0])
+            load.start()
+            load.wait()
+
+            def turn(b, carry):
+                turned[pl.ds(pl.multiple_of(b * SLAB, SLAB), SLAB), :] = slab[:, pl.ds(pl.multiple_of(b * SLAB, SLAB), SLAB)].T
+                return carry
+            lax.fori_loop(0, half // SLAB, turn, 0)
+            col = pl.multiple_of(half * chip + owner * rows + a * SLAB, SLAB)
+            store = pltpu.make_async_copy(turned, far.at[:, pl.ds(col, SLAB)], sems.at[1])
+            store.start()
+            store.wait()
+
+    def corner(k, carry):
+        cc = core + k - 2 * core * k
+        base, other = cc * rows, (1 - cc) * rows
+        spots = [(base, base), (base, base + quad), (base + quad, base + quad),
+                 (base, other + quad * cc), (base + quad * cc, other + quad)]
+        loads = [pltpu.make_async_copy(blocks.at[k, b], slab.at[:, pl.ds(b % 4 * quad, quad)] if b < 4 else
+                                       turned.at[pl.ds(3 * quad, quad), :], sems.at[2 + b]) for b in range(5)]
+        for load in loads:
+            load.start()
+        for load in loads:
+            load.wait()
+        turned[pl.ds(0, quad), :] = slab[:, quad:2 * quad].T
+        turned[pl.ds(quad, quad), :] = slab[:, 3 * quad:4 * quad].T
+        turned[pl.ds(2 * quad, quad), :] = turned[pl.ds(3 * quad, quad), :].T
+        stores = []
+
+        def put(source, row, col):
+            target = far.at[pl.ds(pl.multiple_of(row, quad), quad), pl.ds(pl.multiple_of(away + col, quad), quad)]
+            stores.append(pltpu.make_async_copy(source, target, sems.at[7 + len(stores)]))
+            stores[-1].start()
+        for b in range(4):
+            put(slab.at[:, pl.ds(b * quad, quad)], *spots[b])
+        put(turned.at[pl.ds(3 * quad, quad), :], *spots[4])
+        for t, b in enumerate((1, 3, 4)):
+            put(turned.at[pl.ds(t * quad, quad), :], spots[b][1], spots[b][0])
+        for store in stores:
+            store.wait()
+        return carry
+    lax.fori_loop(0, 2, corner, 0)
+
+
+def first_kernel(src, tgt, start, feats, gain, src_near, src_blocks, src_far, tgt_near, tgt_blocks, feat_peer,
+                 start_near, start_far, acc, tgt_keep, src_buf, start_buf, own_buf, near_buf, slab, turned, feat_buf,
+                 load_sem, src_sem, block_sem, send_sem, recv_sem, free_sem):
+    rows, cols = src.shape
+    half = cols // 2
+    steps = half // STEP
+    me, chip, core, near, same, cross = places()
+    links = Links(send_sem, recv_sem)
+    keep = pltpu.make_async_copy(tgt, tgt_keep, load_sem.at[0])
+    keep.start()
+    entry_barrier((near, same, cross))
+
+    def col_span(base, s):
+        return pl.ds(pl.multiple_of(base + s * STEP, STEP), STEP)
+
+    mine, other = half * core, half * (1 - core)
+    local = [links.copy(src, src_near, near, 0),
+             links.copy(feats, feat_peer.at[0], near, 1),
+             links.copy(start.at[:, pl.ds(pl.multiple_of(other, half), half)], start_near, near, 2),
+             links.copy(tgt, tgt_near, near, 3)]
+    src_out = [links.copy(block, src_blocks.at[0, b], same, 4 + b) for b, block in enumerate(block_sources(src, me, core, rows))]
+    feat_out = links.copy(feats, feat_peer.at[1], same, 9)
+    tgt_out = [links.copy(block, tgt_blocks.at[0, b], same, 10 + b) for b, block in enumerate(block_sources(tgt, me, core, rows))]
+    src_pass = links.copy(src_blocks.at[0], src_blocks.at[1], near, 15)
+    feat_pass = links.copy(feat_peer.at[1], feat_peer.at[2], near, 16)
+    tgt_pass = links.copy(tgt_blocks.at[0], tgt_blocks.at[1], near, 17)
+
+    def start_out(s):
+        return [links.copy(start.at[:, col_span(mine, s)], start_far.at[0, :, col_span(0, s)], same, 18 + s),
+                links.copy(start.at[:, col_span(other, s)], start_far.at[1, :, col_span(0, s)], cross, 18 + steps + s)]
+
+    def near_copy(s, slot):
+        return links.copy(own_buf.at[slot], near_buf.at[slot], near, 18 + 2 * steps + slot)
+
+    for copy in local[:3] + src_out + [feat_out]:
+        copy.start()
+    for s in range(steps):
+        for copy in start_out(s):
+            copy.start()
+    for copy in tgt_out + [local[3]]:
+        copy.start()
+
+    for copy in src_out:
+        copy.wait_recv()
+    src_pass.start()
+    local[0].wait_recv()
+    src_pass.wait_recv()
+    assemble(src, src_near, src_blocks, src_far, slab, turned, block_sem, chip, core, rows)
+
+    feat_out.wait_recv()
+    feat_pass.start()
+    local[1].wait_recv()
+    feat_pass.wait_recv()
+    depth = feats.shape[1] // 2
+    own_feat = pltpu.make_async_copy(feats, feat_buf.at[0], load_sem.at[1])
+    own_feat.start()
+    own_feat.wait()
+    for k, device in enumerate((me, near, same, cross)):
+        source = feats if k == 0 else feat_peer.at[k - 1]
+        load = pltpu.make_async_copy(source, feat_buf.at[1], load_sem.at[1])
+        load.start()
+        load.wait()
+
+        def cross_term(h, carry, device=device):
+            block = mm(feat_buf[0, :, depth:], feat_buf[1, pl.ds(pl.multiple_of(h * 256, 256), 256), :depth], NT)
+            acc[:, pl.ds(pl.multiple_of(device * rows + h * 256, 256), 256)] = weighted(block, 2.0 * ALPHA)
+            return carry
+        lax.fori_loop(0, rows // 256, cross_term, 0)
+    keep.wait()
+
+    per = rows // SLAB
+    n_blocks = 4 * per
+
+    def src_load(b):
+        if b < per:
+            source = src.at[pl.ds(b * SLAB, SLAB)]
+        elif b < 2 * per:
+            source = src_near.at[pl.ds((b - per) * SLAB, SLAB)]
+        else:
+            source = src_far.at[pl.ds((b - 2 * per) * SLAB, SLAB)]
+        return pltpu.make_async_copy(source, src_buf.at[b % 2], src_sem.at[b % 2])
+
+    def row_of(b):
+        if b < per:
+            return me * rows + b * SLAB
+        if b < 2 * per:
+            return near * rows + (b - per) * SLAB
+        return (1 - chip) * half + (b - 2 * per) * SLAB
+
+    def gather(left_base, left_s, right, slot):
+        def update(h, carry):
+            span = pl.ds(pl.multiple_of(h * 512, 512), 512)
+            block = mm(tgt_keep[:, col_span(left_base, left_s)], right[slot, span, :], NT)
+            acc[:, span] += weighted(block, 2.0 * (1.0 - ALPHA))
+            return carry
+        lax.fori_loop(0, cols // 512, update, 0)
+
+    local[2].wait_recv()
+    src_load(0).start()
+
+    def step(s, carry):
+        slot = lax.rem(s, 2)
+        for copy in start_out(s):
+            copy.wait_recv()
+        loads = []
+        for k, device in enumerate((me, near, same, cross)):
+            source = (start.at[:, col_span(mine, s)] if k == 0 else start_near.at[:, col_span(0, s)] if k == 1
+                      else start_far.at[k - 2, :, col_span(0, s)])
+            loads.append(pltpu.make_async_copy(source, start_buf.at[pl.ds(pl.multiple_of(device * rows, rows), rows)],
+                                               load_sem.at[2 + k]))
+        for load in loads:
+            load.start()
+
+        @pl.when(s >= 2)
+        def _():
+            near_copy(s - 2, slot).wait_send()
+        for load in loads:
+            load.wait()
+        for b in range(n_blocks):
+            src_load(b).wait()
+            if b + 1 < n_blocks:
+                src_load(b + 1).start()
+            else:
+                @pl.when(s + 1 < steps)
+                def _():
+                    src_load(0).start()
+            own_buf[slot, pl.ds(pl.multiple_of(row_of(b), SLAB), SLAB), :] = mm(src_buf[b % 2], start_buf[...], NN).astype(jnp.bfloat16)
+
+        @pl.when(s >= 2)
+        def _():
+            pl.semaphore_wait(free_sem, 1)
+        near_copy(s, slot).start()
+        gather(mine, s, own_buf, slot)
+
+        @pl.when(s >= 1)
+        def _():
+            near_copy(s - 1, 1 - slot).wait_recv()
+            gather(other, s - 1, near_buf, 1 - slot)
+
+        @pl.when(jnp.logical_and(s >= 1, s - 1 < steps - 2))
+        def _():
+            pl.semaphore_signal(free_sem, inc=1, device_id={'rows': near}, device_id_type=MESH)
+        return carry
+    lax.fori_loop(0, steps, step, 0)
+    final = (steps - 1) % 2
+    near_copy(steps - 1, final).wait_recv()
+    gather(other, steps - 1, near_buf, final)
+    store = pltpu.make_async_copy(acc, gain, load_sem.at[0])
+    store.start()
+    for copy in tgt_out:
+        copy.wait_recv()
+    tgt_pass.start()
+    local[3].wait_recv()
+    tgt_pass.wait_recv()
+    for slot in range(2):
+        near_copy(0, slot).wait_send()
+    for copy in local + src_out + [feat_out] + tgt_out + [src_pass, feat_pass, tgt_pass]:
+        copy.wait_send()
+    for s in range(steps):
+        for copy in start_out(s):
+            copy.wait_send()
+    store.wait()
+
+
+def first_step(src, tgt, start, feats):
+    rows, cols = src.shape
+    quad = rows // 2
+    half = cols // 2
+    steps = half // STEP
+    n_links = 18 + 2 * steps + 2
+    any_spec = pl.BlockSpec(memory_space=pl.ANY)
+    bf16 = jnp.bfloat16
+    shapes = [((rows, cols), jnp.float32), ((rows, cols), bf16), ((2, 5, quad, quad), bf16), ((half, cols), bf16),
+              ((rows, cols), bf16), ((2, 5, quad, quad), bf16), ((3,) + feats.shape, bf16),
+              ((rows, half), bf16), ((2, rows, half), bf16)]
+    return pl.pallas_call(
+        first_kernel,
+        out_shape=[jax.ShapeDtypeStruct(*s) for s in shapes],
+        in_specs=[any_spec] * 4,
+        out_specs=[any_spec] * len(shapes),
+        scratch_shapes=[
+            pltpu.VMEM((rows, cols), jnp.float32),
+            pltpu.VMEM((rows, cols), bf16),
+            pltpu.VMEM((2, SLAB, cols), bf16),
+            pltpu.VMEM((cols, STEP), bf16),
+            pltpu.VMEM((2, cols, STEP), bf16),
+            pltpu.VMEM((2, cols, STEP), bf16),
+            pltpu.VMEM((SLAB, half), bf16),
+            pltpu.VMEM((half, SLAB), bf16),
+            pltpu.VMEM((2,) + feats.shape, bf16),
+            pltpu.SemaphoreType.DMA((6,)),
+            pltpu.SemaphoreType.DMA((2,)),
+            pltpu.SemaphoreType.DMA((15,)),
+            pltpu.SemaphoreType.DMA((n_links,)),
+            pltpu.SemaphoreType.DMA((n_links,)),
+            pltpu.SemaphoreType.REGULAR,
+        ],
+        compiler_params=pltpu.CompilerParams(collective_id=2, has_side_effects=True, vmem_limit_bytes=62 * 1024 * 1024),
+        cost_estimate=pl.CostEstimate(flops=6 * rows * cols * cols, bytes_accessed=400000000, transcendentals=0),
+        name='first_step',
+    )(src, tgt, start, feats)
+
+
+def second_kernel(plan_t, src, src_near, src_far, tgt, tgt_near, tgt_blocks, feats, feat_peer, gain, tgt_far,
+                  acc, plan_keep, src_buf, made, ready, slab, turned, feat_buf,
+                  load_sem, src_sem, block_sem, send_sem, recv_sem):
+    rows, cols = src.shape
+    half = cols // 2
+    me, chip, core, near, same, cross = places()
+    links = Links(send_sem, recv_sem)
+    per = rows // SLAB
+    keep = pltpu.make_async_copy(plan_t, plan_keep, load_sem.at[0])
+    keep.start()
+    entry_barrier((near, same, cross))
+
+    def block(matrix, matrix_near, matrix_far, k, h):
+        if k == 0:
+            return matrix.at[pl.ds(h * SLAB, SLAB)]
+        if k == 1:
+            return matrix_near.at[pl.ds(h * SLAB, SLAB)]
+        which = core if k == 2 else 1 - core
+        return matrix_far.at[pl.ds(pl.multiple_of(which * rows + h * SLAB, SLAB), SLAB)]
+
+    order = [(k, h) for k in (2, 3, 1, 0) for h in range(per)]
+    devices = (me, near, same, cross)
+
+    def src_load(n):
+        k, h = order[n]
+        return pltpu.make_async_copy(block(src, src_near, src_far, k, h), src_buf.at[n % 2], src_sem.at[n % 2])
+
+    column = pl.ds(pl.multiple_of(me * rows, rows), rows)
+    copies = []
+    src_load(0).start()
+    keep.wait()
+    for n, (k, h) in enumerate(order):
+        src_load(n).wait()
+        if n + 1 < len(order):
+            src_load(n + 1).start()
+
+        def make(t, carry, n=n, k=k, h=h):
+            span = pl.ds(pl.multiple_of(t * 256, 256), 256)
+            value = mm(src_buf[n % 2], plan_keep[span, :], NT).astype(jnp.bfloat16)
+            if k == 0:
+                ready[pl.ds(h * SLAB, SLAB), pl.ds(pl.multiple_of(me * rows + t * 256, 256), 256)] = value
+            else:
+                made[n, :, span] = value
+            return carry
+        lax.fori_loop(0, rows // 256, make, 0)
+        if k:
+            copies.append(links.copy(made.at[n], ready.at[pl.ds(h * SLAB, SLAB), column], devices[k], n))
+            copies[-1].start()
+
+    def tgt_load(n):
+        k, h = turn[n]
+        return pltpu.make_async_copy(block(tgt, tgt_near, tgt_far, k, h), src_buf.at[n % 2], src_sem.at[n % 2])
+
+    depth = feats.shape[1] // 2
+    own_feat = pltpu.make_async_copy(feats, feat_buf.at[0], load_sem.at[1])
+    own_feat.start()
+    own_feat.wait()
+    for k, device in enumerate(devices):
+        source = feats if k == 0 else feat_peer.at[k - 1]
+        load = pltpu.make_async_copy(source, feat_buf.at[1], load_sem.at[1])
+        load.start()
+        load.wait()
+
+        def cross_term(h, carry, device=device):
+            value = mm(feat_buf[0, :, :depth], feat_buf[1, pl.ds(pl.multiple_of(h * 256, 256), 256), depth:], NT)
+            acc[:, pl.ds(pl.multiple_of(device * rows + h * 256, 256), 256)] = weighted(value, 2.0 * ALPHA)
+            return carry
+        lax.fori_loop(0, rows // 256, cross_term, 0)
+
+    assemble(tgt, tgt_near, tgt_blocks, tgt_far, slab, turned, block_sem, chip, core, rows)
+    turn = [(k, h) for k in (0, 1, 2, 3) for h in range(per)]
+    tgt_load(0).start()
+    for n, (k, h) in enumerate(turn):
+        tgt_load(n).wait()
+        if n + 1 < len(turn):
+            tgt_load(n + 1).start()
+        if k and h == 0:
+            for copy, (kk, hh) in zip(copies, order):
+                if kk == k:
+                    copy.wait_recv()
+        left = pl.ds(pl.multiple_of(devices[k] * rows + h * SLAB, SLAB), SLAB)
+
+        def update(t, carry, n=n, left=left):
+            span = pl.ds(pl.multiple_of(t * 256, 256), 256)
+            acc[:, span] += weighted(mm(ready[:, left], src_buf[n % 2, :, span], NN), 2.0 * (1.0 - ALPHA))
+            return carry
+        lax.fori_loop(0, cols // 256, update, 0)
+    store = pltpu.make_async_copy(acc, gain, load_sem.at[0])
+    store.start()
+    for copy in copies:
+        copy.wait_send()
+    store.wait()
+
+
+def second_step(plan_t, src, src_near, src_far, tgt, tgt_near, tgt_blocks, feats, feat_peer):
+    rows, cols = src.shape
+    half = cols // 2
+    n_copies = 3 * rows // SLAB
+    any_spec = pl.BlockSpec(memory_space=pl.ANY)
+    bf16 = jnp.bfloat16
+    gain, _ = pl.pallas_call(
+        second_kernel,
+        out_shape=[jax.ShapeDtypeStruct((rows, cols), jnp.float32), jax.ShapeDtypeStruct((half, cols), bf16)],
+        in_specs=[any_spec] * 9,
+        out_specs=[any_spec] * 2,
+        scratch_shapes=[
+            pltpu.VMEM((rows, cols), jnp.float32),
+            pltpu.VMEM((rows, cols), bf16),
+            pltpu.VMEM((2, SLAB, cols), bf16),
+            pltpu.VMEM((n_copies, SLAB, rows), bf16),
+            pltpu.VMEM((rows, cols), bf16),
+            pltpu.VMEM((SLAB, half), bf16),
+            pltpu.VMEM((half, SLAB), bf16),
+            pltpu.VMEM((2,) + feats.shape, bf16),
+            pltpu.SemaphoreType.DMA((2,)),
+            pltpu.SemaphoreType.DMA((2,)),
+            pltpu.SemaphoreType.DMA((15,)),
+            pltpu.SemaphoreType.DMA((n_copies,)),
+            pltpu.SemaphoreType.DMA((n_copies,)),
+        ],
+        compiler_params=pltpu.CompilerParams(collective_id=3, has_side_effects=True, vmem_limit_bytes=62 * 1024 * 1024),
+        cost_estimate=pl.CostEstimate(flops=4 * rows * cols * cols, bytes_accessed=200000000, transcendentals=0),
+        name='second_step',
+    )(plan_t, src, src_near, src_far, tgt, tgt_near, tgt_blocks, feats, feat_peer)
+    return gain
 
 
 def solution(mesh):
     group = mesh.shape['rows']
 
     def local_fgw(cost_src, cost_tgt, plan_init, mass_src, mass_tgt, feat_src, feat_tgt, epsilon):
-        rows, cols = cost_src.shape
-        half = cols // 2
-        quad = rows // 2
+        rows = cost_src.shape[0]
         me = lax.axis_index('rows')
-        chip, core = me // 2, me % 2
-        even = core == 0
-        dot = functools.partial(jnp.einsum, preferred_element_type=jnp.float32)
-        wire = Wire()
-
-        def ordered(mine, other, axis=0):
-            return jnp.where(even, jnp.concatenate([mine, other], axis), jnp.concatenate([other, mine], axis))
-
-        def chip_order(mine, other, axis):
-            return jnp.where(chip == 0, jnp.concatenate([mine, other], axis), jnp.concatenate([other, mine], axis))
-
-        def pack(cost):
-            diag = lax.dynamic_slice(cost, (0, rows * me), (rows, rows))
-            off = lax.dynamic_slice(cost, (0, rows * (me + 1 - 2 * core)), (rows, rows))
-            edge = jnp.where(even, off[:quad, :], off[:, quad:].T)
-            return jnp.concatenate([diag[:quad, :quad], diag[:quad, quad:], diag[quad:, quad:],
-                                    edge[:, :quad], edge[:, quad:]], axis=0)
-
-        def assemble(cost, packed):
-            near = ordered(cost, swap(cost, 1))
-            packed_pair = swap(packed, 1)
-            packs = [jnp.where(even, packed, packed_pair), jnp.where(even, packed_pair, packed)]
-            diags, edges = [], []
-            for item in packs:
-                p = [item[k * quad:(k + 1) * quad] for k in range(5)]
-                diags.append(jnp.block([[p[0], p[1]], [p[1].T, p[2]]]))
-                edges.append(jnp.concatenate([p[3], p[4]], axis=1))
-            edge = jnp.concatenate(edges, axis=0)
-            far = jnp.block([[diags[0], edge], [edge.T, diags[1]]])
-            turned = lax.dynamic_slice(near, (0, half * (1 - chip)), (half, half)).T
-            return jnp.concatenate([near, chip_order(turned, far, 1)], axis=0)
-
         src_half = cost_src.astype(jnp.bfloat16)
         tgt_half = cost_tgt.astype(jnp.bfloat16)
+        start = plan_init.astype(jnp.bfloat16)
         feats = jnp.concatenate([feat_src, feat_tgt], axis=1).astype(jnp.bfloat16)
-        start = plan_init.astype(jnp.bfloat16)
-        depth = feat_src.shape[1]
-
-        src_wire = wire.send(pack(src_half), 2)
-        feat_wire = wire.send(feats, 2)
-        start_mine = lax.dynamic_slice(start, (0, half * core), (rows, half))
-        start_other = lax.dynamic_slice(start, (0, half * (1 - core)), (rows, half))
-        spans, at = [], 0
-        for w in STEP_WIDTHS:
-            spans.append((at, at + w))
-            at += w
-        plan_wires = []
-        for lo, hi in spans:
-            plan_wires.append((wire.send(start_mine[:, lo:hi], 2), wire.send(start_other[:, lo:hi], 3)))
-        tgt_wire = wire.send(pack(tgt_half), 2)
-
-        src_all = assemble(src_half, wire.get(src_wire))
-        feat_near = ordered(feats, swap(feats, 1))
-        feat_far = ordered(wire.get(feat_wire), swap(wire.get(feat_wire), 1))
-        feat_all = chip_order(feat_near, feat_far, 0)
-        start_pair = swap(start_other, 1)
-        tgt_mine = lax.dynamic_slice(tgt_half, (0, half * core), (rows, half))
-        tgt_other = lax.dynamic_slice(tgt_half, (0, half * (1 - core)), (rows, half))
         mass_all = lax.all_gather(mass_src, 'rows', tiled=True)
         mass_cols = lax.dynamic_slice(mass_tgt, (rows * me,), (rows,))
-
-        gain = (2.0 * ALPHA) * dot('jd,id->ji', feats[:, depth:], feat_all[:, :depth])
-        for (lo, hi), (same, cross) in zip(spans, plan_wires):
-            near = ordered(start_mine[:, lo:hi], start_pair[:, lo:hi])
-            far = ordered(wire.get(same), wire.get(cross))
-            prod_a = dot('kj,ki->ji', jnp.concatenate([near, far], axis=0), src_all).astype(jnp.bfloat16)
-            both_a = jnp.concatenate([prod_a, swap(prod_a, 1)], axis=0)
-            both_c = jnp.concatenate([tgt_mine[:, lo:hi], tgt_other[:, lo:hi]], axis=1)
-            gain = gain + (2.0 * (1.0 - ALPHA)) * dot('rj,ji->ri', both_c, both_a)
+        gain, src_near, _, src_far, tgt_near, tgt_blocks, feat_peer, _, _ = first_step(src_half, tgt_half, start, feats)
         plan_t = sinkhorn(group, [gain], mass_cols, mass_all, epsilon, jnp.bfloat16, True, 0)
-
-        tgt_all = assemble(tgt_half, wire.get(tgt_wire))
-        part = rows // ROW_PARTS
-        src_parts = src_all.reshape(4, ROW_PARTS, part, cols)
-        arrived = []
-        for h in range(ROW_PARTS):
-            blocks = [dot('ik,jk->ij', src_parts[2 + k, h], plan_t).astype(jnp.bfloat16) for k in range(2)]
-            arrived.append((wire.send(jnp.where(even, blocks[0], blocks[1]), 2),
-                            wire.send(jnp.where(even, blocks[1], blocks[0]), 3)))
-        near_blocks = [dot('ik,jk->ij', src_all[k * rows:(k + 1) * rows], plan_t).astype(jnp.bfloat16) for k in range(2)]
-        near_mine = jnp.where(even, near_blocks[0], near_blocks[1])
-        near_pair = swap(jnp.where(even, near_blocks[1], near_blocks[0]), 1)
-        near = ordered(near_mine, near_pair, 1)
-        gains = []
-        for h in range(ROW_PARTS):
-            span = slice(h * part, (h + 1) * part)
-            far = ordered(wire.get(arrived[h][0]), wire.get(arrived[h][1]), 1)
-            prod_b = dot('ij,jl->il', jnp.concatenate([near[span], far], axis=1), tgt_all)
-            cross = dot('id,jd->ij', feats[span, :depth], feat_all[:, depth:])
-            gains.append((2.0 * ALPHA) * cross + (2.0 * (1.0 - ALPHA)) * prod_b)
-        return sinkhorn(group, gains, mass_src, mass_tgt, epsilon, jnp.float32, False, 1)
+        gain = second_step(plan_t, src_half, src_near, src_far, tgt_half, tgt_near, tgt_blocks, feats, feat_peer)
+        return sinkhorn(group, [gain], mass_src, mass_tgt, epsilon, jnp.float32, False, 1)
 
     row_spec = P(('pairs', 'rows'), None)
     vec_spec = P(('pairs', 'rows'))

time: 1230 us -> 647 us (0.53)
  Pallas kernels: 121 us -> 598 us
  matrix products: 347 us -> 0 us
  other arithmetic: 362 us -> 19.6 us
  local copies, waits for them, and re-layouts: 202 us -> 19.1 us
  waiting for transfers between devices: 122 us -> 0 us
  blocking collectives: 39.6 us -> 8 us
  starting transfers between devices: 23 us -> 0 us
    pallas_call x0 -> x2, Pallas kernels: none -> 477 us  [the longest x1 334 us: first_step(): pl.pallas_call(first_kernel, out_shape=[jax.ShapeDtypeStruct(*s) for s in...]
    dot_general x29 -> x0, matrix products: 347 us -> none  [the longest x5 103 us: local_fgw(): dot('kj,ki->ji', jnp.concatenate([near, far], axis=0), src_all)]
    select_n x26 -> x0, other arithmetic: 255 us -> none  [the longest x3 166 us: chip_order(): jnp.where(chip == 0, jnp.concatenate([mine, other], axis), jnp.concatenat...]
    ppermute x34 -> x0, waiting for transfers between devices: 122 us -> none  [swap(): return lax.ppermute(value, 'rows', [(i, i ^ distance) for i in range(4)])]
    concatenate x5 -> x0, other arithmetic: 81.6 us -> none  [the longest x1 36.4 us: assemble(): far = jnp.block([[diags[0], edge], [edge.T, diags[1]]])]
    concatenate x3 -> x0, local copies, waits for them, and re-layouts: 75.2 us -> none  [the longest x1 40.4 us: assemble(): return jnp.concatenate([near, chip_order(turned, far, 1)], axis=0)]
    slice x18 -> x0, local copies, waits for them, and re-layouts: 34.9 us -> none  [the longest x3 8.67 us: local_fgw(): near = ordered(start_mine[:, lo:hi], start_pair[:, lo:hi])]
    transpose x8 -> x0, local copies, waits for them, and re-layouts: 34.7 us -> none  [the longest x2 20.7 us: assemble(): turned = lax.dynamic_slice(near, (0, half * (1 - chip)), (half, half)).T]
  transfers between devices with their start and end apart: 34 -> 0, of which waited for: 11 -> 0; matrix products, arithmetic and copies ran while one was open for 66% -> 0% of each run, Pallas kernels for 0% -> 0%
where the time goes in v3:
time: 647 us; the launch traced here: 646 us
  Pallas kernels  598 us (92%)
  other arithmetic  19.6 us (3%)
  local copies, waits for them, and re-layouts  19.1 us (3%)
  blocking collectives  8 us (1%)
    pallas_call x1, Pallas kernels, first_step(): pl.pallas_call(first_kernel, out_shape=[jax.ShapeDtypeStruct(*s) for s in...  334 us
    pallas_call x1, Pallas kernels, second_step(): pl.pallas_call(second_kernel, out_shape=[jax.ShapeDtypeStruct((rows, cols...  144 us
    pallas_call x2, Pallas kernels, sinkhorn(): pl.pallas_call(functools.partial(sinkhorn_kernel, group, len(gains), tran...  121 us
    unnamed x19, local copies, waits for them, and re-layouts  18.7 us

profile of v3, /device:TPU:0, one launch (start us, length us, event | category | flops | bytes accessed | tf_op | source)
XLA Modules:
  0.0 645.7 jit_solution(3138169405154812403)
XLA Ops:
  0.0 0.0 copy-start.1
  0.0 0.0 slice-start
  0.0 0.0 slice-start.1
  0.0 9.9 %convert_element_type.10.src = bf16[1024,4096]{1,0:T(8,128)(2,1)} convert(f32[1024,4096]{1,0:T(8,128)} %param.8) | non-fusion elementwise | flops 4194304 | bytes 25165824 | tf_op jit(solution)/shard_map/convert_element_type | solution.py:688
  9.9 3.7 copy-done.1
  13.6 0.0 copy-start.2
  13.6 0.0 copy-start.3
  13.6 0.0 slice-start.2
  13.6 0.0 slice-start.3
  13.6 4.4 convert_element_type.11.tgt
  18.1 0.0 copy-done.2
  18.1 0.1 convert.6
  18.1 0.9 copy-done.3
  19.0 0.1 convert.7
  19.0 1.1 pad_maximum_fusion.feats
  20.2 0.0 slice-done
  20.2 0.0 slice-done.1
  20.2 1.2 slice-done.2
  21.4 1.2 slice-done.3
  22.6 4.0 convert_element_type.12.start
  26.6 0.0 copy-start
  26.6 0.0 copy-start.4
  26.6 333.6 %first_step.1 = (f32[1024,4096]{1,0:T(8,128)}, bf16[1024,4096]{1,0:T(8,128)(2,1)}, bf16[2,5,512,512]{3,2,1,0:T(8,128)(2,1)}, bf16[2048,4096]{1,0:T(8,128)(2,1)},...) custom-call(bf16[1024,4096]{1,0:T(8,128)(2,1)} %convert_element_type, ...), custom_call_target="tpu_custom_call" | custom-call | flops 103079215104 | bytes 400000000 | tf_op jit(solution)/shard_map/first_step/pallas_call | solution.py:527
  360.2 0.0 copy-done
  360.2 0.2 broadcast_in_dim.4.refs_1_
  361.0 0.0 copy-done.4
  361.0 8.0 %all_gather.3 = f32[4096]{0:T(1024)S(1)} all-gather(f32[1024]{0:T(1024)S(1)} %copy-done.4), channel_id=1, replica_groups=mesh['pairs'=2,'rows'=4] {'rows'}, dimensions={0}, use_global_device_ids=true | all-gather | bytes 20480 | tf_op jit(solution)/shard_map/all_gather | solution.py:692
  369.0 59.8 %sinkhorn_cols.1.plan_t = bf16[1024,4096]{1,0:T(8,128)(2,1)} custom-call(f32[1024,4096]{1,0:T(8,128)} %get-tuple-element.12.refs_0_, f32[1024,128]{1,0:T(8,128)S(1)} %broadcast_in_dim.4.refs_1_, f32[4,8,128]{2,1,0:T(8,128)S(1)} %bitcast.5, f32[1]{0:T(128)} %bitcast.3.refs_3_), custom_call_target="tpu_custom_call" | custom-call | flops 167772160 | bytes 33554432 | tf_op jit(solution)/shard_map/sinkhorn_cols/pallas_call | solution.py:223
  428.8 143.7 %second_step.1 = (f32[1024,4096]{1,0:T(8,128)}, bf16[2048,4096]{1,0:T(8,128)(2,1)}) custom-call(bf16[1024,4096]{1,0:T(8,128)(2,1)} %sinkhorn_cols.1.plan_t, bf16[1024,4096]{1,0:T(8,128)(2,1)} %convert_element_type.10.src, bf16[1024,4096]{1,0:T(8,128)(2,1)} %get-tuple-element.13.src_near, bf16[2048,4096]{1,0:T(8,128)(2,1)} %get-tuple-element.14.src_far, ...), custom_call_target="tpu_custom_call" | custom-call | flops 68719476736 | bytes 200000000 | tf_op jit(solution)/shard_map/second_step/pallas_call | solution.py:655
  572.5 0.2 broadcast_in_dim.5.refs_1_
  572.7 61.3 %sinkhorn_rows.1 = f32[1024,4096]{1,0:T(8,128)} custom-call(f32[1024,4096]{1,0:T(8,128)} %get-tuple-element.18.refs_0_, f32[1024,128]{1,0:T(8,128)S(1)} %broadcast_in_dim.5.refs_1_, f32[4,8,128]{2,1,0:T(8,128)S(1)} %bitcast.6, f32[1]{0:T(128)} %bitcast.4.refs_3_), custom_call_target="tpu_custom_call" | custom-call | flops 167772160 | bytes 33554432 | tf_op jit(solution)/shard_map/sinkhorn_rows/pallas_call | solution.py:223
  634.0 11.7 %copy.11 = f32[1024,4096]{1,0:T(8,128)} copy(f32[1024,4096]{1,0:T(8,128)} %sinkhorn_rows.1) | data formatting | bytes 33554432
  (2 shorter events, 0.0 us)
Async XLA Ops:
  0.0 13.6 %copy-start.1 = (f32[1024,4096]{1,0:T(8,128)S(1)}, f32[1024,4096]{1,0:T(8,128)}, u32[]{:S(2)}) copy-start(f32[1024,4096]{1,0:T(8,128)} %param.9) | copy-start | bytes 50331652
  0.0 20.2 %slice-start = ((s8[16777216]{0:T(1024)(128)(4,1)}), s8[4194304]{0:T(1024)(128)(4,1)S(1)}, s32[]{:S(2)}) async-start(s8[16777216]{0:T(1024)(128)(4,1)} %bitcast.7), calls=%async_computation | async-start | bytes 8388608
  0.0 20.2 %slice-start.1 = ((s8[16777216]{0:T(1024)(128)(4,1)}), s8[4194304]{0:T(1024)(128)(4,1)S(1)}, s32[]{:S(2)}) async-start(s8[16777216]{0:T(1024)(128)(4,1)} %bitcast.7), calls=%async_computation.1 | async-start | bytes 8388608
  13.6 4.4 copy-start.2
  13.6 5.3 copy-start.3
  13.6 7.7 %slice-start.2 = ((s8[16777216]{0:T(1024)(128)(4,1)}), s8[4194304]{0:T(1024)(128)(4,1)S(1)}, s32[]{:S(2)}) async-start(s8[16777216]{0:T(1024)(128)(4,1)} %bitcast.7), calls=%async_computation.2 | async-start | bytes 8388608
  13.6 8.9 %slice-start.3 = ((s8[16777216]{0:T(1024)(128)(4,1)}), s8[4194304]{0:T(1024)(128)(4,1)S(1)}, s32[]{:S(2)}) async-start(s8[16777216]{0:T(1024)(128)(4,1)} %bitcast.7), calls=%async_computation.3 | async-start | bytes 8388608
  26.6 333.6 %copy-start = (f32[4096]{0:T(1024)S(1)}, f32[4096]{0:T(1024)}, u32[]{:S(2)}) copy-start(f32[4096]{0:T(1024)} %param.12) | copy-start | bytes 49156
  26.6 334.5 %copy-start.4 = (f32[1024]{0:T(1024)S(1)}, f32[1024]{0:T(1024)}, u32[]{:S(2)}) copy-start(f32[1024]{0:T(1024)} %param.11) | copy-start | bytes 12292

commit v4 on v0

v4 whole, which is shorter than its diff:
```python
import functools

import jax
import jax.numpy as jnp
from jax import lax
from jax.experimental import pallas as pl
from jax.experimental.pallas import tpu as pltpu
from jax.sharding import PartitionSpec as P

ALPHA = 0.5
SWEEPS = 10
LANES = 128
CHUNKS = 4
BLOCK = 64
STEP = 256
SLAB = 512
TILE = 512
EARLY_STEPS = 1
TAIL_PIECES = 4
GROUP = 4
MESH = pl.DeviceIdType.MESH
NT = (((1,), (1,)), ((), ()))
NN = (((1,), (0,)), ((), ()))
BF16 = jnp.bfloat16
F32 = jnp.float32


def weighted(value, factor):
    return value if factor == 1.0 else value * factor


def mm(left, right, dims):
    return lax.dot_general(left, right, dims, preferred_element_type=F32)


def split(val):
    return val.reshape(val.shape[0] // 8, 8, LANES)


def aligned(start, size):
    return pl.ds(pl.multiple_of(start, size), size)


def assemble(cost, cost_near, blocks, far, slab, turned, sems, chip, core, rows):
    quad = rows // 2
    half = 2 * rows
    away = half * (1 - chip)
    for source, owner in ((cost, core), (cost_near, 1 - core)):
        for a in range(rows // SLAB):
            load = pltpu.make_async_copy(source.at[pl.ds(a * SLAB, SLAB), aligned(away, half)], slab, sems.at[0])
            load.start()
            load.wait()

            def turn(b, carry):
                turned[aligned(b * SLAB, SLAB), :] = slab[:, aligned(b * SLAB, SLAB)].T
                return carry
            lax.fori_loop(0, half // SLAB, turn, 0)
            store = pltpu.make_async_copy(turned, far.at[:, aligned(half * chip + owner * rows + a * SLAB, SLAB)], sems.at[1])
            store.start()
            store.wait()

    def corner(k, carry):
        cc = core + k - 2 * core * k
        base, other = cc * rows, (1 - cc) * rows
        spots = [(base, base), (base, base + quad), (base + quad, base + quad),
                 (base, other + quad * cc), (base + quad * cc, other + quad)]
        loads = [pltpu.make_async_copy(blocks.at[k, b], slab.at[:, pl.ds(b * quad, quad)] if b < 4 else
                                       turned.at[pl.ds(3 * quad, quad), :], sems.at[2 + b]) for b in range(5)]
        for load in loads:
            load.start()
        for load in loads:
            load.wait()
        turned[pl.ds(0, quad), :] = slab[:, quad:2 * quad].T
        turned[pl.ds(quad, quad), :] = slab[:, 3 * quad:4 * quad].T
        turned[pl.ds(2 * quad, quad), :] = turned[pl.ds(3 * quad, quad), :].T
        stores = []

        def put(source, row, col):
            target = far.at[aligned(row, quad), aligned(away + col, quad)]
            stores.append(pltpu.make_async_copy(source, target, sems.at[7 + len(stores)]))
            stores[-1].start()
        for b in range(4):
            put(slab.at[:, pl.ds(b * quad, quad)], *spots[b])
        put(turned.at[pl.ds(3 * quad, quad), :], *spots[4])
        for t, b in enumerate((1, 3, 4)):
            put(turned.at[pl.ds(t * quad, quad), :], spots[b][1], spots[b][0])
        for store in stores:
            store.wait()
        return carry
    lax.fori_loop(0, 2, corner, 0)


def kernel(src_f32, tgt_f32, start, feat_src, feat_tgt, mass_mine, mass_rows_t, mass_rows, mass_cols, epsilon,
           kern_out, row_out, col_out, src, tgt, src_near, src_blocks, src_far, tgt_near, tgt_blocks, tgt_far,
           src_feat_peer, tgt_feat_peer, start_near, start_far, ready,
           acc, keep, src_buf, start_buf, own_buf, near_buf, made, left_buf, slab, turned, feat_buf, mass_all,
           row_scale, row_acc, col_scale, shift_fix, part_sum, peer_sum, part_top, peer_top,
           load_sem, src_sem, block_sem, send_sem, recv_sem, sum_send, sum_recv, top_send, top_recv, free_sem):
    rows, cols = src_f32.shape
    half = cols // 2
    quad = rows // 2
    steps = half // STEP
    per = rows // SLAB
    tiles = cols // LANES // CHUNKS
    width = cols // CHUNKS
    me = lax.axis_index('rows')
    chip, core = me // 2, me % 2
    near, same, cross = chip * 2 + (1 - core), (1 - chip) * 2 + core, (1 - chip) * 2 + (1 - core)
    peers = (near, same, cross)
    devices = (me, near, same, cross)
    inv_eps = 1.0 / epsilon[0]

    src_load_all = [pltpu.make_async_copy(src_f32.at[pl.ds(b * quad, quad)], acc.at[pl.ds(b * quad, quad)], load_sem.at[b])
                    for b in range(2)]
    for load in src_load_all:
        load.start()
    mass_all[me] = mass_mine[...]
    barrier = pltpu.get_barrier_semaphore()
    for peer in peers:
        pl.semaphore_signal(barrier, inc=1, device_id={'rows': peer}, device_id_type=MESH)
    pl.semaphore_wait(barrier, GROUP - 1)

    counter = [0]

    def reserve(count):
        counter[0] += count
        return counter[0] - count

    def remote(source, target, peer, index):
        return pltpu.make_async_remote_copy(src_ref=source, dst_ref=target, send_sem=send_sem.at[index],
                                            recv_sem=recv_sem.at[index], device_id={'rows': peer}, device_id_type=MESH)

    def col_span(base, s):
        return aligned(base + s * STEP, STEP)

    def block_spots():
        diag, off = me * rows, (me + 1 - 2 * core) * rows
        return [(0, diag), (0, diag + quad), (quad, diag + quad), (0, off + quad * core), (quad * core, off + quad)]

    mine, other = half * core, half * (1 - core)
    src_near_out = remote(src, src_near, near, reserve(1))
    src_feat_near = remote(feat_src, src_feat_peer.at[0], near, reserve(1))
    start_near_out = remote(start.at[:, aligned(other, half)], start_near, near, reserve(1))
    tgt_near_out = remote(tgt, tgt_near, near, reserve(1))
    tgt_feat_near = remote(feat_tgt, tgt_feat_peer.at[0], near, reserve(1))
    src_out = [remote(src.at[aligned(row, quad), aligned(col, quad)], src_blocks.at[0, b], same, reserve(1))
               for b, (row, col) in enumerate(block_spots())]
    src_feat_out = remote(feat_src, src_feat_peer.at[1], same, reserve(1))
    tgt_feat_out = remote(feat_tgt, tgt_feat_peer.at[1], same, reserve(1))
    piece = quad // 2
    tgt_out = [remote(tgt.at[aligned(row + h * piece, piece), aligned(col, quad)],
                      tgt_blocks.at[0, b, pl.ds(h * piece, piece)], same, reserve(1))
               for b, (row, col) in enumerate(block_spots()) for h in range(2)]
    src_pass = remote(src_blocks.at[0], src_blocks.at[1], near, reserve(1))
    src_feat_pass = remote(src_feat_peer.at[1], src_feat_peer.at[2], near, reserve(1))
    tgt_pass = remote(tgt_blocks.at[0], tgt_blocks.at[1], near, reserve(1))
    tgt_feat_pass = remote(tgt_feat_peer.at[1], tgt_feat_peer.at[2], near, reserve(1))
    mass_out = [remote(mass_mine, mass_all.at[me], peer, reserve(1)) for peer in peers]
    start_base = reserve(2 * steps)
    near_base = reserve(2)
    late_pieces = tgt_out[TAIL_PIECES:] + [tgt_feat_out]

    def start_out(s):
        return [remote(start.at[:, col_span(mine, s)], start_far.at[0, :, col_span(0, s)], same, start_base + s),
                remote(start.at[:, col_span(other, s)], start_far.at[1, :, col_span(0, s)], cross, start_base + steps + s)]

    def near_copy(slot):
        return remote(own_buf.at[slot], near_buf.at[slot], near, near_base + slot)

    for s in range(EARLY_STEPS):
        for copy in start_out(s):
            copy.start()
    for copy in [start_near_out, src_feat_near, tgt_feat_near] + mass_out:
        copy.start()

    src_stores = []
    for b in range(2):
        src_load_all[b].wait()

        def cast(t, carry, b=b):
            span = aligned(t * BLOCK, BLOCK)
            src_buf[b, span, :] = acc[aligned(b * quad + t * BLOCK, BLOCK), :].astype(BF16)
            return carry
        lax.fori_loop(0, quad // BLOCK, cast, 0)
        src_stores.append(pltpu.make_async_copy(src_buf.at[b], src.at[pl.ds(b * quad, quad)], src_sem.at[b]))
        src_stores[-1].start()
    tgt_load_all = pltpu.make_async_copy(tgt_f32, acc, load_sem.at[0])
    tgt_load_all.start()
    for store in src_stores:
        store.wait()
    for copy in src_out + [src_near_out, src_feat_out]:
        copy.start()
    for s in range(EARLY_STEPS, steps):
        for copy in start_out(s):
            copy.start()
    tgt_load_all.wait()

    def cast_tgt(t, carry):
        span = aligned(t * BLOCK, BLOCK)
        keep[span, :] = acc[span, :].astype(BF16)
        return carry
    lax.fori_loop(0, rows // BLOCK, cast_tgt, 0)
    tgt_store = pltpu.make_async_copy(keep, tgt, load_sem.at[0])
    tgt_store.start()
    tgt_store.wait()
    tgt_near_out.start()
    for copy in tgt_out[:TAIL_PIECES]:
        copy.start()

    def cross_terms(first, peer_second):
        own = pltpu.make_async_copy(first, feat_buf.at[0], load_sem.at[1])
        own.start()
        own.wait()
        for k, device in enumerate(devices):
            load = pltpu.make_async_copy(peer_second(k), feat_buf.at[1], load_sem.at[1])
            load.start()
            load.wait()

            def cross_term(h, carry, device=device):
                block = mm(feat_buf[0], feat_buf[1, aligned(h * 256, 256), :], NT)
                acc[:, aligned(device * rows + h * 256, 256)] = weighted(block, 2.0 * ALPHA)
                return carry
            lax.fori_loop(0, rows // 256, cross_term, 0)

    src_feat_near.wait_recv()
    for copy in src_out:
        copy.wait_recv()
    src_pass.start()
    src_feat_out.wait_recv()
    src_feat_pass.start()
    src_near_out.wait_recv()
    src_pass.wait_recv()
    assemble(src, src_near, src_blocks, src_far, slab, turned, block_sem, chip, core, rows)
    src_feat_pass.wait_recv()
    cross_terms(feat_tgt, lambda k: feat_src if k == 0 else src_feat_peer.at[k - 1])

    def rows_of(matrix, matrix_near, matrix_far, k, h):
        if k == 0:
            return matrix.at[pl.ds(h * SLAB, SLAB)]
        if k == 1:
            return matrix_near.at[pl.ds(h * SLAB, SLAB)]
        which = core if k == 2 else 1 - core
        return matrix_far.at[aligned(which * rows + h * SLAB, SLAB)]

    ordered = [(k, h) for k in range(GROUP) for h in range(per)]

    def src_load(b):
        return pltpu.make_async_copy(rows_of(src, src_near, src_far, *ordered[b]), src_buf.at[b % 2], src_sem.at[b % 2])

    def gather(base, s, right, slot):
        def update(h, carry):
            span = aligned(h * TILE, TILE)
            block = mm(keep[:, col_span(base, s)], right[slot, span, :], NT)
            acc[:, span] += weighted(block, 2.0 * (1.0 - ALPHA))
            return carry
        lax.fori_loop(0, cols // TILE, update, 0)

    start_near_out.wait_recv()
    src_load(0).start()

    def step(s, carry):
        slot = lax.rem(s, 2)
        for copy in start_out(s):
            copy.wait_recv()
        loads = []
        for k, device in enumerate(devices):
            source = (start.at[:, col_span(mine, s)] if k == 0 else start_near.at[:, col_span(0, s)] if k == 1
                      else start_far.at[k - 2, :, col_span(0, s)])
            loads.append(pltpu.make_async_copy(source, start_buf.at[aligned(device * rows, rows)], load_sem.at[2 + k]))
        for load in loads:
            load.start()

        @pl.when(s >= 2)
        def _():
            near_copy(slot).wait_send()
        for load in loads:
            load.wait()
        for b, (k, h) in enumerate(ordered):
            src_load(b).wait()
            if b + 1 < len(ordered):
                src_load(b + 1).start()
            else:
                @pl.when(s + 1 < steps)
                def _():
                    src_load(0).start()
            own_buf[slot, aligned(devices[k] * rows + h * SLAB, SLAB), :] = mm(src_buf[b % 2], start_buf[...], NN).astype(BF16)

        @pl.when(s >= 2)
        def _():
            pl.semaphore_wait(free_sem, 1)
        near_copy(slot).start()
        gather(mine, s, own_buf, slot)

        @pl.when(s >= 1)
        def _():
            near_copy(1 - slot).wait_recv()
            gather(other, s - 1, near_buf, 1 - slot)

        @pl.when(jnp.logical_and(s >= 1, s - 1 < steps - 2))
        def _():
            pl.semaphore_signal(free_sem, inc=1, device_id={'rows': near}, device_id_type=MESH)
        return carry
    lax.fori_loop(0, steps, step, 0)
    final = (steps - 1) % 2
    near_copy(final).wait_recv()
    gather(other, steps - 1, near_buf, final)

    def tile(j, t):
        begin = j * width + t * LANES
        return slice(begin, begin + LANES)

    def sweeps(phase, transposed, mass_row, mass_col, extra):
        def sends(slot, j):
            return [pltpu.make_async_remote_copy(
                src_ref=part_sum.at[phase, slot, j], dst_ref=peer_sum.at[phase, slot, k, j],
                send_sem=sum_send.at[phase, slot, k, j], recv_sem=sum_recv.at[phase, slot, k, j],
                device_id={'rows': peers[k]}, device_id_type=MESH) for k in range(GROUP - 1)]

        def top_sends(j):
            return [pltpu.make_async_remote_copy(
                src_ref=part_top.at[j], dst_ref=peer_top.at[k, j], send_sem=top_send.at[k, j],
                recv_sem=top_recv.at[k, j], device_id={'rows': peers[k]}, device_id_type=MESH) for k in range(GROUP - 1)]

        def row_update():
            for h in range(0, rows, 256):
                span = slice(h, h + 256)
                row_scale[span, :] = mass_row[span, :] / jnp.sum(row_acc[span, :], axis=1, keepdims=True)

        def col_pass(slot, j):
            def body(i, sums):
                span = pl.ds(i * BLOCK, BLOCK)
                scale = split(row_scale[span, :])
                return tuple(sums[t] + jnp.sum(split(acc[span, tile(j, t)]) * scale, axis=0) for t in range(tiles))
            sums = lax.fori_loop(0, rows // BLOCK, body, tuple(jnp.zeros((8, LANES), F32) for _ in range(tiles)))
            total = jnp.concatenate([jnp.sum(s, axis=0, keepdims=True) for s in sums], axis=0)
            if transposed:
                total = total * shift_fix[j]
            part_sum[phase, slot, j] = total
            for send in sends(slot, j):
                send.start()

        def col_update(slot, j):
            for send in sends(slot, j):
                send.wait()
            total = part_sum[phase, slot, j]
            for k in range(GROUP - 1):
                total = total + peer_sum[phase, slot, k, j]
            scale = mass_col[j] / total
            if transposed:
                scale = scale * shift_fix[j]
            col_scale[j] = scale

        def scale_rows(j):
            return [jnp.broadcast_to(col_scale[j, t:t + 1, :], (8, LANES)) for t in range(tiles)]

        def row_pass(j):
            scale = scale_rows(j)

            def body(i, carry):
                span = pl.ds(i * BLOCK, BLOCK)
                total = None if j == 0 else split(row_acc[span, :])
                for t in range(tiles):
                    term = split(acc[span, tile(j, t)]) * scale[t][None]
                    total = term if total is None else total + term
                row_acc[span, :] = total.reshape(BLOCK, LANES)
                return carry
            lax.fori_loop(0, rows // BLOCK, body, 0)

        if transposed:
            for j in range(CHUNKS):
                def top_block(i, tops, j=j):
                    span = pl.ds(i * BLOCK, BLOCK)
                    return tuple(jnp.maximum(tops[t], jnp.max(split(acc[span, tile(j, t)]), axis=0)) for t in range(tiles))
                tops = lax.fori_loop(0, rows // BLOCK, top_block, tuple(acc[0:8, tile(j, t)] for t in range(tiles)))
                tops = [jnp.max(top, axis=0, keepdims=True) for top in tops]
                wide = [jnp.broadcast_to(top, (8, LANES)) for top in tops]

                def exp_block(i, sums, j=j, wide=wide):
                    span = pl.ds(i * BLOCK, BLOCK)
                    out = []
                    for t in range(tiles):
                        val = jnp.exp((split(acc[span, tile(j, t)]) - wide[t][None]) * inv_eps)
                        acc[span, tile(j, t)] = val.reshape(BLOCK, LANES)
                        out.append(sums[t] + jnp.sum(val, axis=0))
                    return tuple(out)
                sums = lax.fori_loop(0, rows // BLOCK, exp_block, tuple(jnp.zeros((8, LANES), F32) for _ in range(tiles)))
                part_top[j, 0] = jnp.concatenate(tops, axis=0)
                part_top[j, 1] = jnp.concatenate([jnp.sum(s, axis=0, keepdims=True) for s in sums], axis=0)
                for send in top_sends(j):
                    send.start()
            for j in range(CHUNKS):
                for send in top_sends(j):
                    send.wait()
                top = part_top[j, 0]
                for k in range(GROUP - 1):
                    top = jnp.maximum(top, peer_top[k, j, 0])
                fix = jnp.exp((part_top[j, 0] - top) * inv_eps)
                total = part_top[j, 1] * fix
                for k in range(GROUP - 1):
                    total = total + peer_top[k, j, 1] * jnp.exp((peer_top[k, j, 0] - top) * inv_eps)
                shift_fix[j] = fix
                col_scale[j] = mass_col[j] / total * fix
                row_pass(j)
        else:
            def exp_rows(i, carry):
                span = pl.ds(i * BLOCK, BLOCK)
                top = acc[span, 0:LANES]
                for t in range(1, cols // LANES):
                    top = jnp.maximum(top, acc[span, t * LANES:(t + 1) * LANES])
                top = jnp.max(top, axis=1, keepdims=True)
                total = jnp.zeros((BLOCK, LANES), F32)
                for t in range(cols // LANES):
                    val = jnp.exp((acc[span, t * LANES:(t + 1) * LANES] - top) * inv_eps)
                    acc[span, t * LANES:(t + 1) * LANES] = val
                    total = total + val
                row_acc[span, :] = total
                return carry
            lax.fori_loop(0, rows // BLOCK, exp_rows, 0)
        row_update()

        def sweep(n, carry):
            slot = lax.rem(n, 2)
            for j in range(CHUNKS):
                col_pass(slot, j)
            extra(n)
            for j in range(CHUNKS):
                col_update(slot, j)
                row_pass(j)
            row_update()
            return carry
        if not transposed:
            extra(0)
        lax.fori_loop(0, SWEEPS - 1, sweep, 0)
        if transposed:
            for j in range(CHUNKS):
                scale = scale_rows(j)

                def plan_block(i, carry, j=j, scale=scale):
                    span = pl.ds(i * BLOCK, BLOCK)
                    left = split(row_scale[span, :])
                    for t in range(tiles):
                        val = left * split(acc[span, tile(j, t)]) * scale[t][None]
                        keep[span, tile(j, t)] = val.reshape(BLOCK, LANES).astype(BF16)
                    return carry
                lax.fori_loop(0, rows // BLOCK, plan_block, 0)
        else:
            for j in range(CHUNKS):
                col_pass((SWEEPS - 1) % 2, j)
            for j in range(CHUNKS):
                col_update((SWEEPS - 1) % 2, j)

    def late(n):
        for index, copy in enumerate(late_pieces):
            pl.when(n == index)(copy.start)

    for copy in mass_out:
        copy.wait_recv()
    sweeps(0, True, mass_rows_t, mass_all, late)

    order = [(k, h) for k in (2, 3, 1, 0) for h in range(per)]

    def src_again(n):
        return pltpu.make_async_copy(rows_of(src, src_near, src_far, *order[n]), src_buf.at[n % 2], src_sem.at[n % 2])

    column = aligned(me * rows, rows)
    a_copies, own_stores = [], []
    src_again(0).start()
    for n, (k, h) in enumerate(order):
        src_again(n).wait()
        if n + 1 < len(order):
            src_again(n + 1).start()

        def make(t, carry, n=n):
            span = aligned(t * 256, 256)
            made[n, :, span] = mm(src_buf[n % 2], keep[span, :], NT).astype(BF16)
            return carry
        lax.fori_loop(0, rows // 256, make, 0)
        target = ready.at[pl.ds(h * SLAB, SLAB), column]
        if k:
            a_copies.append(remote(made.at[n], target, devices[k], reserve(1)))
            a_copies[-1].start()
        else:
            own_stores.append(pltpu.make_async_copy(made.at[n], target, block_sem.at[h]))
            own_stores[-1].start()

    tgt_feat_near.wait_recv()
    tgt_feat_out.wait_recv()
    tgt_feat_pass.start()
    for copy in tgt_out:
        copy.wait_recv()
    tgt_pass.start()
    tgt_near_out.wait_recv()
    tgt_feat_pass.wait_recv()
    cross_terms(feat_src, lambda k: feat_tgt if k == 0 else tgt_feat_peer.at[k - 1])
    tgt_pass.wait_recv()
    for store in own_stores:
        store.wait()
    assemble(tgt, tgt_near, tgt_blocks, tgt_far, slab, turned, block_sem, chip, core, rows)

    def tgt_load(n):
        return pltpu.make_async_copy(rows_of(tgt, tgt_near, tgt_far, *ordered[n]), src_buf.at[n % 2], src_sem.at[n % 2])

    def left_load(n):
        k, h = ordered[n]
        return pltpu.make_async_copy(ready.at[:, aligned(devices[k] * rows + h * SLAB, SLAB)], left_buf.at[n % 2],
                                     load_sem.at[n % 2])

    def prepare(n):
        k, h = ordered[n]
        if k and h == 0:
            for copy, (kk, hh) in zip(a_copies, order):
                if kk == k:
                    copy.wait_recv()
        tgt_load(n).start()
        left_load(n).start()

    prepare(0)
    for n, (k, h) in enumerate(ordered):
        tgt_load(n).wait()
        left_load(n).wait()
        if n + 1 < len(ordered) and not (k and h == per - 1):
            prepare(n + 1)

        def update(t, carry, n=n):
            span = aligned(t * TILE, TILE)
            acc[:, span] += weighted(mm(left_buf[n % 2], src_buf[n % 2, :, span], NN), 2.0 * (1.0 - ALPHA))
            return carry
        lax.fori_loop(0, cols // TILE, update, 0)
        if n + 1 < len(ordered) and k and h == per - 1:
            prepare(n + 1)

    kern_store = pltpu.make_async_copy(acc, kern_out, load_sem.at[2])

    def store_kernel(n):
        if isinstance(n, int):
            kern_store.start()
    sweeps(1, False, mass_rows, mass_cols, store_kernel)
    row_out[...] = row_scale[...]
    col_out[...] = col_scale[...]
    kern_store.wait()
    for slot in range(2):
        near_copy(slot).wait_send()
    for copy in ([src_near_out, src_feat_near, start_near_out, tgt_near_out, tgt_feat_near, src_feat_out, tgt_feat_out,
                  src_pass, src_feat_pass, tgt_pass, tgt_feat_pass] + src_out + tgt_out + mass_out + a_copies):
        copy.wait_send()
    for s in range(steps):
        for copy in start_out(s):
            copy.wait_send()


def solution(mesh):
    def local_fgw(cost_src, cost_tgt, plan_init, mass_src, mass_tgt, feat_src, feat_tgt, epsilon):
        rows, cols = cost_src.shape
        half, quad = cols // 2, rows // 2
        depth = feat_src.shape[1]
        tiles = cols // LANES // CHUNKS
        me = lax.axis_index('rows')
        mass_cols_mine = lax.dynamic_slice(mass_tgt, (rows * me,), (rows,))
        vec = (CHUNKS, tiles, LANES)
        n_links = 31 + 2 * (half // STEP) + 2 + 3 * rows // SLAB
        any_spec = pl.BlockSpec(memory_space=pl.ANY)
        vmem_spec = pl.BlockSpec(memory_space=pltpu.VMEM)
        hbm = [((rows, cols), BF16), ((rows, cols), BF16),
               ((rows, cols), BF16), ((2, 5, quad, quad), BF16), ((half, cols), BF16),
               ((rows, cols), BF16), ((2, 5, quad, quad), BF16), ((half, cols), BF16),
               ((GROUP - 1, rows, depth), BF16), ((GROUP - 1, rows, depth), BF16),
               ((rows, half), BF16), ((2, rows, half), BF16), ((rows, cols), BF16)]
        outs = [((rows, cols), F32), ((rows, LANES), F32), (vec, F32)] + hbm
        vmem = [((rows, cols), F32), ((rows, cols), BF16), ((2, SLAB, cols), BF16), ((cols, STEP), BF16),
                ((2, cols, STEP), BF16), ((2, cols, STEP), BF16), ((GROUP * rows // SLAB, SLAB, rows), BF16),
                ((2, rows, SLAB), BF16), ((SLAB, half), BF16), ((half, SLAB), BF16), ((2, rows, depth), BF16),
                (vec, F32), ((rows, LANES), F32), ((rows, LANES), F32), (vec, F32), (vec, F32),
                ((2, 2) + vec, F32), ((2, 2, GROUP - 1) + vec, F32),
                ((CHUNKS, 2, tiles, LANES), F32), ((GROUP - 1, CHUNKS, 2, tiles, LANES), F32)]
        sems = [(6,), (2,), (15,), (n_links,), (n_links,), (2, 2, GROUP - 1, CHUNKS), (2, 2, GROUP - 1, CHUNKS),
                (GROUP - 1, CHUNKS), (GROUP - 1, CHUNKS)]
        result = pl.pallas_call(
            kernel,
            out_shape=[jax.ShapeDtypeStruct(*s) for s in outs],
            in_specs=[any_spec] * 5 + [vmem_spec] * 4 + [pl.BlockSpec(memory_space=pltpu.SMEM)],
            out_specs=[any_spec, vmem_spec, vmem_spec] + [any_spec] * len(hbm),
            scratch_shapes=[pltpu.VMEM(*s) for s in vmem] + [pltpu.SemaphoreType.DMA(s) for s in sems]
            + [pltpu.SemaphoreType.REGULAR],
            compiler_params=pltpu.CompilerParams(collective_id=0, has_side_effects=True, vmem_limit_bytes=67000000),
            cost_estimate=pl.CostEstimate(flops=10 * rows * cols * cols, bytes_accessed=700000000,
                                          transcendentals=2 * rows * cols),
            name='fused_gw',
        )(cost_src, cost_tgt, plan_init.astype(BF16), feat_src.astype(BF16), feat_tgt.astype(BF16),
          mass_src.reshape(tiles, LANES), jnp.broadcast_to(mass_cols_mine[:, None], (rows, LANES)),
          jnp.broadcast_to(mass_src[:, None], (rows, LANES)), mass_tgt.reshape(vec), epsilon.reshape(1))
        kern, row_scale, col_scale = result[:3]
        return row_scale[:, :1] * kern * col_scale.reshape(1, cols)

    row_spec = P(('pairs', 'rows'), None)
    vec_spec = P(('pairs', 'rows'))
    in_specs = (row_spec, row_spec, row_spec, vec_spec, P('pairs'), row_spec, row_spec, P())
    return jax.shard_map(local_fgw, mesh=mesh, in_specs=in_specs, out_specs=row_spec, check_vma=False)
```

time: 1310 us -> 642 us (0.49)
  Pallas kernels: 0 us -> 610 us
  waiting for transfers between devices: 551 us -> 0 us
  other arithmetic: 345 us -> 25 us
  blocking collectives: 203 us -> 0 us
  matrix products: 184 us -> 0 us
  between operations: 13.9 us -> 0.67 us
    pallas_call x0 -> x1, Pallas kernels: none -> 610 us  [local_fgw(): pl.pallas_call(kernel, out_shape=[jax.ShapeDtypeStruct(*s) for s in outs]...]
    all_gather x4 -> x0, waiting for transfers between devices: 551 us -> none  [the longest x2 391 us: local_fgw(): lax.all_gather(transport.astype(jnp.bfloat16), 'rows', tiled=True)]
    reduce_sum x40 -> x0, other arithmetic: 284 us -> none  [the longest x20 143 us: value_a14(): col_sum = lax.psum(jnp.sum(kernel * row_scale[:, None], axis=0), 'rows')]
    psum x20 -> x0, blocking collectives: 203 us -> none  [value_a14(): col_sum = lax.psum(jnp.sum(kernel * row_scale[:, None], axis=0), 'rows')]
    dot_general x5 -> x0, matrix products: 184 us -> none  [the longest x2 89.8 us: local_fgw(): jnp.dot(src_half, transport_all, preferred_element_type=jnp.float32)]
    convert_element_type x4 -> x3, other arithmetic: 31.1 us -> 13.1 us  [the longest x1 8.97 us: local_fgw(): plan_init.astype(BF16)]
    exp x2 -> x0, other arithmetic: 16.1 us -> none  [gibbs_kernel(): jnp.exp(-(cost_rows - jnp.min(cost_rows, axis=1, keepdims=True)) / epsilon)]
  transfers between devices with their start and end apart: 4 -> 0, of which waited for: 4 -> 0; matrix products, arithmetic and copies ran while one was open for 6% -> 0% of each run, Pallas kernels for 0% -> 0%
where the time goes in v4:
time: 642 us; the launch traced here: 640 us
  Pallas kernels  610 us (95%)
  other arithmetic  25 us (4%)
    pallas_call x1, Pallas kernels, local_fgw(): pl.pallas_call(kernel, out_shape=[jax.ShapeDtypeStruct(*s) for s in outs]...  610 us

profile of v4, /device:TPU:0, one launch (start us, length us, event | category | flops | bytes accessed | tf_op | source)
XLA Modules:
  0.0 640.3 jit_solution(10642341701497284656)
XLA Ops:
  0.7 0.7 dynamic_slice.3
  1.3 1.0 broadcast_in_dim.4.mass_rows_t
  2.4 2.1 convert_element_type.10.feat_src
  4.4 2.1 convert_element_type.11.feat_tgt
  6.5 1.7 broadcast_in_dim.5.mass_rows
  8.2 9.0 %convert_element_type.9.start = bf16[1024,4096]{1,0:T(8,128)(2,1)} convert(f32[1024,4096]{1,0:T(8,128)} %param.10) | non-fusion elementwise | flops 4194304 | bytes 25165824 | tf_op jit(solution)/shard_map/convert_element_type | solution.py:588
  17.2 610.0 %fused_gw.1 = (f32[1024,4096]{1,0:T(8,128)}, f32[1024,128]{1,0:T(8,128)}, f32[4,8,128]{2,1,0:T(8,128)}, bf16[1024,4096]{1,0:T(8,128)(2,1)}, bf16[1024,4096]{1,0:...) custom-call(f32[1024,4096]{1,0:T(8,128)} %src_f32.1, ...), custom_call_target="tpu_custom_call" | custom-call | flops 171798691840 | bytes 700000000 | tf_op jit(solution)/shard_map/fused_gw/pallas_call | solution.py:577
  627.2 1.2 slice_reduce_fusion
  628.4 11.9 %multiply_multiply_fusion = f32[1024,4096]{1,0:T(8,128)} fusion(f32[1024,4096]{1,0:T(8,128)} %get-tuple-element.9, f32[4096]{0:T(1024)} %bitcast.5, f32[1024]{0:T(1024)S(1)} %slice_reduce_fusion), kind=kLoop, calls=%fused_computation | loop fusion | flops 8388608 | bytes 33574912 | tf_op jit(solution)/shard_map/mul | solution.py:592

commit v5 on v4

--- a/solution.py
+++ b/solution.py
@@ -18,6 +18,8 @@
 EARLY_STEPS = 1
 TAIL_PIECES = 4
 GROUP = 4
+PART = 256
+SPLIT = 4
 MESH = pl.DeviceIdType.MESH
 NT = (((1,), (1,)), ((), ()))
 NN = (((1,), (0,)), ((), ()))
@@ -33,6 +35,21 @@
     return lax.dot_general(left, right, dims, preferred_element_type=F32)
 
 
+class Copies:
+    def __init__(self, source, target, sems, rows):
+        part = rows // SPLIT
+        self.parts = [pltpu.make_async_copy(source.at[pl.ds(i * part, part)], target.at[pl.ds(i * part, part)], sems.at[i])
+                      for i in range(SPLIT)]
+
+    def start(self):
+        for part in self.parts:
+            part.start()
+
+    def wait(self):
+        for part in self.parts:
+            part.wait()
+
+
 def split(val):
     return val.reshape(val.shape[0] // 8, 8, LANES)
 
@@ -41,8 +58,7 @@
     return pl.ds(pl.multiple_of(start, size), size)
 
 
-def assemble(cost, cost_near, blocks, far, slab, turned, sems, chip, core, rows):
-    quad = rows // 2
+def turn_corner(cost, cost_near, far, slab, turned, sems, chip, core, rows):
     half = 2 * rows
     away = half * (1 - chip)
     for source, owner in ((cost, core), (cost_near, 1 - core)):
@@ -58,6 +74,12 @@
             store = pltpu.make_async_copy(turned, far.at[:, aligned(half * chip + owner * rows + a * SLAB, SLAB)], sems.at[1])
             store.start()
             store.wait()
+
+
+def place_corner(blocks, far, slab, turned, sems, chip, core, rows):
+    quad = rows // 2
+    half = 2 * rows
+    away = half * (1 - chip)
 
     def corner(k, carry):
         cc = core + k - 2 * core * k
@@ -182,13 +204,13 @@
             src_buf[b, span, :] = acc[aligned(b * quad + t * BLOCK, BLOCK), :].astype(BF16)
             return carry
         lax.fori_loop(0, quad // BLOCK, cast, 0)
-        src_stores.append(pltpu.make_async_copy(src_buf.at[b], src.at[pl.ds(b * quad, quad)], src_sem.at[b]))
+        src_stores.append(pltpu.make_async_copy(src_buf.at[b], src.at[pl.ds(b * quad, quad)], src_sem.at[b, 0]))
         src_stores[-1].start()
     tgt_load_all = pltpu.make_async_copy(tgt_f32, acc, load_sem.at[0])
     tgt_load_all.start()
     for store in src_stores:
         store.wait()
-    for copy in src_out + [src_near_out, src_feat_out]:
+    for copy in [src_feat_out, src_near_out] + src_out:
         copy.start()
     for s in range(EARLY_STEPS, steps):
         for copy in start_out(s):
@@ -208,31 +230,36 @@
         copy.start()
 
     def cross_terms(first, peer_second):
-        own = pltpu.make_async_copy(first, feat_buf.at[0], load_sem.at[1])
-        own.start()
-        own.wait()
+        depth = feat_buf.shape[1]
+        seconds = [left_buf.at[k // 2, :, pl.ds(k % 2 * depth, depth)] for k in range(GROUP)]
+        loads = [pltpu.make_async_copy(first, feat_buf, load_sem.at[1])]
+        loads += [pltpu.make_async_copy(peer_second(k), seconds[k], load_sem.at[2 + k]) for k in range(GROUP)]
+        for load in loads:
+            load.start()
+        for load in loads:
+            load.wait()
         for k, device in enumerate(devices):
-            load = pltpu.make_async_copy(peer_second(k), feat_buf.at[1], load_sem.at[1])
-            load.start()
-            load.wait()
-
-            def cross_term(h, carry, device=device):
-                block = mm(feat_buf[0], feat_buf[1, aligned(h * 256, 256), :], NT)
-                acc[:, aligned(device * rows + h * 256, 256)] = weighted(block, 2.0 * ALPHA)
+
+            def cross_term(h, carry, device=device, k=k):
+                second = left_buf[k // 2, aligned(h * TILE, TILE), k % 2 * depth:(k % 2 + 1) * depth]
+                acc[:, aligned(device * rows + h * TILE, TILE)] = weighted(mm(feat_buf[...], second, NT), 2.0 * ALPHA)
                 return carry
-            lax.fori_loop(0, rows // 256, cross_term, 0)
-
+            lax.fori_loop(0, rows // TILE, cross_term, 0)
+
+    src_near_out.wait_recv()
+    turn_corner(src, src_near, src_far, slab, turned, block_sem, chip, core, rows)
     src_feat_near.wait_recv()
+    src_feat_out.wait_recv()
+    src_feat_pass.start()
+    src_feat_pass.wait_recv()
+    cross_terms(feat_tgt, lambda k: feat_src if k == 0 else src_feat_peer.at[k - 1])
+    tgt_near_out.wait_recv()
+    turn_corner(tgt, tgt_near, tgt_far, slab, turned, block_sem, chip, core, rows)
     for copy in src_out:
         copy.wait_recv()
     src_pass.start()
-    src_feat_out.wait_recv()
-    src_feat_pass.start()
-    src_near_out.wait_recv()
     src_pass.wait_recv()
-    assemble(src, src_near, src_blocks, src_far, slab, turned, block_sem, chip, core, rows)
-    src_feat_pass.wait_recv()
-    cross_terms(feat_tgt, lambda k: feat_src if k == 0 else src_feat_peer.at[k - 1])
+    place_corner(src_blocks, src_far, slab, turned, block_sem, chip, core, rows)
 
     def rows_of(matrix, matrix_near, matrix_far, k, h):
         if k == 0:
@@ -245,15 +272,17 @@
     ordered = [(k, h) for k in range(GROUP) for h in range(per)]
 
     def src_load(b):
-        return pltpu.make_async_copy(rows_of(src, src_near, src_far, *ordered[b]), src_buf.at[b % 2], src_sem.at[b % 2])
-
-    def gather(base, s, right, slot):
+        return Copies(rows_of(src, src_near, src_far, *ordered[b]), src_buf.at[b % 2], src_sem.at[b % 2], SLAB)
+
+    def gather(parts):
         def update(h, carry):
             span = aligned(h * TILE, TILE)
-            block = mm(keep[:, col_span(base, s)], right[slot, span, :], NT)
+            left = [keep[:, col_span(base, s)] for base, s, _, _ in parts]
+            right = [buf[slot, span, :] for _, _, buf, slot in parts]
+            block = mm(jnp.concatenate(left, axis=1), jnp.concatenate(right, axis=1), NT)
             acc[:, span] += weighted(block, 2.0 * (1.0 - ALPHA))
             return carry
-        lax.fori_loop(0, cols // TILE, update, 0)
+        lax.fori_loop(0, cols // TILE, update, 0, unroll=2)
 
     start_near_out.wait_recv()
     src_load(0).start()
@@ -266,15 +295,22 @@
         for k, device in enumerate(devices):
             source = (start.at[:, col_span(mine, s)] if k == 0 else start_near.at[:, col_span(0, s)] if k == 1
                       else start_far.at[k - 2, :, col_span(0, s)])
-            loads.append(pltpu.make_async_copy(source, start_buf.at[aligned(device * rows, rows)], load_sem.at[2 + k]))
+            landing = turned.at[pl.ds(k // 2 * rows, rows), pl.ds(k % 2 * STEP, STEP)]
+            loads.append(pltpu.make_async_copy(source, landing, load_sem.at[2 + k]))
         for load in loads:
             load.start()
 
         @pl.when(s >= 2)
         def _():
             near_copy(slot).wait_send()
-        for load in loads:
+        for k, load in enumerate(loads):
             load.wait()
+
+            def turn(t, carry, k=k):
+                block = turned[aligned(k // 2 * rows + t * STEP, STEP), pl.ds(k % 2 * STEP, STEP)]
+                start_buf[:, aligned(devices[k] * rows + t * STEP, STEP)] = block.T
+                return carry
+            lax.fori_loop(0, rows // STEP, turn, 0, unroll=2)
         for b, (k, h) in enumerate(ordered):
             src_load(b).wait()
             if b + 1 < len(ordered):
@@ -283,18 +319,26 @@
                 @pl.when(s + 1 < steps)
                 def _():
                     src_load(0).start()
-            own_buf[slot, aligned(devices[k] * rows + h * SLAB, SLAB), :] = mm(src_buf[b % 2], start_buf[...], NN).astype(BF16)
+
+            def part_a(t, carry, b=b, k=k, h=h):
+                value = mm(src_buf[b % 2, aligned(t * PART, PART), :], start_buf[...], NT).astype(BF16)
+                own_buf[slot, aligned(devices[k] * rows + h * SLAB + t * PART, PART), :] = value
+                return carry
+            lax.fori_loop(0, SLAB // PART, part_a, 0)
 
         @pl.when(s >= 2)
         def _():
             pl.semaphore_wait(free_sem, 1)
         near_copy(slot).start()
-        gather(mine, s, own_buf, slot)
+
+        @pl.when(s == 0)
+        def _():
+            gather([(mine, s, own_buf, slot)])
 
         @pl.when(s >= 1)
         def _():
             near_copy(1 - slot).wait_recv()
-            gather(other, s - 1, near_buf, 1 - slot)
+            gather([(mine, s, own_buf, slot), (other, s - 1, near_buf, 1 - slot)])
 
         @pl.when(jnp.logical_and(s >= 1, s - 1 < steps - 2))
         def _():
@@ -303,7 +347,7 @@
     lax.fori_loop(0, steps, step, 0)
     final = (steps - 1) % 2
     near_copy(final).wait_recv()
-    gather(other, steps - 1, near_buf, final)
+    gather([(other, steps - 1, near_buf, final)])
 
     def tile(j, t):
         begin = j * width + t * LANES
@@ -331,7 +375,7 @@
                 span = pl.ds(i * BLOCK, BLOCK)
                 scale = split(row_scale[span, :])
                 return tuple(sums[t] + jnp.sum(split(acc[span, tile(j, t)]) * scale, axis=0) for t in range(tiles))
-            sums = lax.fori_loop(0, rows // BLOCK, body, tuple(jnp.zeros((8, LANES), F32) for _ in range(tiles)))
+            sums = lax.fori_loop(0, rows // BLOCK, body, tuple(jnp.zeros((8, LANES), F32) for _ in range(tiles)), unroll=2)
             total = jnp.concatenate([jnp.sum(s, axis=0, keepdims=True) for s in sums], axis=0)
             if transposed:
                 total = total * shift_fix[j]
@@ -364,7 +408,7 @@
                     total = term if total is None else total + term
                 row_acc[span, :] = total.reshape(BLOCK, LANES)
                 return carry
-            lax.fori_loop(0, rows // BLOCK, body, 0)
+            lax.fori_loop(0, rows // BLOCK, body, 0, unroll=2)
 
         if transposed:
             for j in range(CHUNKS):
@@ -460,7 +504,7 @@
     order = [(k, h) for k in (2, 3, 1, 0) for h in range(per)]
 
     def src_again(n):
-        return pltpu.make_async_copy(rows_of(src, src_near, src_far, *order[n]), src_buf.at[n % 2], src_sem.at[n % 2])
+        return Copies(rows_of(src, src_near, src_far, *order[n]), src_buf.at[n % 2], src_sem.at[n % 2], SLAB)
 
     column = aligned(me * rows, rows)
     a_copies, own_stores = [], []
@@ -474,7 +518,7 @@
             span = aligned(t * 256, 256)
             made[n, :, span] = mm(src_buf[n % 2], keep[span, :], NT).astype(BF16)
             return carry
-        lax.fori_loop(0, rows // 256, make, 0)
+        lax.fori_loop(0, rows // 256, make, 0, unroll=2)
         target = ready.at[pl.ds(h * SLAB, SLAB), column]
         if k:
             a_copies.append(remote(made.at[n], target, devices[k], reserve(1)))
@@ -489,16 +533,15 @@
     for copy in tgt_out:
         copy.wait_recv()
     tgt_pass.start()
-    tgt_near_out.wait_recv()
     tgt_feat_pass.wait_recv()
     cross_terms(feat_src, lambda k: feat_tgt if k == 0 else tgt_feat_peer.at[k - 1])
     tgt_pass.wait_recv()
     for store in own_stores:
         store.wait()
-    assemble(tgt, tgt_near, tgt_blocks, tgt_far, slab, turned, block_sem, chip, core, rows)
+    place_corner(tgt_blocks, tgt_far, slab, turned, block_sem, chip, core, rows)
 
     def tgt_load(n):
-        return pltpu.make_async_copy(rows_of(tgt, tgt_near, tgt_far, *ordered[n]), src_buf.at[n % 2], src_sem.at[n % 2])
+        return Copies(rows_of(tgt, tgt_near, tgt_far, *ordered[n]), src_buf.at[n % 2], src_sem.at[n % 2], SLAB)
 
     def left_load(n):
         k, h = ordered[n]
@@ -525,7 +568,7 @@
             span = aligned(t * TILE, TILE)
             acc[:, span] += weighted(mm(left_buf[n % 2], src_buf[n % 2, :, span], NN), 2.0 * (1.0 - ALPHA))
             return carry
-        lax.fori_loop(0, cols // TILE, update, 0)
+        lax.fori_loop(0, cols // TILE, update, 0, unroll=2)
         if n + 1 < len(ordered) and k and h == per - 1:
             prepare(n + 1)
 
@@ -566,13 +609,13 @@
                ((GROUP - 1, rows, depth), BF16), ((GROUP - 1, rows, depth), BF16),
                ((rows, half), BF16), ((2, rows, half), BF16), ((rows, cols), BF16)]
         outs = [((rows, cols), F32), ((rows, LANES), F32), (vec, F32)] + hbm
-        vmem = [((rows, cols), F32), ((rows, cols), BF16), ((2, SLAB, cols), BF16), ((cols, STEP), BF16),
+        vmem = [((rows, cols), F32), ((rows, cols), BF16), ((2, SLAB, cols), BF16), ((STEP, cols), BF16),
                 ((2, cols, STEP), BF16), ((2, cols, STEP), BF16), ((GROUP * rows // SLAB, SLAB, rows), BF16),
-                ((2, rows, SLAB), BF16), ((SLAB, half), BF16), ((half, SLAB), BF16), ((2, rows, depth), BF16),
+                ((2, rows, SLAB), BF16), ((SLAB, half), BF16), ((half, SLAB), BF16), ((rows, depth), BF16),
                 (vec, F32), ((rows, LANES), F32), ((rows, LANES), F32), (vec, F32), (vec, F32),
                 ((2, 2) + vec, F32), ((2, 2, GROUP - 1) + vec, F32),
                 ((CHUNKS, 2, tiles, LANES), F32), ((GROUP - 1, CHUNKS, 2, tiles, LANES), F32)]
-        sems = [(6,), (2,), (15,), (n_links,), (n_links,), (2, 2, GROUP - 1, CHUNKS), (2, 2, GROUP - 1, CHUNKS),
+        sems = [(6,), (2, SPLIT), (15,), (n_links,), (n_links,), (2, 2, GROUP - 1, CHUNKS), (2, 2, GROUP - 1, CHUNKS),
                 (GROUP - 1, CHUNKS), (GROUP - 1, CHUNKS)]
         result = pl.pallas_call(
             kernel,

time: 642 us -> 577 us (0.90); the launches traced: 640 us -> 567 us
  Pallas kernels: 610 us -> 536 us
    pallas_call x1, Pallas kernels: 610 us -> 536 us  [local_fgw(): pl.pallas_call(kernel, out_shape=[jax.ShapeDtypeStruct(*s) for s in outs]...]
where the time goes in v5:
time: 577 us; the launch traced here: 567 us
  Pallas kernels  536 us (93%)
  other arithmetic  25 us (4%)
    pallas_call x1, Pallas kernels, local_fgw(): pl.pallas_call(kernel, out_shape=[jax.ShapeDtypeStruct(*s) for s in outs]...  536 us
    mul x1, other arithmetic, local_fgw(): return row_scale[:, :1] * kern * col_scale.reshape(1, cols)  11.9 us

profile of v5, /device:TPU:0, one launch (start us, length us, event | category | flops | bytes accessed | tf_op | source)
XLA Modules:
  0.0 567.0 jit_solution(12231298681702050539)
XLA Ops:
  0.7 0.7 dynamic_slice.3
  1.3 1.0 broadcast_in_dim.4.mass_rows_t
  2.4 2.1 convert_element_type.10.feat_src
  4.4 2.1 convert_element_type.11.feat_tgt
  6.5 1.7 broadcast_in_dim.5.mass_rows
  8.2 9.0 %convert_element_type.9.start = bf16[1024,4096]{1,0:T(8,128)(2,1)} convert(f32[1024,4096]{1,0:T(8,128)} %param.10) | non-fusion elementwise | flops 4194304 | bytes 25165824 | tf_op jit(solution)/shard_map/convert_element_type | solution.py:631
  17.2 536.2 %fused_gw.1 = (f32[1024,4096]{1,0:T(8,128)}, f32[1024,128]{1,0:T(8,128)}, f32[4,8,128]{2,1,0:T(8,128)}, bf16[1024,4096]{1,0:T(8,128)(2,1)}, bf16[1024,4096]{1,0:...) custom-call(f32[1024,4096]{1,0:T(8,128)} %src_f32.1, ...), custom_call_target="tpu_custom_call" | custom-call | flops 171798691840 | bytes 700000000 | tf_op jit(solution)/shard_map/fused_gw/pallas_call | solution.py:620
  553.4 1.2 slice_reduce_fusion
  554.7 11.9 %multiply_multiply_fusion = f32[1024,4096]{1,0:T(8,128)} fusion(f32[1024,4096]{1,0:T(8,128)} %get-tuple-element.9, f32[4096]{0:T(1024)} %bitcast.5, f32[1024]{0:T(1024)S(1)} %slice_reduce_fusion), kind=kLoop, calls=%fused_computation | loop fusion | flops 8388608 | bytes 33574912 | tf_op jit(solution)/shard_map/mul | solution.py:635

commit v6 on v5

--- a/solution.py
+++ b/solution.py
@@ -15,8 +15,7 @@
 STEP = 256
 SLAB = 512
 TILE = 512
-EARLY_STEPS = 1
-TAIL_PIECES = 4
+TAIL_PIECES = 7
 GROUP = 4
 PART = 256
 SPLIT = 4
@@ -112,8 +111,8 @@
     lax.fori_loop(0, 2, corner, 0)
 
 
-def kernel(src_f32, tgt_f32, start, feat_src, feat_tgt, mass_mine, mass_rows_t, mass_rows, mass_cols, epsilon,
-           kern_out, row_out, col_out, src, tgt, src_near, src_blocks, src_far, tgt_near, tgt_blocks, tgt_far,
+def kernel(src_f32, tgt_f32, start_f32, feat_src_f32, feat_tgt_f32, mass_mine, mass_rows_t, mass_rows, mass_cols, epsilon,
+           kern_out, row_out, col_out, start, feat_src, feat_tgt, src, tgt, src_near, src_blocks, src_far, tgt_near, tgt_blocks, tgt_far,
            src_feat_peer, tgt_feat_peer, start_near, start_far, ready,
            acc, keep, src_buf, start_buf, own_buf, near_buf, made, left_buf, slab, turned, feat_buf, mass_all,
            row_scale, row_acc, col_scale, shift_fix, part_sum, peer_sum, part_top, peer_top,
@@ -134,8 +133,20 @@
 
     src_load_all = [pltpu.make_async_copy(src_f32.at[pl.ds(b * quad, quad)], acc.at[pl.ds(b * quad, quad)], load_sem.at[b])
                     for b in range(2)]
-    for load in src_load_all:
-        load.start()
+    mine, other = half * core, half * (1 - core)
+    depth = feat_src_f32.shape[1]
+
+    def col_span(base, s):
+        return aligned(base + s * STEP, STEP)
+
+    heads = [(start_f32.at[:, col_span(mine, 0)], start.at[:, col_span(mine, 0)], STEP),
+             (start_f32.at[:, col_span(other, 0)], start.at[:, col_span(other, 0)], STEP),
+             (feat_src_f32, feat_src, depth), (feat_tgt_f32, feat_tgt, depth)]
+    head_loads, head_stores = [], []
+    for n, (source, target, size) in enumerate(heads):
+        head_loads.append(pltpu.make_async_copy(source, acc.at[:, pl.ds(n * size, size)], load_sem.at[2 + n]))
+        head_loads[-1].start()
+        head_stores.append(pltpu.make_async_copy(left_buf.at[n // 2, :, pl.ds(n % 2 * size, size)], target, load_sem.at[2 + n]))
     mass_all[me] = mass_mine[...]
     barrier = pltpu.get_barrier_semaphore()
     for peer in peers:
@@ -152,14 +163,10 @@
         return pltpu.make_async_remote_copy(src_ref=source, dst_ref=target, send_sem=send_sem.at[index],
                                             recv_sem=recv_sem.at[index], device_id={'rows': peer}, device_id_type=MESH)
 
-    def col_span(base, s):
-        return aligned(base + s * STEP, STEP)
-
     def block_spots():
         diag, off = me * rows, (me + 1 - 2 * core) * rows
         return [(0, diag), (0, diag + quad), (quad, diag + quad), (0, off + quad * core), (quad * core, off + quad)]
 
-    mine, other = half * core, half * (1 - core)
     src_near_out = remote(src, src_near, near, reserve(1))
     src_feat_near = remote(feat_src, src_feat_peer.at[0], near, reserve(1))
     start_near_out = remote(start.at[:, aligned(other, half)], start_near, near, reserve(1))
@@ -189,10 +196,22 @@
     def near_copy(slot):
         return remote(own_buf.at[slot], near_buf.at[slot], near, near_base + slot)
 
-    for s in range(EARLY_STEPS):
-        for copy in start_out(s):
-            copy.start()
-    for copy in [start_near_out, src_feat_near, tgt_feat_near] + mass_out:
+    for n, (_, _, size) in enumerate(heads):
+        head_loads[n].wait()
+
+        def cast_head(t, carry, n=n, size=size):
+            span = aligned(t * 256, 256)
+            left_buf[n // 2, span, n % 2 * size:(n % 2 + 1) * size] = acc[span, n * size:(n + 1) * size].astype(BF16)
+            return carry
+        lax.fori_loop(0, rows // 256, cast_head, 0)
+        head_stores[n].start()
+    for load in src_load_all:
+        load.start()
+    for store in head_stores:
+        store.wait()
+    for copy in start_out(0):
+        copy.start()
+    for copy in [src_feat_near, tgt_feat_near] + mass_out:
         copy.start()
 
     src_stores = []
@@ -206,22 +225,35 @@
         lax.fori_loop(0, quad // BLOCK, cast, 0)
         src_stores.append(pltpu.make_async_copy(src_buf.at[b], src.at[pl.ds(b * quad, quad)], src_sem.at[b, 0]))
         src_stores[-1].start()
-    tgt_load_all = pltpu.make_async_copy(tgt_f32, acc, load_sem.at[0])
-    tgt_load_all.start()
+    start_load = pltpu.make_async_copy(start_f32, acc, load_sem.at[0])
+    start_load.start()
     for store in src_stores:
         store.wait()
     for copy in [src_feat_out, src_near_out] + src_out:
         copy.start()
-    for s in range(EARLY_STEPS, steps):
-        for copy in start_out(s):
-            copy.start()
-    tgt_load_all.wait()
-
-    def cast_tgt(t, carry):
+
+    def cast_keep(t, carry):
         span = aligned(t * BLOCK, BLOCK)
         keep[span, :] = acc[span, :].astype(BF16)
         return carry
-    lax.fori_loop(0, rows // BLOCK, cast_tgt, 0)
+    start_load.wait()
+    lax.fori_loop(0, rows // BLOCK, cast_keep, 0)
+    tgt_load_all = pltpu.make_async_copy(tgt_f32, acc, load_sem.at[0])
+    tgt_load_all.start()
+    rest = half - STEP
+    start_stores = []
+    for n, base in enumerate((mine, other)):
+        span = pl.ds(pl.multiple_of(base + STEP, STEP), rest)
+        start_stores.append(pltpu.make_async_copy(keep.at[:, span], start.at[:, span], load_sem.at[2 + n]))
+        start_stores[-1].start()
+    for store in start_stores:
+        store.wait()
+    for s in range(1, steps):
+        for copy in start_out(s):
+            copy.start()
+    start_near_out.start()
+    tgt_load_all.wait()
+    lax.fori_loop(0, rows // BLOCK, cast_keep, 0)
     tgt_store = pltpu.make_async_copy(keep, tgt, load_sem.at[0])
     tgt_store.start()
     tgt_store.wait()
@@ -324,7 +356,7 @@
                 value = mm(src_buf[b % 2, aligned(t * PART, PART), :], start_buf[...], NT).astype(BF16)
                 own_buf[slot, aligned(devices[k] * rows + h * SLAB + t * PART, PART), :] = value
                 return carry
-            lax.fori_loop(0, SLAB // PART, part_a, 0)
+            lax.fori_loop(0, SLAB // PART, part_a, 0, unroll=2)
 
         @pl.when(s >= 2)
         def _():
@@ -540,37 +572,49 @@
         store.wait()
     place_corner(tgt_blocks, tgt_far, slab, turned, block_sem, chip, core, rows)
 
-    def tgt_load(n):
-        return Copies(rows_of(tgt, tgt_near, tgt_far, *ordered[n]), src_buf.at[n % 2], src_sem.at[n % 2], SLAB)
-
-    def left_load(n):
-        k, h = ordered[n]
-        return pltpu.make_async_copy(ready.at[:, aligned(devices[k] * rows + h * SLAB, SLAB)], left_buf.at[n % 2],
-                                     load_sem.at[n % 2])
-
-    def prepare(n):
-        k, h = ordered[n]
-        if k and h == 0:
-            for copy, (kk, hh) in zip(a_copies, order):
-                if kk == k:
-                    copy.wait_recv()
-        tgt_load(n).start()
-        left_load(n).start()
-
-    prepare(0)
-    for n, (k, h) in enumerate(ordered):
-        tgt_load(n).wait()
-        left_load(n).wait()
-        if n + 1 < len(ordered) and not (k and h == per - 1):
-            prepare(n + 1)
-
-        def update(t, carry, n=n):
+    def stage(k):
+        if k % 2 == 0:
+            return [src_buf.at[h] for h in range(per)], [left_buf.at[h] for h in range(per)]
+        return [keep.at[pl.ds(h * SLAB, SLAB)] for h in range(per)], [turned.at[pl.ds(h * rows, rows)] for h in range(per)]
+
+    def tgt_loads(k):
+        return [Copies(rows_of(tgt, tgt_near, tgt_far, k, h), stage(k)[0][h], src_sem.at[k % 2 * per + h], SLAB)
+                for h in range(per)]
+
+    def left_loads(k):
+        return [pltpu.make_async_copy(ready.at[:, aligned(devices[k] * rows + h * SLAB, SLAB)], stage(k)[1][h],
+                                      load_sem.at[k % 2 * per + h]) for h in range(per)]
+
+    def begin_left(k):
+        for copy, (kk, _) in zip(a_copies, order):
+            if kk == k:
+                copy.wait_recv()
+        for load in left_loads(k):
+            load.start()
+
+    for load in tgt_loads(0):
+        load.start()
+    begin_left(0)
+    for k in range(GROUP):
+        if k + 1 < GROUP:
+            for load in tgt_loads(k + 1):
+                load.start()
+        if k + 1 < GROUP - 1:
+            begin_left(k + 1)
+        elif k == GROUP - 1:
+            begin_left(k)
+        for load in tgt_loads(k) + left_loads(k):
+            load.wait()
+        rights, lefts = stage(k)
+
+        def update(t, carry, rights=rights, lefts=lefts):
             span = aligned(t * TILE, TILE)
-            acc[:, span] += weighted(mm(left_buf[n % 2], src_buf[n % 2, :, span], NN), 2.0 * (1.0 - ALPHA))
+            total = mm(lefts[0][...], rights[0][:, span], NN)
+            for h in range(1, per):
+                total = total + mm(lefts[h][...], rights[h][:, span], NN)
+            acc[:, span] += weighted(total, 2.0 * (1.0 - ALPHA))
             return carry
-        lax.fori_loop(0, cols // TILE, update, 0, unroll=2)
-        if n + 1 < len(ordered) and k and h == per - 1:
-            prepare(n + 1)
+        lax.fori_loop(0, cols // TILE, update, 0)
 
     kern_store = pltpu.make_async_copy(acc, kern_out, load_sem.at[2])
 
@@ -603,7 +647,8 @@
         n_links = 31 + 2 * (half // STEP) + 2 + 3 * rows // SLAB
         any_spec = pl.BlockSpec(memory_space=pl.ANY)
         vmem_spec = pl.BlockSpec(memory_space=pltpu.VMEM)
-        hbm = [((rows, cols), BF16), ((rows, cols), BF16),
+        hbm = [((rows, cols), BF16), ((rows, depth), BF16), ((rows, depth), BF16),
+               ((rows, cols), BF16), ((rows, cols), BF16),
                ((rows, cols), BF16), ((2, 5, quad, quad), BF16), ((half, cols), BF16),
                ((rows, cols), BF16), ((2, 5, quad, quad), BF16), ((half, cols), BF16),
                ((GROUP - 1, rows, depth), BF16), ((GROUP - 1, rows, depth), BF16),
@@ -615,7 +660,7 @@
                 (vec, F32), ((rows, LANES), F32), ((rows, LANES), F32), (vec, F32), (vec, F32),
                 ((2, 2) + vec, F32), ((2, 2, GROUP - 1) + vec, F32),
                 ((CHUNKS, 2, tiles, LANES), F32), ((GROUP - 1, CHUNKS, 2, tiles, LANES), F32)]
-        sems = [(6,), (2, SPLIT), (15,), (n_links,), (n_links,), (2, 2, GROUP - 1, CHUNKS), (2, 2, GROUP - 1, CHUNKS),
+        sems = [(8,), (4, SPLIT), (15,), (n_links,), (n_links,), (2, 2, GROUP - 1, CHUNKS), (2, 2, GROUP - 1, CHUNKS),
                 (GROUP - 1, CHUNKS), (GROUP - 1, CHUNKS)]
         result = pl.pallas_call(
             kernel,
@@ -628,7 +673,7 @@
             cost_estimate=pl.CostEstimate(flops=10 * rows * cols * cols, bytes_accessed=700000000,
                                           transcendentals=2 * rows * cols),
             name='fused_gw',
-        )(cost_src, cost_tgt, plan_init.astype(BF16), feat_src.astype(BF16), feat_tgt.astype(BF16),
+        )(cost_src, cost_tgt, plan_init, feat_src, feat_tgt,
           mass_src.reshape(tiles, LANES), jnp.broadcast_to(mass_cols_mine[:, None], (rows, LANES)),
           jnp.broadcast_to(mass_src[:, None], (rows, LANES)), mass_tgt.reshape(vec), epsilon.reshape(1))
         kern, row_scale, col_scale = result[:3]

time: 577 us -> 553 us (0.958)
  other arithmetic: 25 us -> 11.9 us
    convert_element_type x3 -> x0, other arithmetic: 13.1 us -> none  [the longest x1 8.97 us: local_fgw(): plan_init.astype(BF16)]
where the time goes in v6:
time: 553 us; the launch traced here: 548 us
  Pallas kernels  531 us (96%)
  other arithmetic  11.9 us (2%)
    pallas_call x1, Pallas kernels, local_fgw(): pl.pallas_call(kernel, out_shape=[jax.ShapeDtypeStruct(*s) for s in outs]...  531 us
    mul x1, other arithmetic, local_fgw(): return row_scale[:, :1] * kern * col_scale.reshape(1, cols)  11.9 us

profile of v6, /device:TPU:0, one launch (start us, length us, event | category | flops | bytes accessed | tf_op | source)
XLA Modules:
  0.0 548.4 jit_solution(6603860889562627089)
XLA Ops:
  0.7 0.7 dynamic_slice.3
  1.3 1.0 broadcast_in_dim.4.mass_rows_t
  2.3 1.7 broadcast_in_dim.5.mass_rows
  4.0 530.8 %fused_gw.1 = (f32[1024,4096]{1,0:T(8,128)}, f32[1024,128]{1,0:T(8,128)}, f32[4,8,128]{2,1,0:T(8,128)}, bf16[1024,4096]{1,0:T(8,128)(2,1)}, bf16[1024,256]{1,0:T...) custom-call(f32[1024,4096]{1,0:T(8,128)} %src_f32.1, ...), custom_call_target="tpu_custom_call" | custom-call | flops 171798691840 | bytes 700000000 | tf_op jit(solution)/shard_map/fused_gw/pallas_call | solution.py:665
  534.8 1.2 slice_reduce_fusion
  536.1 11.9 %multiply_multiply_fusion = f32[1024,4096]{1,0:T(8,128)} fusion(f32[1024,4096]{1,0:T(8,128)} %get-tuple-element.9, f32[4096]{0:T(1024)} %bitcast.5, f32[1024]{0:T(1024)S(1)} %slice_reduce_fusion), kind=kLoop, calls=%fused_computation | loop fusion | flops 8388608 | bytes 33574912 | tf_op jit(solution)/shard_map/mul | solution.py:680

commit v7 on v6

--- a/solution.py
+++ b/solution.py
@@ -15,7 +15,8 @@
 STEP = 256
 SLAB = 512
 TILE = 512
-TAIL_PIECES = 7
+TAIL_PIECES = 16
+PIECES = 4
 GROUP = 4
 PART = 256
 SPLIT = 4
@@ -175,11 +176,13 @@
     src_out = [remote(src.at[aligned(row, quad), aligned(col, quad)], src_blocks.at[0, b], same, reserve(1))
                for b, (row, col) in enumerate(block_spots())]
     src_feat_out = remote(feat_src, src_feat_peer.at[1], same, reserve(1))
-    tgt_feat_out = remote(feat_tgt, tgt_feat_peer.at[1], same, reserve(1))
-    piece = quad // 2
+    feat_part = rows // PIECES
+    tgt_feat_out = [remote(feat_tgt.at[pl.ds(i * feat_part, feat_part)], tgt_feat_peer.at[1, pl.ds(i * feat_part, feat_part)],
+                           same, reserve(1)) for i in range(PIECES)]
+    piece = quad // PIECES
     tgt_out = [remote(tgt.at[aligned(row + h * piece, piece), aligned(col, quad)],
                       tgt_blocks.at[0, b, pl.ds(h * piece, piece)], same, reserve(1))
-               for b, (row, col) in enumerate(block_spots()) for h in range(2)]
+               for b, (row, col) in enumerate(block_spots()) for h in range(PIECES)]
     src_pass = remote(src_blocks.at[0], src_blocks.at[1], near, reserve(1))
     src_feat_pass = remote(src_feat_peer.at[1], src_feat_peer.at[2], near, reserve(1))
     tgt_pass = remote(tgt_blocks.at[0], tgt_blocks.at[1], near, reserve(1))
@@ -187,7 +190,7 @@
     mass_out = [remote(mass_mine, mass_all.at[me], peer, reserve(1)) for peer in peers]
     start_base = reserve(2 * steps)
     near_base = reserve(2)
-    late_pieces = tgt_out[TAIL_PIECES:] + [tgt_feat_out]
+    late_pieces = tgt_out[TAIL_PIECES:] + tgt_feat_out
 
     def start_out(s):
         return [remote(start.at[:, col_span(mine, s)], start_far.at[0, :, col_span(0, s)], same, start_base + s),
@@ -314,7 +317,7 @@
             block = mm(jnp.concatenate(left, axis=1), jnp.concatenate(right, axis=1), NT)
             acc[:, span] += weighted(block, 2.0 * (1.0 - ALPHA))
             return carry
-        lax.fori_loop(0, cols // TILE, update, 0, unroll=2)
+        lax.fori_loop(0, cols // TILE, update, 0)
 
     start_near_out.wait_recv()
     src_load(0).start()
@@ -560,7 +563,8 @@
             own_stores[-1].start()
 
     tgt_feat_near.wait_recv()
-    tgt_feat_out.wait_recv()
+    for copy in tgt_feat_out:
+        copy.wait_recv()
     tgt_feat_pass.start()
     for copy in tgt_out:
         copy.wait_recv()
@@ -585,6 +589,12 @@
         return [pltpu.make_async_copy(ready.at[:, aligned(devices[k] * rows + h * SLAB, SLAB)], stage(k)[1][h],
                                       load_sem.at[k % 2 * per + h]) for h in range(per)]
 
+    def half_loads(part):
+        k = GROUP - 1
+        return [pltpu.make_async_copy(
+            ready.at[pl.ds(part * SLAB, SLAB), aligned(devices[k] * rows + h * SLAB, SLAB)],
+            stage(k)[1][h].at[pl.ds(part * SLAB, SLAB)], load_sem.at[k % 2 * per + h]) for h in range(per)]
+
     def begin_left(k):
         for copy, (kk, _) in zip(a_copies, order):
             if kk == k:
@@ -599,22 +609,44 @@
         if k + 1 < GROUP:
             for load in tgt_loads(k + 1):
                 load.start()
+        if k == GROUP - 1:
+            break
         if k + 1 < GROUP - 1:
             begin_left(k + 1)
-        elif k == GROUP - 1:
-            begin_left(k)
         for load in tgt_loads(k) + left_loads(k):
             load.wait()
         rights, lefts = stage(k)
 
         def update(t, carry, rights=rights, lefts=lefts):
-            span = aligned(t * TILE, TILE)
+            span = aligned(t * STEP, STEP)
             total = mm(lefts[0][...], rights[0][:, span], NN)
             for h in range(1, per):
                 total = total + mm(lefts[h][...], rights[h][:, span], NN)
             acc[:, span] += weighted(total, 2.0 * (1.0 - ALPHA))
             return carry
-        lax.fori_loop(0, cols // TILE, update, 0)
+        lax.fori_loop(0, cols // STEP, update, 0)
+
+    for load in tgt_loads(GROUP - 1):
+        load.wait()
+    rights, lefts = stage(GROUP - 1)
+    for part in range(per):
+        for copy, spot in zip(a_copies, order):
+            if spot == (GROUP - 1, part):
+                copy.wait_recv()
+        for load in half_loads(part):
+            load.start()
+        for load in half_loads(part):
+            load.wait()
+        row_span = pl.ds(part * SLAB, SLAB)
+
+        def update_half(t, carry, row_span=row_span):
+            span = aligned(t * TILE, TILE)
+            total = mm(lefts[0][row_span, :], rights[0][:, span], NN)
+            for h in range(1, per):
+                total = total + mm(lefts[h][row_span, :], rights[h][:, span], NN)
+            acc[row_span, span] += weighted(total, 2.0 * (1.0 - ALPHA))
+            return carry
+        lax.fori_loop(0, cols // TILE, update_half, 0)
 
     kern_store = pltpu.make_async_copy(acc, kern_out, load_sem.at[2])
 
@@ -627,8 +659,8 @@
     kern_store.wait()
     for slot in range(2):
         near_copy(slot).wait_send()
-    for copy in ([src_near_out, src_feat_near, start_near_out, tgt_near_out, tgt_feat_near, src_feat_out, tgt_feat_out,
-                  src_pass, src_feat_pass, tgt_pass, tgt_feat_pass] + src_out + tgt_out + mass_out + a_copies):
+    for copy in ([src_near_out, src_feat_near, start_near_out, tgt_near_out, tgt_feat_near, src_feat_out,
+                  src_pass, src_feat_pass, tgt_pass, tgt_feat_pass] + src_out + tgt_out + tgt_feat_out + mass_out + a_copies):
         copy.wait_send()
     for s in range(steps):
         for copy in start_out(s):
@@ -644,7 +676,7 @@
         me = lax.axis_index('rows')
         mass_cols_mine = lax.dynamic_slice(mass_tgt, (rows * me,), (rows,))
         vec = (CHUNKS, tiles, LANES)
-        n_links = 31 + 2 * (half // STEP) + 2 + 3 * rows // SLAB
+        n_links = 44 + 2 * (half // STEP) + 2 + 3 * rows // SLAB
         any_spec = pl.BlockSpec(memory_space=pl.ANY)
         vmem_spec = pl.BlockSpec(memory_space=pltpu.VMEM)
         hbm = [((rows, cols), BF16), ((rows, depth), BF16), ((rows, depth), BF16),

time: 553 us -> 548 us (level)
  no operation moved by 1% of the time
where the time goes in v7:
time: 548 us; the launch traced here: 544 us
  Pallas kernels  526 us (96%)
  other arithmetic  11.9 us (2%)
    pallas_call x1, Pallas kernels, local_fgw(): pl.pallas_call(kernel, out_shape=[jax.ShapeDtypeStruct(*s) for s in outs]...  526 us
    mul x1, other arithmetic, local_fgw(): return row_scale[:, :1] * kern * col_scale.reshape(1, cols)  11.9 us

profile of v7, /device:TPU:0, one launch (start us, length us, event | category | flops | bytes accessed | tf_op | source)
XLA Modules:
  0.0 543.6 jit_solution(15092461990284873536)
XLA Ops:
  0.7 0.7 dynamic_slice.3
  1.3 1.0 broadcast_in_dim.4.mass_rows_t
  2.3 1.7 broadcast_in_dim.5.mass_rows
  4.0 526.0 %fused_gw.1 = (f32[1024,4096]{1,0:T(8,128)}, f32[1024,128]{1,0:T(8,128)}, f32[4,8,128]{2,1,0:T(8,128)}, bf16[1024,4096]{1,0:T(8,128)(2,1)}, bf16[1024,256]{1,0:T...) custom-call(f32[1024,4096]{1,0:T(8,128)} %src_f32.1, ...), custom_call_target="tpu_custom_call" | custom-call | flops 171798691840 | bytes 700000000 | tf_op jit(solution)/shard_map/fused_gw/pallas_call | solution.py:697
  530.0 1.2 slice_reduce_fusion
  531.3 11.9 %multiply_multiply_fusion = f32[1024,4096]{1,0:T(8,128)} fusion(f32[1024,4096]{1,0:T(8,128)} %get-tuple-element.9, f32[4096]{0:T(1024)} %bitcast.5, f32[1024]{0:T(1024)S(1)} %slice_reduce_fusion), kind=kLoop, calls=%fused_computation | loop fusion | flops 8388608 | bytes 33574912 | tf_op jit(solution)/shard_map/mul | solution.py:712
